TPU v7x, 32 devices: a whole 2x2x4 slice. The times are simulated.
32 devices in a mesh: depth: 8 (over y, x, core), image: 4 (over z).
Axes of the slice: x: 2, y: 2, z: 4, core: 2. Of those that a mesh axis runs over, the one named last changes fastest.
Arguments:
- bricks: bfloat16 [8, 1024, 16, 256], P('depth', 'image'), may hold values from -6 to 6
- cost: int32 [8, 1024], P('depth', 'image'), may hold values from 0 to 4, as said below
- order: int32 [2, 8], replicated, may hold values from 0 to 7, as said below
- color_gain: float32 [3], replicated, may hold values from 0.5 to 2
- color_bias: float32 [3], replicated, may hold values from -1 to 1
- ext_gain: float32 [1], replicated, may hold values from 0.6 to 1.4
- ext_bias: float32 [1], replicated, may hold values from -4.6 to -3.6
Outputs:
- frames: float32 [2, 4, 256, 1024], P(None, None, 'depth', 'image')
Inputs may be any that keep to these rules, and one draw needn't show every extreme that they name: In each slab the 4 tiles hold together exactly 512 bricks of cost above 0, and one tile of each slab has all 256 of its bricks nonempty. `order`: row v holds, for slab s, the bitwise exclusive or of s with a number m_v of 0 to 8 - 1 (the same for the whole row).
All inputs are finite; a program needn't handle non-finite values.
Results may differ from a plain program's by a relative error of at most 0.0003.
Values may be sent and summed in bfloat16 or wider, within the bound.
No kernel may reach another device: no remote copies, remote signals or barrier semaphores. Data moves between devices by JAX's collectives and lax.ppermute only.
A program may use at most 128 MiB of HBM per device.

v0:
```python
import math

import jax
import jax.numpy as jnp
from jax import lax
from jax.sharding import PartitionSpec as P

BC = 16


SHEAR = (0.45, -0.3)


def swapped(x, axis, distance):
    return lax.ppermute(x, axis, [(i, i ^ 1 << distance) for i in range(lax.axis_size(axis))])


def shear_taps(brick_edge, view):
    slice_index = jnp.arange(brick_edge, dtype=jnp.float32)[:, None]
    position = jnp.arange(brick_edge, dtype=jnp.float32)[None, :] + SHEAR[view] * (
        slice_index - (brick_edge - 1) / 2.0
    )
    anchor = jnp.floor(position)
    fraction = position - anchor
    weight_low = lax.optimization_barrier((1.0 - fraction).astype(jnp.bfloat16)).astype(jnp.float32)
    weight_high = lax.optimization_barrier(fraction.astype(jnp.bfloat16)).astype(jnp.float32)
    return (anchor.astype(jnp.int32), weight_low, weight_high)


def shear_table(brick_edge):
    cells = jnp.arange(brick_edge * brick_edge, dtype=jnp.int32)
    source_row = (cells // brick_edge)[None, :, None]
    source_col = (cells % brick_edge)[None, :, None]
    target_row = (cells // brick_edge)[None, None, :]
    target_col = (cells % brick_edge)[None, None, :]
    tables = []
    for view in range(2):
        anchor, weight_low, weight_high = shear_taps(brick_edge, view)
        if view == 0:
            along_target = cells % brick_edge
            same_line = source_row == target_row
            moving = source_col
        else:
            along_target = cells // brick_edge
            same_line = source_col == target_col
            moving = source_row
        start_cell = anchor[:, along_target][:, None, :]
        entry = jnp.where(
            same_line & (moving == start_cell), weight_low[:, along_target][:, None, :], 0.0
        )
        entry = entry + jnp.where(
            same_line & (moving == start_cell + 1), weight_high[:, along_target][:, None, :], 0.0
        )
        tables.append(entry.astype(jnp.bfloat16))
    return jnp.stack(tables)


def shade_samples(samples, levels, flip, color_gain, color_bias, ext_gain, ext_bias):
    brick_edge = samples.shape[1]
    slice_index = jnp.arange(brick_edge, dtype=jnp.int32)
    occupied = (slice_index[None, :] * 4 < levels[:, None] * brick_edge).astype(samples.dtype)[
        :, :, None
    ]
    samples = jnp.where(flip, samples[:, ::-1], samples)
    occupied = jnp.where(flip, occupied[:, ::-1], occupied)
    extinction = jnp.exp(ext_gain[0] * samples + ext_bias[0])
    opacity = (1.0 - jnp.exp(-extinction)) * occupied
    remaining = jnp.cumprod(1.0 - opacity, axis=1)
    ahead_clear = jnp.concatenate([jnp.ones_like(remaining[:, :1]), remaining[:, :-1]], axis=1)
    weight = ahead_clear * opacity
    colors = [
        jnp.sum(
            weight * jax.nn.sigmoid(color_gain[channel] * samples + color_bias[channel]), axis=1
        )
        for channel in range(3)
    ]
    return jnp.stack(colors + [1.0 - remaining[:, -1]], axis=1)


def render(density, levels, table, flips, transfer):
    total_bricks = density.shape[0]
    block_size = math.gcd(total_bricks, 32)

    def render_block(pair):
        block_density, block_levels = pair
        views = []
        for view in range(2):
            samples = jnp.einsum(
                "nkp,kpq->nkq", block_density, table[view], preferred_element_type=jnp.float32
            )
            views.append(shade_samples(samples, block_levels, flips[view], *transfer))
        return jnp.stack(views, axis=1)

    blocks = (
        density.reshape(total_bricks // block_size, block_size, density.shape[1], density.shape[2]),
        levels.reshape(total_bricks // block_size, block_size),
    )
    rendered = lax.map(render_block, blocks)
    return rendered.reshape(total_bricks, 2, 4, density.shape[2])


def blend(front_part, back_part):
    return front_part + (1.0 - front_part[:, 3:4]) * back_part


def shards(bricks, cost, order, color_gain, color_bias, ext_gain, ext_bias):
    density = bricks[0]
    levels = cost[0]
    brick_count, brick_edge, plane_size = density.shape
    flips = order[:, 0] > order[:, -1]
    masks = order[:, 0]
    table = shear_table(brick_edge)
    transfer = (color_gain, color_bias, ext_gain, ext_bias)
    segments = render(density, levels, table, flips, transfer)
    rows = brick_count // BC
    tile_image = segments.reshape(rows, BC, 2, 4, brick_edge, brick_edge).transpose(
        2, 3, 0, 4, 1, 5
    )
    tile_image = tile_image.reshape(2, 4, rows * brick_edge, BC * brick_edge)
    depth_count = lax.axis_size("depth")
    my_index = lax.axis_index("depth")
    rounds = depth_count.bit_length() - 1
    block_rows = tile_image.shape[2] // depth_count
    merged = tile_image.reshape(2, 4, depth_count, block_rows, tile_image.shape[3])
    my_ranks = jnp.bitwise_xor(my_index, masks)
    for round_bit in range(rounds):
        upper_flag = my_index >> round_bit & 1 == 1
        lower_part = merged[:, :, 0::2]
        upper_part = merged[:, :, 1::2]
        outgoing_half = jnp.where(upper_flag, lower_part, upper_part)
        kept_half = jnp.where(upper_flag, upper_part, lower_part)
        incoming = swapped(outgoing_half, "depth", round_bit)
        partner_front = (my_ranks >> round_bit & 1 == 1)[:, None, None, None, None]
        front_part = jnp.where(partner_front, incoming, kept_half)
        back_part = jnp.where(partner_front, kept_half, incoming)
        merged = blend(front_part, back_part)
    return merged[:, :, 0]


def solution(mesh):
    in_specs = (P("depth", "image", None, None), P("depth", "image"), P(), P(), P(), P(), P())
    out_specs = P(None, None, "depth", "image")
    return jax.shard_map(shards, mesh=mesh, in_specs=in_specs, out_specs=out_specs, check_vma=False)
```

profile of v0, /device:TPU:0, one launch (start us, length us, event | category | flops | bytes accessed | tf_op | source)
XLA Modules:
  0.0 260.5 jit_solution(4837927381943795360)
XLA Ops:
  0.1 1.0 compare_reduce_fusion.3
  6.7 1.4 reduce.11
  8.3 185.1 %while.11 = (s32[]{:T(128)}, f32[8,32,2,4,256]{4,1,0,3,2:T(8,128)S(1)}, f32[1]{0:T(128)}, pred[2]{0:T(512)(128)(4,1)S(1)}, bf16[8,32,16,256]{3,2,1,0:T(8,128)(2,...) while((s32[]{:T(128)}, ...), condition=%wide.region_9.10_spmd.clone, body=%wide.region_0.9_spmd.clone.sunk | while | flops 164334640 | bytes 11951275 | solution.py:98
  9.0 1.3 fusion.55
  11.3 1.8 fusion.52
  13.1 1.8 fusion.56
  14.9 2.9 %subtract_multiply_fusion.3 = (f32[32,16,256]{2,0,1:T(8,128)S(1)}, f32[32,16,256]{2,0,1:T(8,128)S(1)}) fusion(f32[32,16,256]{2,0,1:T(8,128)S(1)} %fusion.52, f32[32,16]{0,1:T(8,128)S(1)} %get-tuple-element.384, f32[]{:T(128)} %bitcast.96, f32[]{:T(128)} %bitcast.97, pred[]{:T(512)} %bitcast.95, f32[32,16]{0,1:T(8,128)S(1)} %get-tuple-element.385, ...), kind=kLoop, calls=%fused_computation.26.clone.4 | loop fusion | flops 1572864 | bytes 2101258 | tf_op jit(solution)/shard_map/while/body/eval_jaxpr/mul | solution.py:67
  18.7 6.3 %multiply_reduce_fusion.9 = (f32[32,256]{1,0:T(8,128)S(1)}, f32[32,256]{1,0:T(8,128)S(1)}, f32[32,256]{1,0:T(8,128)S(1)}) fusion(f32[32,16,256]{2,0,1:T(8,128)S(1)} %fusion.56, f32[]{:T(128)} %bitcast.98, f32[]{:T(128)} %bitcast.99, pred[]{:T(512)} %bitcast.94, f32[32,15,256]{2,0,1:T(8,128)S(1)} %slice.203, f32[32,16]{0,1:T(8,128)S(1)} %get-tuple-element.385, ...), kind=kLoop, calls=%fused_computation.29.clone.1 | loop fusion | flops 3645440 | bytes 1116193 | tf_op jit(solution)/shard_map/while/body/eval_jaxpr/reduce_sum | solution.py:72
  25.2 6.2 %multiply_reduce_fusion.8 = (f32[32,256]{1,0:T(8,128)S(1)}, f32[32,256]{1,0:T(8,128)S(1)}, f32[32,256]{1,0:T(8,128)S(1)}) fusion(f32[32,16,256]{2,0,1:T(8,128)S(1)} %fusion.52, f32[]{:T(128)} %bitcast.98, f32[]{:T(128)} %bitcast.99, pred[]{:T(512)} %bitcast.95, f32[32,15,256]{2,0,1:T(8,128)S(1)} %slice.202, f32[32,16]{0,1:T(8,128)S(1)} %get-tuple-element.384, ...), kind=kLoop, calls=%fused_computation.22.clone.1 | loop fusion | flops 3645440 | bytes 1116193 | tf_op jit(solution)/shard_map/while/body/eval_jaxpr/reduce_sum | solution.py:72
  32.2 1.3 fusion.55
  34.5 1.8 fusion.52
  36.3 1.8 fusion.56
  38.1 2.9 %subtract_multiply_fusion.3 = (f32[32,16,256]{2,0,1:T(8,128)S(1)}, f32[32,16,256]{2,0,1:T(8,128)S(1)}) fusion(f32[32,16,256]{2,0,1:T(8,128)S(1)} %fusion.52, f32[32,16]{0,1:T(8,128)S(1)} %get-tuple-element.384, f32[]{:T(128)} %bitcast.96, f32[]{:T(128)} %bitcast.97, pred[]{:T(512)} %bitcast.95, f32[32,16]{0,1:T(8,128)S(1)} %get-tuple-element.385, ...), kind=kLoop, calls=%fused_computation.26.clone.4 | loop fusion | flops 1572864 | bytes 2101258 | tf_op jit(solution)/shard_map/while/body/eval_jaxpr/mul | solution.py:67
  41.8 6.3 %multiply_reduce_fusion.9 = (f32[32,256]{1,0:T(8,128)S(1)}, f32[32,256]{1,0:T(8,128)S(1)}, f32[32,256]{1,0:T(8,128)S(1)}) fusion(f32[32,16,256]{2,0,1:T(8,128)S(1)} %fusion.56, f32[]{:T(128)} %bitcast.98, f32[]{:T(128)} %bitcast.99, pred[]{:T(512)} %bitcast.94, f32[32,15,256]{2,0,1:T(8,128)S(1)} %slice.203, f32[32,16]{0,1:T(8,128)S(1)} %get-tuple-element.385, ...), kind=kLoop, calls=%fused_computation.29.clone.1 | loop fusion | flops 3645440 | bytes 1116193 | tf_op jit(solution)/shard_map/while/body/eval_jaxpr/reduce_sum | solution.py:72
  48.3 6.2 %multiply_reduce_fusion.8 = (f32[32,256]{1,0:T(8,128)S(1)}, f32[32,256]{1,0:T(8,128)S(1)}, f32[32,256]{1,0:T(8,128)S(1)}) fusion(f32[32,16,256]{2,0,1:T(8,128)S(1)} %fusion.52, f32[]{:T(128)} %bitcast.98, f32[]{:T(128)} %bitcast.99, pred[]{:T(512)} %bitcast.95, f32[32,15,256]{2,0,1:T(8,128)S(1)} %slice.202, f32[32,16]{0,1:T(8,128)S(1)} %get-tuple-element.384, ...), kind=kLoop, calls=%fused_computation.22.clone.1 | loop fusion | flops 3645440 | bytes 1116193 | tf_op jit(solution)/shard_map/while/body/eval_jaxpr/reduce_sum | solution.py:72
  55.3 1.3 fusion.55
  56.6 1.0 constant_dynamic-slice_fusion.3
  57.6 1.8 fusion.52
  59.4 1.8 fusion.56
  61.2 2.9 %subtract_multiply_fusion.3 = (f32[32,16,256]{2,0,1:T(8,128)S(1)}, f32[32,16,256]{2,0,1:T(8,128)S(1)}) fusion(f32[32,16,256]{2,0,1:T(8,128)S(1)} %fusion.52, f32[32,16]{0,1:T(8,128)S(1)} %get-tuple-element.384, f32[]{:T(128)} %bitcast.96, f32[]{:T(128)} %bitcast.97, pred[]{:T(512)} %bitcast.95, f32[32,16]{0,1:T(8,128)S(1)} %get-tuple-element.385, ...), kind=kLoop, calls=%fused_computation.26.clone.4 | loop fusion | flops 1572864 | bytes 2101258 | tf_op jit(solution)/shard_map/while/body/eval_jaxpr/mul | solution.py:67
  64.9 6.3 %multiply_reduce_fusion.9 = (f32[32,256]{1,0:T(8,128)S(1)}, f32[32,256]{1,0:T(8,128)S(1)}, f32[32,256]{1,0:T(8,128)S(1)}) fusion(f32[32,16,256]{2,0,1:T(8,128)S(1)} %fusion.56, f32[]{:T(128)} %bitcast.98, f32[]{:T(128)} %bitcast.99, pred[]{:T(512)} %bitcast.94, f32[32,15,256]{2,0,1:T(8,128)S(1)} %slice.203, f32[32,16]{0,1:T(8,128)S(1)} %get-tuple-element.385, ...), kind=kLoop, calls=%fused_computation.29.clone.1 | loop fusion | flops 3645440 | bytes 1116193 | tf_op jit(solution)/shard_map/while/body/eval_jaxpr/reduce_sum | solution.py:72
  71.4 6.2 %multiply_reduce_fusion.8 = (f32[32,256]{1,0:T(8,128)S(1)}, f32[32,256]{1,0:T(8,128)S(1)}, f32[32,256]{1,0:T(8,128)S(1)}) fusion(f32[32,16,256]{2,0,1:T(8,128)S(1)} %fusion.52, f32[]{:T(128)} %bitcast.98, f32[]{:T(128)} %bitcast.99, pred[]{:T(512)} %bitcast.95, f32[32,15,256]{2,0,1:T(8,128)S(1)} %slice.202, f32[32,16]{0,1:T(8,128)S(1)} %get-tuple-element.384, ...), kind=kLoop, calls=%fused_computation.22.clone.1 | loop fusion | flops 3645440 | bytes 1116193 | tf_op jit(solution)/shard_map/while/body/eval_jaxpr/reduce_sum | solution.py:72
  78.4 1.3 fusion.55
  79.8 1.0 constant_dynamic-slice_fusion.3
  80.7 1.8 fusion.52
  82.5 1.8 fusion.56
  84.3 2.9 %subtract_multiply_fusion.3 = (f32[32,16,256]{2,0,1:T(8,128)S(1)}, f32[32,16,256]{2,0,1:T(8,128)S(1)}) fusion(f32[32,16,256]{2,0,1:T(8,128)S(1)} %fusion.52, f32[32,16]{0,1:T(8,128)S(1)} %get-tuple-element.384, f32[]{:T(128)} %bitcast.96, f32[]{:T(128)} %bitcast.97, pred[]{:T(512)} %bitcast.95, f32[32,16]{0,1:T(8,128)S(1)} %get-tuple-element.385, ...), kind=kLoop, calls=%fused_computation.26.clone.4 | loop fusion | flops 1572864 | bytes 2101258 | tf_op jit(solution)/shard_map/while/body/eval_jaxpr/mul | solution.py:67
  88.1 6.3 %multiply_reduce_fusion.9 = (f32[32,256]{1,0:T(8,128)S(1)}, f32[32,256]{1,0:T(8,128)S(1)}, f32[32,256]{1,0:T(8,128)S(1)}) fusion(f32[32,16,256]{2,0,1:T(8,128)S(1)} %fusion.56, f32[]{:T(128)} %bitcast.98, f32[]{:T(128)} %bitcast.99, pred[]{:T(512)} %bitcast.94, f32[32,15,256]{2,0,1:T(8,128)S(1)} %slice.203, f32[32,16]{0,1:T(8,128)S(1)} %get-tuple-element.385, ...), kind=kLoop, calls=%fused_computation.29.clone.1 | loop fusion | flops 3645440 | bytes 1116193 | tf_op jit(solution)/shard_map/while/body/eval_jaxpr/reduce_sum | solution.py:72
  94.6 6.2 %multiply_reduce_fusion.8 = (f32[32,256]{1,0:T(8,128)S(1)}, f32[32,256]{1,0:T(8,128)S(1)}, f32[32,256]{1,0:T(8,128)S(1)}) fusion(f32[32,16,256]{2,0,1:T(8,128)S(1)} %fusion.52, f32[]{:T(128)} %bitcast.98, f32[]{:T(128)} %bitcast.99, pred[]{:T(512)} %bitcast.95, f32[32,15,256]{2,0,1:T(8,128)S(1)} %slice.202, f32[32,16]{0,1:T(8,128)S(1)} %get-tuple-element.384, ...), kind=kLoop, calls=%fused_computation.22.clone.1 | loop fusion | flops 3645440 | bytes 1116193 | tf_op jit(solution)/shard_map/while/body/eval_jaxpr/reduce_sum | solution.py:72
  101.6 1.3 fusion.55
  102.9 1.0 constant_dynamic-slice_fusion.3
  103.9 1.8 fusion.52
  105.7 1.8 fusion.56
  107.5 2.9 %subtract_multiply_fusion.3 = (f32[32,16,256]{2,0,1:T(8,128)S(1)}, f32[32,16,256]{2,0,1:T(8,128)S(1)}) fusion(f32[32,16,256]{2,0,1:T(8,128)S(1)} %fusion.52, f32[32,16]{0,1:T(8,128)S(1)} %get-tuple-element.384, f32[]{:T(128)} %bitcast.96, f32[]{:T(128)} %bitcast.97, pred[]{:T(512)} %bitcast.95, f32[32,16]{0,1:T(8,128)S(1)} %get-tuple-element.385, ...), kind=kLoop, calls=%fused_computation.26.clone.4 | loop fusion | flops 1572864 | bytes 2101258 | tf_op jit(solution)/shard_map/while/body/eval_jaxpr/mul | solution.py:67
  111.2 6.3 %multiply_reduce_fusion.9 = (f32[32,256]{1,0:T(8,128)S(1)}, f32[32,256]{1,0:T(8,128)S(1)}, f32[32,256]{1,0:T(8,128)S(1)}) fusion(f32[32,16,256]{2,0,1:T(8,128)S(1)} %fusion.56, f32[]{:T(128)} %bitcast.98, f32[]{:T(128)} %bitcast.99, pred[]{:T(512)} %bitcast.94, f32[32,15,256]{2,0,1:T(8,128)S(1)} %slice.203, f32[32,16]{0,1:T(8,128)S(1)} %get-tuple-element.385, ...), kind=kLoop, calls=%fused_computation.29.clone.1 | loop fusion | flops 3645440 | bytes 1116193 | tf_op jit(solution)/shard_map/while/body/eval_jaxpr/reduce_sum | solution.py:72
  117.7 6.2 %multiply_reduce_fusion.8 = (f32[32,256]{1,0:T(8,128)S(1)}, f32[32,256]{1,0:T(8,128)S(1)}, f32[32,256]{1,0:T(8,128)S(1)}) fusion(f32[32,16,256]{2,0,1:T(8,128)S(1)} %fusion.52, f32[]{:T(128)} %bitcast.98, f32[]{:T(128)} %bitcast.99, pred[]{:T(512)} %bitcast.95, f32[32,15,256]{2,0,1:T(8,128)S(1)} %slice.202, f32[32,16]{0,1:T(8,128)S(1)} %get-tuple-element.384, ...), kind=kLoop, calls=%fused_computation.22.clone.1 | loop fusion | flops 3645440 | bytes 1116193 | tf_op jit(solution)/shard_map/while/body/eval_jaxpr/reduce_sum | solution.py:72
  124.7 1.3 fusion.55
  127.0 1.8 fusion.52
  128.8 1.8 fusion.56
  130.6 2.9 %subtract_multiply_fusion.3 = (f32[32,16,256]{2,0,1:T(8,128)S(1)}, f32[32,16,256]{2,0,1:T(8,128)S(1)}) fusion(f32[32,16,256]{2,0,1:T(8,128)S(1)} %fusion.52, f32[32,16]{0,1:T(8,128)S(1)} %get-tuple-element.384, f32[]{:T(128)} %bitcast.96, f32[]{:T(128)} %bitcast.97, pred[]{:T(512)} %bitcast.95, f32[32,16]{0,1:T(8,128)S(1)} %get-tuple-element.385, ...), kind=kLoop, calls=%fused_computation.26.clone.4 | loop fusion | flops 1572864 | bytes 2101258 | tf_op jit(solution)/shard_map/while/body/eval_jaxpr/mul | solution.py:67
  134.3 6.3 %multiply_reduce_fusion.9 = (f32[32,256]{1,0:T(8,128)S(1)}, f32[32,256]{1,0:T(8,128)S(1)}, f32[32,256]{1,0:T(8,128)S(1)}) fusion(f32[32,16,256]{2,0,1:T(8,128)S(1)} %fusion.56, f32[]{:T(128)} %bitcast.98, f32[]{:T(128)} %bitcast.99, pred[]{:T(512)} %bitcast.94, f32[32,15,256]{2,0,1:T(8,128)S(1)} %slice.203, f32[32,16]{0,1:T(8,128)S(1)} %get-tuple-element.385, ...), kind=kLoop, calls=%fused_computation.29.clone.1 | loop fusion | flops 3645440 | bytes 1116193 | tf_op jit(solution)/shard_map/while/body/eval_jaxpr/reduce_sum | solution.py:72
  140.9 6.2 %multiply_reduce_fusion.8 = (f32[32,256]{1,0:T(8,128)S(1)}, f32[32,256]{1,0:T(8,128)S(1)}, f32[32,256]{1,0:T(8,128)S(1)}) fusion(f32[32,16,256]{2,0,1:T(8,128)S(1)} %fusion.52, f32[]{:T(128)} %bitcast.98, f32[]{:T(128)} %bitcast.99, pred[]{:T(512)} %bitcast.95, f32[32,15,256]{2,0,1:T(8,128)S(1)} %slice.202, f32[32,16]{0,1:T(8,128)S(1)} %get-tuple-element.384, ...), kind=kLoop, calls=%fused_computation.22.clone.1 | loop fusion | flops 3645440 | bytes 1116193 | tf_op jit(solution)/shard_map/while/body/eval_jaxpr/reduce_sum | solution.py:72
  147.8 1.3 fusion.55
  150.1 1.8 fusion.52
  151.9 1.8 fusion.56
  153.7 2.9 %subtract_multiply_fusion.3 = (f32[32,16,256]{2,0,1:T(8,128)S(1)}, f32[32,16,256]{2,0,1:T(8,128)S(1)}) fusion(f32[32,16,256]{2,0,1:T(8,128)S(1)} %fusion.52, f32[32,16]{0,1:T(8,128)S(1)} %get-tuple-element.384, f32[]{:T(128)} %bitcast.96, f32[]{:T(128)} %bitcast.97, pred[]{:T(512)} %bitcast.95, f32[32,16]{0,1:T(8,128)S(1)} %get-tuple-element.385, ...), kind=kLoop, calls=%fused_computation.26.clone.4 | loop fusion | flops 1572864 | bytes 2101258 | tf_op jit(solution)/shard_map/while/body/eval_jaxpr/mul | solution.py:67
  157.5 6.3 %multiply_reduce_fusion.9 = (f32[32,256]{1,0:T(8,128)S(1)}, f32[32,256]{1,0:T(8,128)S(1)}, f32[32,256]{1,0:T(8,128)S(1)}) fusion(f32[32,16,256]{2,0,1:T(8,128)S(1)} %fusion.56, f32[]{:T(128)} %bitcast.98, f32[]{:T(128)} %bitcast.99, pred[]{:T(512)} %bitcast.94, f32[32,15,256]{2,0,1:T(8,128)S(1)} %slice.203, f32[32,16]{0,1:T(8,128)S(1)} %get-tuple-element.385, ...), kind=kLoop, calls=%fused_computation.29.clone.1 | loop fusion | flops 3645440 | bytes 1116193 | tf_op jit(solution)/shard_map/while/body/eval_jaxpr/reduce_sum | solution.py:72
  164.0 6.2 %multiply_reduce_fusion.8 = (f32[32,256]{1,0:T(8,128)S(1)}, f32[32,256]{1,0:T(8,128)S(1)}, f32[32,256]{1,0:T(8,128)S(1)}) fusion(f32[32,16,256]{2,0,1:T(8,128)S(1)} %fusion.52, f32[]{:T(128)} %bitcast.98, f32[]{:T(128)} %bitcast.99, pred[]{:T(512)} %bitcast.95, f32[32,15,256]{2,0,1:T(8,128)S(1)} %slice.202, f32[32,16]{0,1:T(8,128)S(1)} %get-tuple-element.384, ...), kind=kLoop, calls=%fused_computation.22.clone.1 | loop fusion | flops 3645440 | bytes 1116193 | tf_op jit(solution)/shard_map/while/body/eval_jaxpr/reduce_sum | solution.py:72
  171.0 1.3 fusion.55
  173.3 1.8 fusion.52
  175.1 1.8 fusion.56
  176.9 2.9 %subtract_multiply_fusion.3 = (f32[32,16,256]{2,0,1:T(8,128)S(1)}, f32[32,16,256]{2,0,1:T(8,128)S(1)}) fusion(f32[32,16,256]{2,0,1:T(8,128)S(1)} %fusion.52, f32[32,16]{0,1:T(8,128)S(1)} %get-tuple-element.384, f32[]{:T(128)} %bitcast.96, f32[]{:T(128)} %bitcast.97, pred[]{:T(512)} %bitcast.95, f32[32,16]{0,1:T(8,128)S(1)} %get-tuple-element.385, ...), kind=kLoop, calls=%fused_computation.26.clone.4 | loop fusion | flops 1572864 | bytes 2101258 | tf_op jit(solution)/shard_map/while/body/eval_jaxpr/mul | solution.py:67
  180.6 6.3 %multiply_reduce_fusion.9 = (f32[32,256]{1,0:T(8,128)S(1)}, f32[32,256]{1,0:T(8,128)S(1)}, f32[32,256]{1,0:T(8,128)S(1)}) fusion(f32[32,16,256]{2,0,1:T(8,128)S(1)} %fusion.56, f32[]{:T(128)} %bitcast.98, f32[]{:T(128)} %bitcast.99, pred[]{:T(512)} %bitcast.94, f32[32,15,256]{2,0,1:T(8,128)S(1)} %slice.203, f32[32,16]{0,1:T(8,128)S(1)} %get-tuple-element.385, ...), kind=kLoop, calls=%fused_computation.29.clone.1 | loop fusion | flops 3645440 | bytes 1116193 | tf_op jit(solution)/shard_map/while/body/eval_jaxpr/reduce_sum | solution.py:72
  187.1 6.2 %multiply_reduce_fusion.8 = (f32[32,256]{1,0:T(8,128)S(1)}, f32[32,256]{1,0:T(8,128)S(1)}, f32[32,256]{1,0:T(8,128)S(1)}) fusion(f32[32,16,256]{2,0,1:T(8,128)S(1)} %fusion.52, f32[]{:T(128)} %bitcast.98, f32[]{:T(128)} %bitcast.99, pred[]{:T(512)} %bitcast.95, f32[32,15,256]{2,0,1:T(8,128)S(1)} %slice.202, f32[32,16]{0,1:T(8,128)S(1)} %get-tuple-element.384, ...), kind=kLoop, calls=%fused_computation.22.clone.1 | loop fusion | flops 3645440 | bytes 1116193 | tf_op jit(solution)/shard_map/while/body/eval_jaxpr/reduce_sum | solution.py:72
  193.4 8.7 %reshape_reshape.6 = f32[16,16,2,4,16,16]{5,4,1,0,3,2:T(8,128)} reshape(f32[8,32,2,4,256]{4,1,0,3,2:T(8,128)S(1)} %get-tuple-element.62) | data formatting | bytes 4194304 | tf_op jit(solution)/shard_map/reshape;reshape | solution.py:116
  202.1 15.7 %copy.26 = f32[2,4,16,16,16,16]{5,4,3,2,1,0:T(8,128)} copy(f32[2,4,16,16,16,16]{5,3,4,2,1,0:T(8,128)} %bitcast.110) | data formatting | bytes 4194304 | tf_op jit(solution)/shard_map/transpose | solution.py:116
  217.8 11.4 %reshape_reshape.7 = f32[2,4,8,32,256]{4,3,2,1,0:T(8,128)S(1)} reshape(f32[2,4,16,16,16,16]{5,4,3,2,1,0:T(8,128)} %copy.26) | data formatting | bytes 4194304 | tf_op jit(solution)/shard_map/reshape;reshape | solution.py:124
  229.2 1.1 slice_select_fusion.1
  230.9 2.5 collective-permute-done
  234.4 1.7 multiply_add_fusion
  236.2 2.9 %collective-permute-start.1 = (f32[2,4,2,32,256]{4,3,2,1,0:T(8,128)S(1)}, f32[2,4,2,32,256]{4,3,2,1,0:T(8,128)S(1)}, u32[]{:S(2)}, u32[]{:S(2)}) collective-permute-start(f32[2,4,2,32,256]{4,3,2,1,0:T(8,128)S(1)} %slice_select_fusion.3), channel_id=1, source_target_pairs={{0,8},{4,12},{8,0},{12,4},{16,24},{20,28},{24,16},{28,20},{1,9},{5... | collective-permute-start | bytes 1572872 | tf_op jit(solution)/shard_map/ppermute | solution.py:15
  239.1 12.2 %collective-permute-done.1 = f32[2,4,2,32,256]{4,3,2,1,0:T(8,128)S(1)} collective-permute-done((f32[2,4,2,32,256]{4,3,2,1,0:T(8,128)S(1)}, f32[2,4,2,32,256]{4,3,2,1,0:T(8,128)S(1)}, u32[]{:S(2)}, u32[]{:S(2)}) %collective-permute-start.1) | collective-permute-done | bytes 524320 | tf_op jit(solution)/shard_map/ppermute | solution.py:15
  251.7 1.8 collective-permute-start.2
  253.6 6.0 %collective-permute-done.2 = f32[2,4,1,32,256]{4,3,2,1,0:T(8,128)S(1)} collective-permute-done((f32[2,4,1,32,256]{4,3,2,1,0:T(8,128)S(1)}, f32[2,4,1,32,256]{4,3,2,1,0:T(8,128)S(1)}, u32[]{:S(2)}, u32[]{:S(2)}) %collective-permute-start.2) | collective-permute-done | bytes 262176 | tf_op jit(solution)/shard_map/ppermute | solution.py:15
  (204 shorter events, 27.1 us)
Async XLA Ops:
  13.1 4.8 %copy-start.1 = (f32[3]{0:T(128)S(1)}, f32[3]{0:T(128)}, u32[]{:S(2)}) copy-start(f32[3]{0:T(128)} %get-tuple-element.451) | copy-start | bytes 40 | tf_op jit(solution)/shard_map/while
  13.1 4.8 %copy-start.2 = (f32[3]{0:T(128)S(1)}, f32[3]{0:T(128)}, u32[]{:S(2)}) copy-start(f32[3]{0:T(128)} %get-tuple-element.452) | copy-start | bytes 40 | tf_op jit(solution)/shard_map/while
  36.3 4.8 %copy-start.1 = (f32[3]{0:T(128)S(1)}, f32[3]{0:T(128)}, u32[]{:S(2)}) copy-start(f32[3]{0:T(128)} %get-tuple-element.451) | copy-start | bytes 40 | tf_op jit(solution)/shard_map/while
  36.3 4.8 %copy-start.2 = (f32[3]{0:T(128)S(1)}, f32[3]{0:T(128)}, u32[]{:S(2)}) copy-start(f32[3]{0:T(128)} %get-tuple-element.452) | copy-start | bytes 40 | tf_op jit(solution)/shard_map/while
  59.4 4.8 %copy-start.1 = (f32[3]{0:T(128)S(1)}, f32[3]{0:T(128)}, u32[]{:S(2)}) copy-start(f32[3]{0:T(128)} %get-tuple-element.451) | copy-start | bytes 40 | tf_op jit(solution)/shard_map/while
  59.4 4.8 %copy-start.2 = (f32[3]{0:T(128)S(1)}, f32[3]{0:T(128)}, u32[]{:S(2)}) copy-start(f32[3]{0:T(128)} %get-tuple-element.452) | copy-start | bytes 40 | tf_op jit(solution)/shard_map/while
  82.5 4.8 %copy-start.1 = (f32[3]{0:T(128)S(1)}, f32[3]{0:T(128)}, u32[]{:S(2)}) copy-start(f32[3]{0:T(128)} %get-tuple-element.451) | copy-start | bytes 40 | tf_op jit(solution)/shard_map/while
  82.5 4.8 %copy-start.2 = (f32[3]{0:T(128)S(1)}, f32[3]{0:T(128)}, u32[]{:S(2)}) copy-start(f32[3]{0:T(128)} %get-tuple-element.452) | copy-start | bytes 40 | tf_op jit(solution)/shard_map/while
  105.7 4.8 %copy-start.1 = (f32[3]{0:T(128)S(1)}, f32[3]{0:T(128)}, u32[]{:S(2)}) copy-start(f32[3]{0:T(128)} %get-tuple-element.451) | copy-start | bytes 40 | tf_op jit(solution)/shard_map/while
  105.7 4.8 %copy-start.2 = (f32[3]{0:T(128)S(1)}, f32[3]{0:T(128)}, u32[]{:S(2)}) copy-start(f32[3]{0:T(128)} %get-tuple-element.452) | copy-start | bytes 40 | tf_op jit(solution)/shard_map/while
  128.8 4.8 %copy-start.1 = (f32[3]{0:T(128)S(1)}, f32[3]{0:T(128)}, u32[]{:S(2)}) copy-start(f32[3]{0:T(128)} %get-tuple-element.451) | copy-start | bytes 40 | tf_op jit(solution)/shard_map/while
  128.8 4.8 %copy-start.2 = (f32[3]{0:T(128)S(1)}, f32[3]{0:T(128)}, u32[]{:S(2)}) copy-start(f32[3]{0:T(128)} %get-tuple-element.452) | copy-start | bytes 40 | tf_op jit(solution)/shard_map/while
  151.9 4.8 %copy-start.1 = (f32[3]{0:T(128)S(1)}, f32[3]{0:T(128)}, u32[]{:S(2)}) copy-start(f32[3]{0:T(128)} %get-tuple-element.451) | copy-start | bytes 40 | tf_op jit(solution)/shard_map/while
  151.9 4.8 %copy-start.2 = (f32[3]{0:T(128)S(1)}, f32[3]{0:T(128)}, u32[]{:S(2)}) copy-start(f32[3]{0:T(128)} %get-tuple-element.452) | copy-start | bytes 40 | tf_op jit(solution)/shard_map/while
  175.1 4.8 %copy-start.1 = (f32[3]{0:T(128)S(1)}, f32[3]{0:T(128)}, u32[]{:S(2)}) copy-start(f32[3]{0:T(128)} %get-tuple-element.451) | copy-start | bytes 40 | tf_op jit(solution)/shard_map/while
  175.1 4.8 %copy-start.2 = (f32[3]{0:T(128)S(1)}, f32[3]{0:T(128)}, u32[]{:S(2)}) copy-start(f32[3]{0:T(128)} %get-tuple-element.452) | copy-start | bytes 40 | tf_op jit(solution)/shard_map/while
  230.4 3.0 %collective-permute-start = (f32[2,4,4,32,256]{4,3,2,1,0:T(8,128)}, f32[2,4,4,32,256]{4,3,2,1,0:T(8,128)S(1)}, u32[]{:S(2)}, u32[]{:S(2)}) collective-permute-start(f32[2,4,4,32,256]{4,3,2,1,0:T(8,128)} %slice_select_fusion.1), channel_id=1, source_target_pairs={{0,4},{4,0},{8,12},{12,8},{16,20},{20,16},{24,28},{28,24},{1,5},{5... | collective-permute-start | bytes 3145736 | tf_op jit(solution)/shard_map/ppermute | solution.py:15
  233.4 1.0 copy-start
  236.2 15.1 %collective-permute-start.1 = (f32[2,4,2,32,256]{4,3,2,1,0:T(8,128)S(1)}, f32[2,4,2,32,256]{4,3,2,1,0:T(8,128)S(1)}, u32[]{:S(2)}, u32[]{:S(2)}) collective-permute-start(f32[2,4,2,32,256]{4,3,2,1,0:T(8,128)S(1)} %slice_select_fusion.3), channel_id=1, source_target_pairs={{0,8},{4,12},{8,0},{12,4},{16,24},{20,28},{24,16},{28,20},{1,9},{5... | collective-permute-start | bytes 1572872 | tf_op jit(solution)/shard_map/ppermute | solution.py:15
  251.7 7.8 %collective-permute-start.2 = (f32[2,4,1,32,256]{4,3,2,1,0:T(8,128)S(1)}, f32[2,4,1,32,256]{4,3,2,1,0:T(8,128)S(1)}, u32[]{:S(2)}, u32[]{:S(2)}) collective-permute-start(f32[2,4,1,32,256]{4,3,2,1,0:T(8,128)S(1)} %slice_select_fusion.5), channel_id=1, source_target_pairs={{0,16},{4,20},{8,24},{12,28},{16,0},{20,4},{24,8},{28,12},{1,17},{... | collective-permute-start | bytes 786440 | tf_op jit(solution)/shard_map/ppermute | solution.py:15
where the time goes:
time: 263 us; the launch traced here: 260 us
  other arithmetic  144 us (55%)
  local copies, waits for them, and re-layouts  60.8 us (23%)
  matrix products  28.8 us (11%)
  waiting for transfers between devices  20.7 us (8%)
  starting transfers between devices  5.24 us (2%)
    reduce_sum x16, other arithmetic, shade_samples(): jnp.sum(weight * jax.nn.sigmoid(color_gain[channel] * samples + color_bia...  100 us
    dot_general x16, matrix products, render_block(): jnp.einsum('nkp,kpq->nkq', block_density, table[view], preferred_element_...  28.8 us
    mul x8, other arithmetic, shade_samples(): opacity = (1.0 - jnp.exp(-extinction)) * occupied  23 us
    ppermute x3, waiting for transfers between devices, swapped(): lax.ppermute(x, axis, [(i, i ^ 1 << distance) for i in range(lax.axis_siz...  20.7 us
    transpose x1, local copies, waits for them, and re-layouts, shards(): segments.reshape(rows, BC, 2, 4, brick_edge, brick_edge)  15.7 us
    another operation x1, local copies, waits for them, and re-layouts, shards(): tile_image.reshape(2, 4, depth_count, block_rows, tile_image.shape[3])  11.4 us
    select_n x8, other arithmetic, shade_samples(): occupied = jnp.where(flip, occupied[:, ::-1], occupied)  10.6 us
    another operation x1, local copies, waits for them, and re-layouts, shards(): segments.reshape(rows, BC, 2, 4, brick_edge, brick_edge)  8.66 us
  transfers between devices with their start and end apart: 3, of which 3 were waited for; matrix products, arithmetic and copies ran while one was open for 0% of the time, Pallas kernels for 0%

commit v1 on v0

v1 whole, which is shorter than its diff:
```python
import functools
import math

import jax
import jax.numpy as jnp
import numpy as np
from jax import lax
from jax.experimental import pallas as pl
from jax.experimental.pallas import tpu as pltpu
from jax.sharding import PartitionSpec as P

BC = 16
LANES = 128
SUB = 8
SHEAR = (0.45, -0.3)
LOG2E = 1.0 / math.log(2.0)

CODE_RANGE = 32.0
CODE_STEP = 2047.0
CODE_BIAS = 32768.0


def shear_taps(brick_edge, view):
    f32 = np.float32
    slice_index = np.arange(brick_edge, dtype=f32)[:, None]
    position = np.arange(brick_edge, dtype=f32)[None, :] + f32(SHEAR[view]) * (
        slice_index - f32((brick_edge - 1) / 2.0)
    )
    anchor = np.floor(position)
    fraction = (position - anchor).astype(f32)
    low = (f32(1.0) - fraction).astype(jnp.bfloat16).astype(f32)
    high = fraction.astype(jnp.bfloat16).astype(f32)
    return anchor.astype(np.int32), low, high


def shear_lines(brick_edge, view):
    anchor, low, high = shear_taps(brick_edge, view)
    source = np.arange(brick_edge)[None, :, None]
    table = np.where(source == anchor[:, None, :], low[:, None, :], 0.0)
    return table + np.where(source == anchor[:, None, :] + 1, high[:, None, :], 0.0)


def shear_tables(edge):
    along_cols = shear_lines(edge, 0)
    along_rows = shear_lines(edge, 1)
    block = np.stack([np.kron(np.eye(LANES // edge), t) for t in along_cols])
    full = np.stack([np.kron(t, np.eye(edge)) for t in along_rows])
    lane = np.arange(LANES)
    turned = (-(lane // edge) % (LANES // edge)) * edge + lane % edge
    block = block[:, :, turned]
    full = full.reshape(edge, edge * edge, -1, LANES)[..., turned].reshape(full.shape)
    return block.astype(jnp.bfloat16), full.astype(jnp.bfloat16)


def encode(x):
    logs = jnp.log(jnp.maximum(x, 2.0**-CODE_RANGE))
    code = logs * (CODE_STEP * LOG2E) + (CODE_RANGE * CODE_STEP + 0.5)
    return (code.astype(jnp.int32) - int(CODE_BIAS)).astype(jnp.int16)


def decode(code):
    value = code.astype(jnp.int32).astype(jnp.float32)
    return jnp.exp2(value * (1.0 / CODE_STEP) + (CODE_BIAS / CODE_STEP - CODE_RANGE))


def bit_of(value, bit):
    return lax.bitwise_and(lax.shift_right_logical(value, bit), 1)


def spread_bit(slot, position, bit):
    high = lax.shift_left(lax.shift_right_logical(slot, position), position + 1)
    low = lax.bitwise_and(slot, (1 << position) - 1)
    return high + low + bit * (1 << position)


def render_kernel(
    rounds, keep, low_bits, edge,
    order, cgain, cbias, egain, ebias, cost, bricks, table0, table1,
    out_send, out_keep,
    xin, tab0, tab1, moved, samples, perm, levels, sems,
):
    me = lax.axis_index("depth")
    rows, slabs = xin.shape[0], order.shape[1]
    chunk_bricks = rows * BC
    plane = edge * edge
    halves = plane // LANES
    top = bit_of(me, rounds - 1)
    half = top if keep else 1 - top
    first = half * chunk_bricks

    copies = []
    for r in range(rows):
        copies.append(
            pltpu.make_async_copy(bricks.at[pl.ds(first + r * BC, BC)], xin.at[r], sems.at[r])
        )
    for h in range(halves):
        span = pl.ds(h * LANES, LANES)
        copies.append(pltpu.make_async_copy(table0, tab0.at[:, span, span], sems.at[rows + h]))
    copies.append(pltpu.make_async_copy(table1, tab1, sems.at[rows + halves]))
    for copy in copies:
        copy.start()

    size = BC * edge
    out_row = lax.broadcasted_iota(jnp.int32, (size, size), 0)
    in_row = lax.broadcasted_iota(jnp.int32, (size, size), 1)
    wanted = lax.rem(out_row, BC) * edge + out_row // BC
    perm[...] = jnp.where(wanted == in_row, 1.0, 0.0).astype(jnp.bfloat16)

    here = lax.broadcasted_iota(jnp.int32, (chunk_bricks, chunk_bricks), 0)
    there = lax.broadcasted_iota(jnp.int32, (chunk_bricks, chunk_bricks), 1)
    cost_row = jnp.where(
        half == 0, cost[0:1, :chunk_bricks], cost[0:1, chunk_bricks:]
    ).astype(jnp.float32)
    picked = jnp.where(here == there, cost_row, 0.0).astype(jnp.bfloat16)
    levels[...] = jnp.dot(
        picked, jnp.ones((chunk_bricks, LANES), jnp.bfloat16), preferred_element_type=jnp.float32
    )

    zero = jnp.zeros((LANES, LANES), jnp.bfloat16)
    for k in range(edge):
        for a in range(halves):
            for b in range(halves):
                if a != b:
                    tab0[k, a * LANES : (a + 1) * LANES, b * LANES : (b + 1) * LANES] = zero

    for r in range(rows):
        copies[r].wait()
        line = xin[r].reshape(size, plane)
        slices = jnp.dot(perm[...], line, preferred_element_type=jnp.float32).astype(jnp.bfloat16)
        for k in range(edge):
            moved[k, r * BC : (r + 1) * BC, :] = slices[k * BC : (k + 1) * BC, :]

    flips = [order[v, 0] > order[v, slabs - 1] for v in range(2)]

    def resample(v, k):
        table = tab0 if v == 0 else tab1
        result = jnp.dot(moved[k], table[k], preferred_element_type=jnp.float32)
        place = jnp.where(flips[v], edge - 1 - k, k)
        for h in range(halves):
            samples[v, place, h] = result[:, h * LANES : (h + 1) * LANES]

    ext_slope = egain[0] * LOG2E
    ext_shift = ebias[0] * LOG2E + math.log2(LOG2E)
    slopes = [cgain[c] * 0.5 for c in range(3)]
    shifts = [cbias[c] * 0.5 for c in range(3)]
    mine = bit_of(me, 0)
    per_kind = chunk_bricks // SUB * halves // 2
    per_level = edge // 4

    def shade(v, item, kind, out):
        slot, group = item // 2, lax.rem(item, 2)
        unit = spread_bit(slot, low_bits, mine if kind == 0 else 1 - mine)
        h = lax.rem(unit, halves)
        start = pl.multiple_of((unit // halves) * BC + group * SUB, SUB)
        level = levels[pl.ds(start, SUB), :]
        shift = []
        for j in range(4):
            need = jnp.where(flips[v], 3 - j, j).astype(jnp.float32)
            shift.append(jnp.where(level > need, ext_shift, -1e30))
        clear = jnp.ones((SUB, LANES), jnp.float32)
        sums = [jnp.zeros((SUB, LANES), jnp.float32) for _ in range(3)]
        for k in range(edge):
            s = samples[v, k, h, pl.ds(start, SUB), :]
            passed = jnp.exp2(-jnp.exp2(s * ext_slope + shift[k // per_level]))
            beyond = clear * passed
            weight = clear - beyond
            clear = beyond
            for c in range(3):
                sums[c] = sums[c] + weight * jnp.tanh(s * slopes[c] + shifts[c])
        opacity = 1.0 - clear
        place = pl.multiple_of(group * SUB, SUB)
        for c in range(3):
            out[slot, v, c, pl.ds(place, SUB), :] = (opacity + sums[c]) * 0.5
        out[slot, v, 3, pl.ds(place, SUB), :] = opacity

    for h in range(halves):
        copies[rows + h].wait()
    for k in range(edge):
        resample(0, k)
    copies[rows + halves].wait()

    def both(i, carry):
        resample(1, i)
        for kind, out in ((1, out_send), (0, out_keep)):
            for n in range(per_kind // edge):
                shade(0, i * (per_kind // edge) + n, kind, out)
        return carry

    lax.fori_loop(0, edge, both, 0)

    def last(i, carry):
        for kind, out in ((1, out_send), (0, out_keep)):
            shade(1, i, kind, out)
        return carry

    lax.fori_loop(0, per_kind, last, 0)


def render(rounds, keep, low_bits, scalars, cost, bricks, table0, table1):
    total, edge, plane = bricks.shape
    rows = total // BC // 2
    chunk = rows * BC
    halves = plane // LANES
    units = rows * halves
    shape = jax.ShapeDtypeStruct((units // 2, 2, 4, BC, LANES), jnp.float32)
    smem = pl.BlockSpec(memory_space=pltpu.SMEM)
    vmem = pl.BlockSpec(memory_space=pltpu.VMEM)
    hbm = pl.BlockSpec(memory_space=pl.ANY)
    return pl.pallas_call(
        functools.partial(render_kernel, rounds, keep, low_bits, edge),
        out_shape=(shape, shape),
        in_specs=[smem] * 5 + [vmem, hbm, hbm, hbm],
        out_specs=(vmem, vmem),
        scratch_shapes=[
            pltpu.VMEM((rows, BC, edge, plane), jnp.bfloat16),
            pltpu.VMEM((edge, plane, plane), jnp.bfloat16),
            pltpu.VMEM((edge, plane, plane), jnp.bfloat16),
            pltpu.VMEM((edge, chunk, plane), jnp.bfloat16),
            pltpu.VMEM((2, edge, halves, chunk, LANES), jnp.float32),
            pltpu.VMEM((BC * edge, BC * edge), jnp.bfloat16),
            pltpu.VMEM((chunk, LANES), jnp.float32),
            pltpu.SemaphoreType.DMA((rows + halves + 1,)),
        ],
        compiler_params=pltpu.CompilerParams(vmem_limit_bytes=32 << 20),
        cost_estimate=pl.CostEstimate(
            flops=int(4e6), bytes_accessed=4 << 20, transcendentals=chunk * edge * plane * 10
        ),
        name="render",
    )(*scalars, cost, bricks, table0, table1)


def merged_pair(front_bit, kept, incoming):
    behind = 1.0 - front_bit * incoming[3]
    ahead = 1.0 - (1.0 - front_bit) * kept[3]
    return [kept[c] * behind + incoming[c] * ahead for c in range(4)]


def merge_kernel(bit, low_bits, mode, order, kept, incoming, *outs):
    me = lax.axis_index("depth")
    coded = incoming.dtype == jnp.int16
    units = kept.shape[0]
    mine = bit_of(me, bit + 1)
    for v in range(2):
        front = bit_of(lax.bitwise_xor(me, order[v, 0]), bit).astype(jnp.float32)

        def one(slot, kind, out):
            unit = slot if kind is None else spread_bit(slot, low_bits, mine if kind == 0 else 1 - mine)
            came = [incoming[unit, v, c] for c in range(4)]
            if coded:
                came = [decode(x) for x in came]
            done = merged_pair(front, [kept[unit, v, c] for c in range(4)], came)
            for c in range(4):
                out[slot, v, c] = encode(done[c]) if out.dtype == jnp.int16 else done[c]

        if mode == "split":
            for kind, out in ((1, outs[0]), (0, outs[1])):
                for slot in range(units // 2):
                    one(slot, kind, out)
        else:
            for slot in range(units):
                one(slot, None, outs[0])


def merge(bit, low_bits, mode, order, kept, incoming):
    units = kept.shape[0]
    tail = kept.shape[1:]
    if mode == "split":
        outs = (
            jax.ShapeDtypeStruct((units // 2,) + tail, jnp.int16),
            jax.ShapeDtypeStruct((units // 2,) + tail, jnp.float32),
        )
    elif mode == "send":
        outs = (jax.ShapeDtypeStruct((units,) + tail, jnp.int16),)
    else:
        outs = (jax.ShapeDtypeStruct((units,) + tail, jnp.float32),)
    vmem = pl.BlockSpec(memory_space=pltpu.VMEM)
    return pl.pallas_call(
        functools.partial(merge_kernel, bit, low_bits, mode),
        out_shape=outs,
        in_specs=[pl.BlockSpec(memory_space=pltpu.SMEM), vmem, vmem],
        out_specs=tuple(vmem for _ in outs),
        compiler_params=pltpu.CompilerParams(vmem_limit_bytes=8 << 20),
        cost_estimate=pl.CostEstimate(flops=int(4e5), bytes_accessed=kept.size * 8, transcendentals=0),
        name="merge",
    )(order, kept, incoming)


def finish_kernel(bit, edge, order, kept, incoming, out):
    me = lax.axis_index("depth")
    units = kept.shape[0]
    chunks = LANES // edge
    chunk_of = lax.broadcasted_iota(jnp.int32, (SUB, LANES), 1) // edge
    for v in range(2):
        front = bit_of(lax.bitwise_xor(me, order[v, 0]), bit).astype(jnp.float32)
        for unit in range(units):
            came = [decode(incoming[unit, v, c]) for c in range(4)]
            done = merged_pair(front, [kept[unit, v, c] for c in range(4)], came)
            for c in range(4):
                for g in range(BC // SUB):
                    x = done[c][g * SUB : (g + 1) * SUB, :]
                    x = pltpu.roll(x, 0, 1, stride=edge, stride_axis=0)
                    for step in range(3):
                        turned = pltpu.roll(x, SUB - (1 << step), 0)
                        x = jnp.where(bit_of(chunk_of, step) == 1, turned, x)
                    x = pltpu.roll(x, 0, 1, stride=edge, stride_axis=0)
                    out[v, c, unit * chunks : (unit + 1) * chunks, g * LANES : (g + 1) * LANES] = x


def finish(bit, edge, order, kept, incoming):
    units = kept.shape[0]
    vmem = pl.BlockSpec(memory_space=pltpu.VMEM)
    return pl.pallas_call(
        functools.partial(finish_kernel, bit, edge),
        out_shape=jax.ShapeDtypeStruct((2, 4, units * LANES // edge, BC * edge), jnp.float32),
        in_specs=[pl.BlockSpec(memory_space=pltpu.SMEM), vmem, vmem],
        out_specs=vmem,
        compiler_params=pltpu.CompilerParams(vmem_limit_bytes=8 << 20),
        cost_estimate=pl.CostEstimate(flops=int(4e5), bytes_accessed=kept.size * 8, transcendentals=0),
        name="finish",
    )(order, kept, incoming)


def swapped(x, bit):
    count = lax.axis_size("depth")
    return lax.ppermute(x, "depth", [(i, i ^ 1 << bit) for i in range(count)])


def shards(bricks, cost, order, color_gain, color_bias, ext_gain, ext_bias):
    bricks = bricks[0]
    total, edge, plane = bricks.shape
    count = lax.axis_size("depth")
    rounds = count.bit_length() - 1
    units = total // BC * (plane // LANES)
    low_bits = (units // count).bit_length() - 1
    table0, table1 = (jnp.asarray(t) for t in shear_tables(edge))
    scalars = (order, color_gain, color_bias, ext_gain, ext_bias)

    halves = []
    for keep in (False, True):
        halves.append(render(rounds, keep, low_bits, scalars, cost, bricks, table0, table1))
    parts = []
    for keep, (send, kept) in zip((False, True), halves):
        for bit in range(rounds - 1):
            incoming = swapped(send, bit)
            if bit < rounds - 2:
                send, kept = merge(bit, low_bits, "split", order, kept, incoming)
            else:
                (done,) = merge(bit, low_bits, "keep" if keep else "send", order, kept, incoming)
        parts.append(done)
    incoming = swapped(parts[0], rounds - 1)
    return finish(rounds - 1, edge, order, parts[1], incoming)


def solution(mesh):
    in_specs = (P("depth", "image", None, None), P("depth", "image"), P(), P(), P(), P(), P())
    out_specs = P(None, None, "depth", "image")
    return jax.shard_map(shards, mesh=mesh, in_specs=in_specs, out_specs=out_specs, check_vma=False)
```

time: 263 us -> 46.4 us (0.18)
  other arithmetic: 144 us -> 0 us
  local copies, waits for them, and re-layouts: 60.8 us -> 6.88 us
  matrix products: 28.8 us -> 0 us
  Pallas kernels: 0 us -> 26.3 us
  waiting for transfers between devices: 20.7 us -> 5.01 us
    reduce_sum x16 -> x0, other arithmetic: 100 us -> none  [shade_samples(): jnp.sum(weight * jax.nn.sigmoid(color_gain[channel] * samples + color_bia...]
    dot_general x16 -> x0, matrix products: 28.8 us -> none  [render_block(): jnp.einsum('nkp,kpq->nkq', block_density, table[view], preferred_element_...]
    pallas_call x0 -> x7, Pallas kernels: none -> 26.3 us  [the longest x2 22 us: render(): pl.pallas_call(functools.partial(render_kernel, rounds, keep, low_bits, e...]
    mul x29 -> x0, other arithmetic: 23.2 us -> none  [the longest x8 23 us: shade_samples(): opacity = (1.0 - jnp.exp(-extinction)) * occupied]
    another operation x11 -> x0, local copies, waits for them, and re-layouts: 20.2 us -> none  [the longest x1 11.4 us: shards(): tile_image.reshape(2, 4, depth_count, block_rows, tile_image.shape[3])]
    transpose x1 -> x0, local copies, waits for them, and re-layouts: 15.7 us -> none  [shards(): segments.reshape(rows, BC, 2, 4, brick_edge, brick_edge)]
    ppermute x3 -> x5, waiting for transfers between devices: 20.7 us -> 5.01 us  [swapped(): return lax.ppermute(x, 'depth', [(i, i ^ 1 << bit) for i in range(count)])]
    select_n x18 -> x0, other arithmetic: 12.3 us -> none  [the longest x8 10.6 us: shade_samples(): occupied = jnp.where(flip, occupied[:, ::-1], occupied)]
  transfers between devices with their start and end apart: 3 -> 5, of which waited for: 3 -> 2; matrix products, arithmetic and copies ran while one was open for 0% -> 0% of each run, Pallas kernels for 0% -> 30%
where the time goes in v1:
time: 46.4 us; the launch traced here: 46.1 us
  Pallas kernels  26.3 us (57%)
  local copies, waits for them, and re-layouts  6.88 us (15%)
  starting transfers between devices  6.58 us (14%)
  waiting for transfers between devices  5.01 us (11%)
  between operations  1.36 us (3%)
    pallas_call x2, Pallas kernels, render(): pl.pallas_call(functools.partial(render_kernel, rounds, keep, low_bits, e...  22 us
    unnamed x14, local copies, waits for them, and re-layouts  6.88 us
    ppermute x5, starting transfers between devices, swapped(): return lax.ppermute(x, 'depth', [(i, i ^ 1 << bit) for i in range(count)])  6.58 us
    ppermute x5, waiting for transfers between devices, swapped(): return lax.ppermute(x, 'depth', [(i, i ^ 1 << bit) for i in range(count)])  5.01 us
    pallas_call x4, Pallas kernels, merge(): pl.pallas_call(functools.partial(merge_kernel, bit, low_bits, mode), out_...  2.78 us
    pallas_call x1, Pallas kernels, finish(): pl.pallas_call(functools.partial(finish_kernel, bit, edge), out_shape=jax...  1.54 us
  transfers between devices with their start and end apart: 5, of which 2 were waited for; matrix products, arithmetic and copies ran while one was open for 0% of the time, Pallas kernels for 30%

profile of v1, /device:TPU:0, one launch (start us, length us, event | category | flops | bytes accessed | tf_op | source)
XLA Modules:
  0.0 46.1 jit_solution(14995847681990215572)
XLA Ops:
  1.3 0.0 copy-start
  1.3 0.7 %copy-done = s32[2,8]{1,0:T(2,128)S(1)} copy-done((s32[2,8]{1,0:T(2,128)S(1)}, s32[2,8]{1,0:T(2,128)}, u32[]{:S(2)}) %copy-start) | copy-done | bytes 88
  2.0 0.0 copy-start.1
  2.0 1.6 %copy-done.1 = bf16[1,256,16,256]{3,2,1,0:T(8,128)(2,1)S(1)} copy-done((bf16[1,256,16,256]{3,2,1,0:T(8,128)(2,1)S(1)}, bf16[1,256,16,256]{3,2,1,0:T(8,128)(2,1)}, u32[]{:S(2)}) %copy-start.1) | copy-done | bytes 2097176
  3.6 0.0 copy-start.2
  3.6 0.7 %copy-done.2 = s32[1,256]{1,0:T(1,128)S(1)} copy-done((s32[1,256]{1,0:T(1,128)S(1)}, s32[1,256]{1,0:T(1,128)}, u32[]{:S(2)}) %copy-start.2) | copy-done | bytes 1048
  4.2 0.0 copy-start.3
  4.3 0.7 %copy-done.3 = f32[3]{0:T(128)S(1)} copy-done((f32[3]{0:T(128)S(1)}, f32[3]{0:T(128)}, u32[]{:S(2)}) %copy-start.3) | copy-done | bytes 36
  4.9 0.0 copy-start.4
  4.9 0.7 %copy-done.4 = f32[3]{0:T(128)S(1)} copy-done((f32[3]{0:T(128)S(1)}, f32[3]{0:T(128)}, u32[]{:S(2)}) %copy-start.4) | copy-done | bytes 36
  5.6 0.0 copy-start.5
  5.6 1.6 %copy-done.5 = bf16[16,256,256]{2,1,0:T(8,128)(2,1)S(1)} copy-done((bf16[16,256,256]{2,1,0:T(8,128)(2,1)S(1)}, bf16[16,256,256]{2,1,0:T(8,128)(2,1)}, u32[]{:S(2)}) %copy-start.5) | copy-done | bytes 2097176
  7.2 0.0 copy-start.6
  7.2 1.0 %copy-done.6 = bf16[16,128,128]{2,1,0:T(8,128)(2,1)S(1)} copy-done((bf16[16,128,128]{2,1,0:T(8,128)(2,1)S(1)}, bf16[16,128,128]{2,1,0:T(8,128)(2,1)}, u32[]{:S(2)}) %copy-start.6) | copy-done | bytes 524312
  8.2 11.0 %render.3 = (f32[8,2,4,16,128]{4,3,2,1,0:T(8,128)S(1)}, f32[8,2,4,16,128]{4,3,2,1,0:T(8,128)S(1)}) custom-call(s32[2,8]{1,0:T(2,128)S(1)} %copy-done, f32[3]{0:T(128)S(1)} %copy-done.3, f32[3]{0:T(128)S(1)} %copy-done.4, f32[1]{0:T(128)S(6)} %copy.10.egain, f32[1]{0:T(128)S(6)} %copy.11.ebias, s32[1,256]{1,0:T(1,128)S(1)} %copy-done.2, ...), custom_call_target="tpu_custom_call" | custom-call | flops 4000000 | bytes 4194304 | tf_op jit(solution)/shard_map/render/pallas_call | solution.py:209
  19.2 0.6 %collective-permute-start.2 = (f32[8,2,4,16,128]{4,3,2,1,0:T(8,128)S(1)}, f32[8,2,4,16,128]{4,3,2,1,0:T(8,128)S(1)}, u32[]{:S(2)}, u32[]{:S(2)}) collective-permute-start(f32[8,2,4,16,128]{4,3,2,1,0:T(8,128)S(1)} %get-tuple-element.18), channel_id=1, source_target_pairs={{0,4},{4,0},{8,12},{12,8},{16,20},{20,16},{24,28},{28,24},{1,5},{5... | collective-permute-start | bytes 1572872 | tf_op jit(solution)/shard_map/ppermute | solution.py:325
  19.7 11.0 %render.2 = (f32[8,2,4,16,128]{4,3,2,1,0:T(8,128)S(1)}, f32[8,2,4,16,128]{4,3,2,1,0:T(8,128)S(1)}) custom-call(s32[2,8]{1,0:T(2,128)S(1)} %copy-done, f32[3]{0:T(128)S(1)} %copy-done.3, f32[3]{0:T(128)S(1)} %copy-done.4, f32[1]{0:T(128)S(6)} %copy.10.egain, f32[1]{0:T(128)S(6)} %copy.11.ebias, s32[1,256]{1,0:T(1,128)S(1)} %copy-done.2, ...), custom_call_target="tpu_custom_call" | custom-call | flops 4000000 | bytes 4194304 | tf_op jit(solution)/shard_map/render/pallas_call | solution.py:209
  30.7 0.1 collective-permute-start
  30.8 0.0 collective-permute-done.2.incoming
  30.8 0.7 %merge.6 = (s16[4,2,4,16,128]{4,3,2,1,0:T(8,128)(2,1)S(1)}, f32[4,2,4,16,128]{4,3,2,1,0:T(8,128)S(1)}) custom-call(s32[2,8]{1,0:T(2,128)S(1)} %copy-done, f32[8,2,4,16,128]{4,3,2,1,0:T(8,128)S(1)} %get-tuple-element.17.kept, f32[8,2,4,16,128]{4,3,2,1,0:T(8,128)S(1)} %collective-permute-done.2.incoming), custom_call_target="tpu_custom_call" | custom-call | flops 400000 | bytes 1048576 | tf_op jit(solution)/shard_map/merge/pallas_call | solution.py:277
  31.5 3.0 %collective-permute-start.3 = (s16[4,2,4,16,128]{4,3,2,1,0:T(8,128)(2,1)S(1)}, s16[4,2,4,16,128]{4,3,2,1,0:T(8,128)(2,1)S(1)}, u32[]{:S(2)}, u32[]{:S(2)}) collective-permute-start(s16[4,2,4,16,128]{4,3,2,1,0:T(8,128)(2,1)S(1)} %get-tuple-element.20), channel_id=1, source_target_pairs={{0,8},{4,12},{8,0},{12,4},{16,24},{20,28},{24,16},{28,20},{1,9},{5... | collective-permute-start | bytes 393224 | tf_op jit(solution)/shard_map/ppermute | solution.py:325
  34.6 0.0 collective-permute-done.incoming
  34.6 0.7 %merge.4 = (s16[4,2,4,16,128]{4,3,2,1,0:T(8,128)(2,1)S(1)}, f32[4,2,4,16,128]{4,3,2,1,0:T(8,128)S(1)}) custom-call(s32[2,8]{1,0:T(2,128)S(1)} %copy-done, f32[8,2,4,16,128]{4,3,2,1,0:T(8,128)S(1)} %get-tuple-element.13.kept, f32[8,2,4,16,128]{4,3,2,1,0:T(8,128)S(1)} %collective-permute-done.incoming), custom_call_target="tpu_custom_call" | custom-call | flops 400000 | bytes 1048576 | tf_op jit(solution)/shard_map/merge/pallas_call | solution.py:277
  35.3 0.8 %collective-permute-start.1 = (s16[4,2,4,16,128]{4,3,2,1,0:T(8,128)(2,1)S(1)}, s16[4,2,4,16,128]{4,3,2,1,0:T(8,128)(2,1)S(1)}, u32[]{:S(2)}, u32[]{:S(2)}) collective-permute-start(s16[4,2,4,16,128]{4,3,2,1,0:T(8,128)(2,1)S(1)} %get-tuple-element.16), channel_id=1, source_target_pairs={{0,8},{4,12},{8,0},{12,4},{16,24},{20,28},{24,16},{28,20},{1,9},{5... | collective-permute-start | bytes 393224 | tf_op jit(solution)/shard_map/ppermute | solution.py:325
  36.1 2.7 %collective-permute-done.3.incoming = s16[4,2,4,16,128]{4,3,2,1,0:T(8,128)(2,1)S(1)} collective-permute-done((s16[4,2,4,16,128]{4,3,2,1,0:T(8,128)(2,1)S(1)}, s16[4,2,4,16,128]{4,3,2,1,0:T(8,128)(2,1)S(1)}, u32[]{:S(2)}, u32[]{:S(2)}) %collective-permute-start.3) | collective-permute-done | bytes 131104 | tf_op jit(solution)/shard_map/ppermute | solution.py:325
  38.8 0.7 %merge.7 = s16[4,2,4,16,128]{4,3,2,1,0:T(8,128)(2,1)S(1)} custom-call(s32[2,8]{1,0:T(2,128)S(1)} %copy-done, f32[4,2,4,16,128]{4,3,2,1,0:T(8,128)S(1)} %get-tuple-element.19.kept, s16[4,2,4,16,128]{4,3,2,1,0:T(8,128)(2,1)S(1)} %collective-permute-done.3.incoming), custom_call_target="tpu_custom_call" | custom-call | flops 400000 | bytes 524288 | tf_op jit(solution)/shard_map/merge/pallas_call | solution.py:277
  39.5 2.1 %collective-permute-start.4 = (s16[4,2,4,16,128]{4,3,2,1,0:T(8,128)(2,1)S(1)}, s16[4,2,4,16,128]{4,3,2,1,0:T(8,128)(2,1)S(1)}, u32[]{:S(2)}, u32[]{:S(2)}) collective-permute-start(s16[4,2,4,16,128]{4,3,2,1,0:T(8,128)(2,1)S(1)} %merge.7), channel_id=1, source_target_pairs={{0,16},{4,20},{8,24},{12,28},{16,0},{20,4},{24,8},{28,12},{1,17},{... | collective-permute-start | bytes 393224 | tf_op jit(solution)/shard_map/ppermute | solution.py:325
  41.6 0.0 collective-permute-done.1.incoming
  41.6 0.6 %merge.5.kept = f32[4,2,4,16,128]{4,3,2,1,0:T(8,128)S(1)} custom-call(s32[2,8]{1,0:T(2,128)S(1)} %copy-done, f32[4,2,4,16,128]{4,3,2,1,0:T(8,128)S(1)} %get-tuple-element.15.kept, s16[4,2,4,16,128]{4,3,2,1,0:T(8,128)(2,1)S(1)} %collective-permute-done.1.incoming), custom_call_target="tpu_custom_call" | custom-call | flops 400000 | bytes 524288 | tf_op jit(solution)/shard_map/merge/pallas_call | solution.py:277
  42.3 2.3 %collective-permute-done.4.incoming = s16[4,2,4,16,128]{4,3,2,1,0:T(8,128)(2,1)S(1)} collective-permute-done((s16[4,2,4,16,128]{4,3,2,1,0:T(8,128)(2,1)S(1)}, s16[4,2,4,16,128]{4,3,2,1,0:T(8,128)(2,1)S(1)}, u32[]{:S(2)}, u32[]{:S(2)}) %collective-permute-start.4) | collective-permute-done | bytes 131104 | tf_op jit(solution)/shard_map/ppermute | solution.py:325
  44.6 1.5 %finish.1 = f32[2,4,32,256]{3,2,1,0:T(8,128)} custom-call(s32[2,8]{1,0:T(2,128)S(1)} %copy-done, f32[4,2,4,16,128]{4,3,2,1,0:T(8,128)S(1)} %merge.5.kept, s16[4,2,4,16,128]{4,3,2,1,0:T(8,128)(2,1)S(1)} %collective-permute-done.4.incoming), custom_call_target="tpu_custom_call" | custom-call | flops 400000 | bytes 524288 | tf_op jit(solution)/shard_map/finish/pallas_call | solution.py:312
Async XLA Ops:
  1.3 0.7 %copy-start = (s32[2,8]{1,0:T(2,128)S(1)}, s32[2,8]{1,0:T(2,128)}, u32[]{:S(2)}) copy-start(s32[2,8]{1,0:T(2,128)} %order.13) | copy-start | bytes 196
  2.0 1.6 %copy-start.1 = (bf16[1,256,16,256]{3,2,1,0:T(8,128)(2,1)S(1)}, bf16[1,256,16,256]{3,2,1,0:T(8,128)(2,1)}, u32[]{:S(2)}) copy-start(bf16[1,256,16,256]{3,2,1,0:T(8,128)(2,1)} %param.9) | copy-start | bytes 6291460
  3.6 0.7 %copy-start.2 = (s32[1,256]{1,0:T(1,128)S(1)}, s32[1,256]{1,0:T(1,128)}, u32[]{:S(2)}) copy-start(s32[1,256]{1,0:T(1,128)} %cost.3) | copy-start | bytes 3076
  4.2 0.7 %copy-start.3 = (f32[3]{0:T(128)S(1)}, f32[3]{0:T(128)}, u32[]{:S(2)}) copy-start(f32[3]{0:T(128)} %cgain.3) | copy-start | bytes 40
  4.9 0.7 %copy-start.4 = (f32[3]{0:T(128)S(1)}, f32[3]{0:T(128)}, u32[]{:S(2)}) copy-start(f32[3]{0:T(128)} %cbias.3) | copy-start | bytes 40
  5.6 1.6 %copy-start.5 = (bf16[16,256,256]{2,1,0:T(8,128)(2,1)S(1)}, bf16[16,256,256]{2,1,0:T(8,128)(2,1)}, u32[]{:S(2)}) copy-start(bf16[16,256,256]{2,1,0:T(8,128)(2,1)} %constant.5.clone.table1) | copy-start | bytes 6291460
  7.2 1.0 %copy-start.6 = (bf16[16,128,128]{2,1,0:T(8,128)(2,1)S(1)}, bf16[16,128,128]{2,1,0:T(8,128)(2,1)}, u32[]{:S(2)}) copy-start(bf16[16,128,128]{2,1,0:T(8,128)(2,1)} %constant.4.clone.table0) | copy-start | bytes 1572868
  19.2 11.6 %collective-permute-start.2 = (f32[8,2,4,16,128]{4,3,2,1,0:T(8,128)S(1)}, f32[8,2,4,16,128]{4,3,2,1,0:T(8,128)S(1)}, u32[]{:S(2)}, u32[]{:S(2)}) collective-permute-start(f32[8,2,4,16,128]{4,3,2,1,0:T(8,128)S(1)} %get-tuple-element.18), channel_id=1, source_target_pairs={{0,4},{4,0},{8,12},{12,8},{16,20},{20,16},{24,28},{28,24},{1,5},{5... | collective-permute-start | bytes 1572872 | tf_op jit(solution)/shard_map/ppermute | solution.py:325
  30.7 3.8 %collective-permute-start = (f32[8,2,4,16,128]{4,3,2,1,0:T(8,128)S(1)}, f32[8,2,4,16,128]{4,3,2,1,0:T(8,128)S(1)}, u32[]{:S(2)}, u32[]{:S(2)}) collective-permute-start(f32[8,2,4,16,128]{4,3,2,1,0:T(8,128)S(1)} %get-tuple-element.14), channel_id=1, source_target_pairs={{0,4},{4,0},{8,12},{12,8},{16,20},{20,16},{24,28},{28,24},{1,5},{5... | collective-permute-start | bytes 1572872 | tf_op jit(solution)/shard_map/ppermute | solution.py:325
  31.5 7.3 %collective-permute-start.3 = (s16[4,2,4,16,128]{4,3,2,1,0:T(8,128)(2,1)S(1)}, s16[4,2,4,16,128]{4,3,2,1,0:T(8,128)(2,1)S(1)}, u32[]{:S(2)}, u32[]{:S(2)}) collective-permute-start(s16[4,2,4,16,128]{4,3,2,1,0:T(8,128)(2,1)S(1)} %get-tuple-element.20), channel_id=1, source_target_pairs={{0,8},{4,12},{8,0},{12,4},{16,24},{20,28},{24,16},{28,20},{1,9},{5... | collective-permute-start | bytes 393224 | tf_op jit(solution)/shard_map/ppermute | solution.py:325
  35.3 6.3 %collective-permute-start.1 = (s16[4,2,4,16,128]{4,3,2,1,0:T(8,128)(2,1)S(1)}, s16[4,2,4,16,128]{4,3,2,1,0:T(8,128)(2,1)S(1)}, u32[]{:S(2)}, u32[]{:S(2)}) collective-permute-start(s16[4,2,4,16,128]{4,3,2,1,0:T(8,128)(2,1)S(1)} %get-tuple-element.16), channel_id=1, source_target_pairs={{0,8},{4,12},{8,0},{12,4},{16,24},{20,28},{24,16},{28,20},{1,9},{5... | collective-permute-start | bytes 393224 | tf_op jit(solution)/shard_map/ppermute | solution.py:325
  39.5 5.0 %collective-permute-start.4 = (s16[4,2,4,16,128]{4,3,2,1,0:T(8,128)(2,1)S(1)}, s16[4,2,4,16,128]{4,3,2,1,0:T(8,128)(2,1)S(1)}, u32[]{:S(2)}, u32[]{:S(2)}) collective-permute-start(s16[4,2,4,16,128]{4,3,2,1,0:T(8,128)(2,1)S(1)} %merge.7), channel_id=1, source_target_pairs={{0,16},{4,20},{8,24},{12,28},{16,0},{20,4},{24,8},{28,12},{1,17},{... | collective-permute-start | bytes 393224 | tf_op jit(solution)/shard_map/ppermute | solution.py:325

commit v2 on v1

v2 whole, which is shorter than its diff:
```python
import functools
import math

import jax
import jax.numpy as jnp
import numpy as np
from jax import lax
from jax.experimental import pallas as pl
from jax.experimental.pallas import tpu as pltpu
from jax.sharding import PartitionSpec as P

BC = 16
LANES = 128
SUB = 8
SHEAR = (0.45, -0.3)
LOG2E = 1.0 / math.log(2.0)

CODE_RANGE = 32.0
CODE_STEP = 2047.0
CODE_BIAS = 32768.0


def shear_taps(brick_edge, view):
    f32 = np.float32
    slice_index = np.arange(brick_edge, dtype=f32)[:, None]
    position = np.arange(brick_edge, dtype=f32)[None, :] + f32(SHEAR[view]) * (
        slice_index - f32((brick_edge - 1) / 2.0)
    )
    anchor = np.floor(position)
    fraction = (position - anchor).astype(f32)
    low = (f32(1.0) - fraction).astype(jnp.bfloat16).astype(f32)
    high = fraction.astype(jnp.bfloat16).astype(f32)
    return anchor.astype(np.int32), low, high


def shear_lines(brick_edge, view):
    anchor, low, high = shear_taps(brick_edge, view)
    source = np.arange(brick_edge)[None, :, None]
    table = np.where(source == anchor[:, None, :], low[:, None, :], 0.0)
    return table + np.where(source == anchor[:, None, :] + 1, high[:, None, :], 0.0)


def shear_tables(edge):
    along_cols = shear_lines(edge, 0)
    along_rows = shear_lines(edge, 1)
    block = np.stack([np.kron(np.eye(LANES // edge), t) for t in along_cols])
    full = np.stack([np.kron(t, np.eye(edge)) for t in along_rows])
    lane = np.arange(LANES)
    turned = (-(lane // edge) % (LANES // edge)) * edge + lane % edge
    block = block[:, :, turned]
    full = full.reshape(edge, edge * edge, -1, LANES)[..., turned].reshape(full.shape)
    return block.astype(jnp.bfloat16), full.astype(jnp.bfloat16)


def encode(x):
    logs = jnp.log(jnp.maximum(x, 2.0**-CODE_RANGE))
    code = logs * (CODE_STEP * LOG2E) + (CODE_RANGE * CODE_STEP + 0.5)
    return (code.astype(jnp.int32) - int(CODE_BIAS)).astype(jnp.int16)


def decode(code):
    value = code.astype(jnp.int32).astype(jnp.float32)
    return jnp.exp2(value * (1.0 / CODE_STEP) + (CODE_BIAS / CODE_STEP - CODE_RANGE))


EXT_SLOPE, EXT_SHIFT, SLOPES, SHIFTS, FLIPS, FRONTS = 0, 1, 2, 5, 8, 10


def bit_of(value, bit):
    return lax.bitwise_and(lax.shift_right_logical(value, bit), 1)


def spread_bit(slot, position, bit):
    high = lax.shift_left(lax.shift_right_logical(slot, position), position + 1)
    low = lax.bitwise_and(slot, (1 << position) - 1)
    return high + low + bit * (1 << position)


def shade(item, bit, low_bits, v, samples, levels, splats, out):
    edge, halves = samples.shape[0], samples.shape[1]
    slot, group = item // 2, lax.rem(item, 2)
    unit = spread_bit(slot, low_bits, bit)
    h = lax.rem(unit, halves)
    start = pl.multiple_of((unit // halves) * BC + group * SUB, SUB)
    level = levels[pl.ds(start, SUB), :]
    flip = splats[FLIPS + v]
    ext_slope, ext_shift = splats[EXT_SLOPE], splats[EXT_SHIFT]
    shift = []
    for j in range(4):
        need = j + flip * (3 - 2 * j)
        shift.append(jnp.where(level > need, ext_shift, -1e30))
    clear = jnp.ones((SUB, LANES), jnp.float32)
    sums = [jnp.zeros((SUB, LANES), jnp.float32) for _ in range(3)]
    for k in range(edge):
        s = samples[k, h, pl.ds(start, SUB), :]
        passed = jnp.exp2(-jnp.exp2(s * ext_slope + shift[k // (edge // 4)]))
        beyond = clear * passed
        weight = clear - beyond
        clear = beyond
        for c in range(3):
            sums[c] = sums[c] + weight * jnp.tanh(s * splats[SLOPES + c] + splats[SHIFTS + c])
    opacity = 1.0 - clear
    place = pl.multiple_of(group * SUB, SUB)
    for c in range(3):
        out[slot, c, pl.ds(place, SUB), :] = (opacity + sums[c]) * 0.5
    out[slot, 3, pl.ds(place, SUB), :] = opacity


def shade_pair(i, low_bits, v, samples, levels, splats, send, kept):
    mine = bit_of(lax.axis_index("depth"), 0)
    shade(i, 1 - mine, low_bits, v, samples, levels, splats, send)
    shade(i, mine, low_bits, v, samples, levels, splats, kept)


def to_slices(lines, r, perm, moved):
    edge = moved.shape[0]
    x = lines[r].reshape(BC * edge, lines.shape[-1])
    slices = jnp.dot(perm[...], x, preferred_element_type=jnp.float32).astype(jnp.bfloat16)
    for k in range(edge):
        place = r * BC if isinstance(r, int) else pl.multiple_of(r * BC, BC)
        moved[k, pl.ds(place, BC), :] = slices[k * BC : (k + 1) * BC, :]


def resample(k, v, moved, table, splats, samples):
    edge, halves = samples.shape[0], samples.shape[1]
    result = jnp.dot(moved[k], table[k], preferred_element_type=jnp.float32)
    flip = splats[FLIPS + v, 0, 0] > 0.5
    place = jnp.where(flip, edge - 1 - k, k)
    for h in range(halves):
        samples[place, h] = result[:, h * LANES : (h + 1) * LANES]


def first_kernel(
    rounds, low_bits,
    order, cgain, cbias, egain, ebias, cost, bricks, table0, table1,
    send, kept, next_samples, next_lines, tab0, tab1, perm, levels, splats,
    lines, moved, samples, s_order, s_cgain, s_cbias, v_cost, sems,
):
    me = lax.axis_index("depth")
    rows, edge = lines.shape[0], moved.shape[0]
    halves = samples.shape[1]
    chunk = rows * BC
    top = bit_of(me, rounds - 1)
    small = [(order, s_order), (cgain, s_cgain), (cbias, s_cbias), (cost, v_cost)]
    pairs = list(small)
    pairs.append((bricks.at[pl.ds((1 - top) * rows, rows)], lines))
    for h in range(halves):
        span = pl.ds(h * LANES, LANES)
        pairs.append((table0, tab0.at[:, span, span]))
    pairs.append((table1, tab1))
    pairs.append((bricks.at[pl.ds(top * rows, rows)], next_lines))
    copies = [pltpu.make_async_copy(a, b, sems.at[i]) for i, (a, b) in enumerate(pairs)]
    for copy in copies:
        copy.start()

    size = BC * edge
    out_row = lax.broadcasted_iota(jnp.int32, (size, size), 0)
    in_row = lax.broadcasted_iota(jnp.int32, (size, size), 1)
    wanted = lax.rem(out_row, BC) * edge + out_row // BC
    perm[...] = jnp.where(wanted == in_row, 1.0, 0.0).astype(jnp.bfloat16)
    zero = jnp.zeros((LANES, LANES), jnp.bfloat16)
    for k in range(edge):
        for a in range(halves):
            for b in range(halves):
                if a != b:
                    tab0[k, a * LANES : (a + 1) * LANES, b * LANES : (b + 1) * LANES] = zero

    for copy in copies[: len(small)]:
        copy.wait()

    def splat(value):
        return jnp.full((SUB, LANES), value, jnp.float32)

    splats[EXT_SLOPE] = splat(egain[0] * LOG2E)
    splats[EXT_SHIFT] = splat(ebias[0] * LOG2E + math.log2(LOG2E))
    for c in range(3):
        splats[SLOPES + c] = splat(s_cgain[c] * 0.5)
        splats[SHIFTS + c] = splat(s_cbias[c] * 0.5)
    for v in range(2):
        flip = s_order[v, 0] > s_order[v, order.shape[1] - 1]
        splats[FLIPS + v] = splat(jnp.where(flip, 1.0, 0.0))
        rank = lax.bitwise_xor(me, s_order[v, 0])
        for bit in range(rounds):
            splats[FRONTS + v * rounds + bit] = splat(bit_of(rank, bit).astype(jnp.float32))

    here = lax.broadcasted_iota(jnp.int32, (chunk, chunk), 0)
    there = lax.broadcasted_iota(jnp.int32, (chunk, chunk), 1)
    low, high = v_cost[0:1, :chunk], v_cost[0:1, chunk:]
    ones = jnp.ones((chunk, LANES), jnp.bfloat16)
    for i, row in enumerate((jnp.where(top == 0, high, low), jnp.where(top == 0, low, high))):
        picked = jnp.where(here == there, row.astype(jnp.float32), 0.0).astype(jnp.bfloat16)
        levels[i] = jnp.dot(picked, ones, preferred_element_type=jnp.float32)

    copies[len(small)].wait()
    for r in range(rows):
        to_slices(lines, r, perm, moved)
    for h in range(halves):
        copies[len(small) + 1 + h].wait()
    for k in range(edge):
        resample(k, 0, moved, tab0, splats, samples)
    copies[len(small) + 1 + halves].wait()

    def step(i, carry):
        resample(i, 1, moved, tab1, splats, next_samples)
        shade_pair(i, low_bits, 0, samples, levels.at[0], splats, send, kept)
        return carry

    lax.fori_loop(0, edge, step, 0)
    copies[len(small) + 2 + halves].wait()


def second_kernel(low_bits, samples, lines, tab0, perm, levels, splats, send, kept, next_samples, moved):
    rows, edge = lines.shape[0], moved.shape[0]
    items = edge // rows

    def step(i, carry):
        to_slices(lines, i, perm, moved)
        shade_pair(i, low_bits, 1, samples, levels.at[0], splats, send, kept)
        return carry

    lax.fori_loop(0, rows, step, 0)

    def later(i, carry):
        for n in range(2):
            resample(i * 2 + n, 0, moved, tab0, splats, next_samples)
        shade_pair(rows + i, low_bits, 1, samples, levels.at[0], splats, send, kept)
        return carry

    lax.fori_loop(0, edge // 2, later, 0)


def third_kernel(low_bits, samples, moved, tab1, levels, splats, send, kept, next_samples):
    edge = samples.shape[0]

    def step(i, carry):
        resample(i, 1, moved, tab1, splats, next_samples)
        shade_pair(i, low_bits, 0, samples, levels.at[1], splats, send, kept)
        return carry

    lax.fori_loop(0, edge, step, 0)


def fourth_kernel(low_bits, samples, levels, splats, send, kept):
    edge = samples.shape[0]

    def step(i, carry):
        shade_pair(i, low_bits, 1, samples, levels.at[1], splats, send, kept)
        return carry

    lax.fori_loop(0, edge, step, 0)


VMEM = pl.BlockSpec(memory_space=pltpu.VMEM)
HBM = pl.BlockSpec(memory_space=pltpu.HBM)


def call(kernel, name, ins, outs, cycles, scratch=(), limit=4 << 20, specs=None):
    outs = tuple(jax.ShapeDtypeStruct(shape, dtype) for shape, dtype in outs)
    return pl.pallas_call(
        kernel,
        out_shape=outs,
        in_specs=specs or [VMEM] * len(ins),
        out_specs=tuple(VMEM for _ in outs),
        scratch_shapes=list(scratch),
        compiler_params=pltpu.CompilerParams(vmem_limit_bytes=limit),
        cost_estimate=pl.CostEstimate(flops=cycles * 4096, bytes_accessed=1 << 18, transcendentals=0),
        name=name,
    )(*ins)


def render(rounds, low_bits, order, cgain, cbias, egain, ebias, cost, bricks, table0, table1):
    total, edge, plane = bricks.shape
    rows = total // BC // 2
    chunk, halves, size = rows * BC, plane // LANES, BC * edge
    f32, bf16 = jnp.float32, jnp.bfloat16
    part = ((rows * halves // 2, 4, BC, LANES), f32)
    samples = ((edge, halves, chunk, LANES), f32)
    lines = ((rows, BC, edge, plane), bf16)
    moved = ((edge, chunk, plane), bf16)
    table = ((edge, plane, plane), bf16)
    square = ((size, size), bf16)
    levels = ((2, chunk, LANES), f32)
    splats = ((FRONTS + 2 * rounds, SUB, LANES), f32)
    bricks = bricks.reshape(total // BC, BC, edge, plane)
    far = lambda x: pltpu.with_memory_space_constraint(x, pltpu.HBM)
    ins = (far(order), far(cgain), far(cbias), egain, ebias, far(cost), far(bricks), far(table0), far(table1))
    specs = [HBM] * 3 + [pl.BlockSpec(memory_space=pltpu.SMEM)] * 2 + [HBM] * 4
    send0, kept0, samples1, lines_b, tab0, tab1, perm, levels_, splats_ = call(
        functools.partial(first_kernel, rounds, low_bits), "first", ins,
        (part, part, samples, lines, table, table, square, levels, splats), 6000,
        [pltpu.VMEM(*lines), pltpu.VMEM(*moved), pltpu.VMEM(*samples),
         pltpu.SMEM(order.shape, order.dtype), pltpu.SMEM(cgain.shape, f32), pltpu.SMEM(cbias.shape, f32),
         pltpu.VMEM(cost.shape, cost.dtype),
         pltpu.SemaphoreType.DMA((10 + halves,))],
        24 << 20, specs,
    )
    send1, kept1, samples_b0, moved_b = call(
        functools.partial(second_kernel, low_bits), "second", (samples1, lines_b, tab0, perm, levels_, splats_),
        (part, part, samples, moved), 3500, (), 16 << 20,
    )
    send2, kept2, samples_b1 = call(
        functools.partial(third_kernel, low_bits), "third", (samples_b0, moved_b, tab1, levels_, splats_),
        (part, part, samples), 3500, (), 16 << 20,
    )
    send3, kept3 = call(
        functools.partial(fourth_kernel, low_bits), "fourth", (samples_b1, levels_, splats_),
        (part, part), 3300, (), 8 << 20,
    )
    return splats_, [[(send0, kept0), (send1, kept1)], [(send2, kept2), (send3, kept3)]]


def merged_pair(front, kept, incoming):
    behind = 1.0 - front * incoming[3]
    ahead = 1.0 - (1.0 - front) * kept[3]
    return [kept[c] * behind + incoming[c] * ahead for c in range(4)]


def front_of(splats, v, rounds, bit):
    one = splats[FRONTS + v * rounds + bit]
    return jnp.concatenate([one] * (BC // SUB), axis=0)


def read(ref, unit):
    parts = [ref[unit, c] for c in range(4)]
    return [decode(x) for x in parts] if ref.dtype == jnp.int16 else parts


def merge_kernel(v, rounds, bit, low_bits, splats, kept, incoming, *outs):
    mine = bit_of(lax.axis_index("depth"), bit + 1)
    front = front_of(splats, v, rounds, bit)
    units = kept.shape[0]
    for i, out in enumerate(outs):
        for slot in range(units // len(outs)):
            unit = slot
            if len(outs) > 1:
                unit = spread_bit(slot, low_bits, 1 - mine if i == 0 else mine)
            done = merged_pair(front, read(kept, unit), read(incoming, unit))
            for c in range(4):
                out[slot, c] = encode(done[c]) if out.dtype == jnp.int16 else done[c]


def merge(v, rounds, bit, low_bits, split, splats, kept, incoming):
    units, tail = kept.shape[0], kept.shape[1:]
    outs = ((units, *tail), jnp.int16)
    outs = (((units // 2, *tail), jnp.int16), ((units // 2, *tail), jnp.float32)) if split else (outs,)
    kernel = functools.partial(merge_kernel, v, rounds, bit, low_bits)
    return call(kernel, "merge", (splats, kept, incoming), outs, 600)


def finish_kernel(rounds, edge, splats, *refs):
    out = refs[-1]
    units = out.shape[2] * edge // LANES
    chunks = LANES // edge
    chunk_of = lax.broadcasted_iota(jnp.int32, (SUB, LANES), 1) // edge
    for v in range(2):
        kept, near, far = refs[3 * v : 3 * v + 3]
        for unit in range(units):
            done = merged_pair(front_of(splats, v, rounds, rounds - 2), read(kept, unit), read(near, unit))
            done = merged_pair(front_of(splats, v, rounds, rounds - 1), done, read(far, unit))
            for c in range(4):
                for g in range(BC // SUB):
                    x = done[c][g * SUB : (g + 1) * SUB, :]
                    x = pltpu.roll(x, 0, 1, stride=edge, stride_axis=0)
                    for step in range(3):
                        turned = pltpu.roll(x, SUB - (1 << step), 0)
                        x = jnp.where(bit_of(chunk_of, step) == 1, turned, x)
                    x = pltpu.roll(x, 0, 1, stride=edge, stride_axis=0)
                    out[v, c, unit * chunks : (unit + 1) * chunks, g * LANES : (g + 1) * LANES] = x


def finish(rounds, edge, splats, ins):
    units = ins[0].shape[0]
    out = ((2, 4, units * LANES // edge, BC * edge), jnp.float32)
    return call(functools.partial(finish_kernel, rounds, edge), "finish", (splats, *ins), (out,), 1500)[0]


def swapped(x, bit):
    count = lax.axis_size("depth")
    return lax.ppermute(x, "depth", [(i, i ^ 1 << bit) for i in range(count)])


def shards(bricks, cost, order, color_gain, color_bias, ext_gain, ext_bias):
    bricks = bricks[0]
    total, edge, plane = bricks.shape
    count = lax.axis_size("depth")
    rounds = count.bit_length() - 1
    units = total // BC * (plane // LANES)
    low_bits = (units // count).bit_length() - 1
    table0, table1 = (jnp.asarray(t) for t in shear_tables(edge))
    splats, parts = render(
        rounds, low_bits, order, color_gain, color_bias, ext_gain, ext_bias, cost, bricks, table0, table1
    )
    last = {}
    for half in range(2):
        for v in range(2):
            send, kept = parts[half][v]
            for bit in range(rounds - 2):
                send, kept = merge(v, rounds, bit, low_bits, True, splats, kept, swapped(send, bit))
            incoming = swapped(send, rounds - 2)
            if half == 0:
                (leaving,) = merge(v, rounds, rounds - 2, low_bits, False, splats, kept, incoming)
                last[v] = swapped(leaving, rounds - 1)
            else:
                parts[half][v] = (kept, incoming)
    ins = []
    for v in range(2):
        ins += [*parts[1][v], last[v]]
    return finish(rounds, edge, splats, ins)


def solution(mesh):
    in_specs = (P("depth", "image", None, None), P("depth", "image"), P(), P(), P(), P(), P())
    out_specs = P(None, None, "depth", "image")
    return jax.shard_map(shards, mesh=mesh, in_specs=in_specs, out_specs=out_specs, check_vma=False)
```

time: 46.4 us -> 29.5 us (0.64)
  Pallas kernels: 26.3 us -> 14.8 us
  local copies, waits for them, and re-layouts: 6.88 us -> 0 us
  starting transfers between devices: 6.58 us -> 10.7 us
  waiting for transfers between devices: 5.01 us -> 2.47 us
    pallas_call x7 -> x11, Pallas kernels: 26.3 us -> 14.8 us  [call(): pl.pallas_call(kernel, out_shape=outs, in_specs=specs or [VMEM] * len(ins...]
    unnamed x14 -> x0, local copies, waits for them, and re-layouts: 6.88 us -> none
    ppermute x5 -> x10, starting transfers between devices: 6.58 us -> 10.7 us  [swapped(): return lax.ppermute(x, 'depth', [(i, i ^ 1 << bit) for i in range(count)])]
    ppermute x5 -> x10, waiting for transfers between devices: 5.01 us -> 2.47 us  [swapped(): return lax.ppermute(x, 'depth', [(i, i ^ 1 << bit) for i in range(count)])]
  transfers between devices with their start and end apart: 5 -> 10, of which waited for: 2 -> 3; matrix products, arithmetic and copies ran while one was open for 0% -> 0% of each run, Pallas kernels for 30% -> 18%
where the time goes in v2:
time: 29.5 us; the launch traced here: 29.3 us
  Pallas kernels  14.8 us (50%)
  starting transfers between devices  10.7 us (36%)
  waiting for transfers between devices  2.47 us (8%)
  between operations  1.35 us (5%)
    pallas_call x11, Pallas kernels, call(): pl.pallas_call(kernel, out_shape=outs, in_specs=specs or [VMEM] * len(ins...  14.8 us
    ppermute x10, starting transfers between devices, swapped(): return lax.ppermute(x, 'depth', [(i, i ^ 1 << bit) for i in range(count)])  10.7 us
    ppermute x10, waiting for transfers between devices, swapped(): return lax.ppermute(x, 'depth', [(i, i ^ 1 << bit) for i in range(count)])  2.47 us
  transfers between devices with their start and end apart: 10, of which 3 were waited for; matrix products, arithmetic and copies ran while one was open for 0% of the time, Pallas kernels for 18%

profile of v2, /device:TPU:0, one launch (start us, length us, event | category | flops | bytes accessed | tf_op | source)
XLA Modules:
  0.0 29.3 jit_solution(10479241998182184056)
XLA Ops:
  1.3 5.3 %first.1 = (f32[8,4,16,128]{3,2,1,0:T(8,128)S(1)}, f32[8,4,16,128]{3,2,1,0:T(8,128)S(1)}, f32[16,2,128,128]{3,2,1,0:T(8,128)S(1)}, bf16[8,16,16,256]{3,2,1,0:T(8...) custom-call(s32[2,8]{1,0:T(2,128)} %order.1, ...), custom_call_target="tpu_custom_call" | custom-call | flops 24576000 | bytes 262144 | tf_op jit(solution)/shard_map/first/pallas_call | solution.py:259
  6.6 3.2 %second.1 = (f32[8,4,16,128]{3,2,1,0:T(8,128)S(1)}, f32[8,4,16,128]{3,2,1,0:T(8,128)S(1)}, f32[16,2,128,128]{3,2,1,0:T(8,128)S(1)}, bf16[16,128,256]{2,1,0:T(8,128)(2,1)S(1)}) custom-call(f32[16,2,128,128]{3,2,1,0:T(8,128)S(1)} %get-tuple-element.32.samples, bf16[8,16,16,256]{3,2,1,0:T(8,128)(2,1)S(1)} %get-tuple-element.33.lines, ...), custom_call_target="tpu_custom_call" | custom-call | flops 14336000 | bytes 262144 | tf_op jit(solution)/shard_map/second/pallas_call | solution.py:259
  9.8 0.6 %collective-permute-start.7 = (f32[8,4,16,128]{3,2,1,0:T(8,128)S(1)}, f32[8,4,16,128]{3,2,1,0:T(8,128)S(1)}, u32[]{:S(2)}, u32[]{:S(2)}) collective-permute-start(f32[8,4,16,128]{3,2,1,0:T(8,128)S(1)} %get-tuple-element.54), channel_id=1, source_target_pairs={{0,4},{4,0},{8,12},{12,8},{16,20},{20,16},{24,28},{28,24},{1,5},{5... | collective-permute-start | bytes 786440 | tf_op jit(solution)/shard_map/ppermute | solution.py:379
  10.3 0.1 collective-permute-start.2
  10.4 2.8 %third.1 = (f32[8,4,16,128]{3,2,1,0:T(8,128)S(1)}, f32[8,4,16,128]{3,2,1,0:T(8,128)S(1)}, f32[16,2,128,128]{3,2,1,0:T(8,128)S(1)}) custom-call(f32[16,2,128,128]{3,2,1,0:T(8,128)S(1)} %get-tuple-element.37.samples, bf16[16,128,256]{2,1,0:T(8,128)(2,1)S(1)} %get-tuple-element.38.moved, bf16[16,256,256]{2,1,0:T(8,128)(2,1)S(1)} %get-tuple-element.39.tab1, ...), custom_call_target="tpu_custom_call" | custom-call | flops 14336000 | bytes 262144 | tf_op jit(solution)/shard_map/third/pallas_call | solution.py:259
  13.2 0.5 %collective-permute-start = (f32[8,4,16,128]{3,2,1,0:T(8,128)S(1)}, f32[8,4,16,128]{3,2,1,0:T(8,128)S(1)}, u32[]{:S(2)}, u32[]{:S(2)}) collective-permute-start(f32[8,4,16,128]{3,2,1,0:T(8,128)S(1)} %get-tuple-element.41), channel_id=1, source_target_pairs={{0,4},{4,0},{8,12},{12,8},{16,20},{20,16},{24,28},{28,24},{1,5},{5... | collective-permute-start | bytes 786440 | tf_op jit(solution)/shard_map/ppermute | solution.py:379
  13.7 2.0 %fourth.1 = (f32[8,4,16,128]{3,2,1,0:T(8,128)S(1)}, f32[8,4,16,128]{3,2,1,0:T(8,128)S(1)}) custom-call(f32[16,2,128,128]{3,2,1,0:T(8,128)S(1)} %get-tuple-element.48.samples, f32[2,128,128]{2,1,0:T(8,128)S(1)} %get-tuple-element.36.levels, f32[16,8,128]{2,1,0:T(8,128)S(1)} %get-tuple-element.31.splats), custom_call_target="tpu_custom_call" | custom-call | flops 13516800 | bytes 262144 | tf_op jit(solution)/shard_map/fourth/pallas_call | solution.py:259
  15.7 0.1 collective-permute-start.5
  15.8 0.0 collective-permute-done.7.incoming
  15.8 0.1 merge.10
  15.9 3.0 %collective-permute-start.8 = (s16[4,4,16,128]{3,2,1,0:T(8,128)(2,1)S(1)}, s16[4,4,16,128]{3,2,1,0:T(8,128)(2,1)S(1)}, u32[]{:S(2)}, u32[]{:S(2)}) collective-permute-start(s16[4,4,16,128]{3,2,1,0:T(8,128)(2,1)S(1)} %get-tuple-element.56), channel_id=1, source_target_pairs={{0,8},{4,12},{8,0},{12,4},{16,24},{20,28},{24,16},{28,20},{1,9},{5... | collective-permute-start | bytes 196616 | tf_op jit(solution)/shard_map/ppermute | solution.py:379
  18.9 0.0 collective-permute-done.2.incoming
  18.9 0.1 merge.7
  19.0 0.1 collective-permute-start.3
  19.1 0.0 collective-permute-done.incoming
  19.1 0.1 merge.6
  19.2 2.1 %collective-permute-start.1 = (s16[4,4,16,128]{3,2,1,0:T(8,128)(2,1)S(1)}, s16[4,4,16,128]{3,2,1,0:T(8,128)(2,1)S(1)}, u32[]{:S(2)}, u32[]{:S(2)}) collective-permute-start(s16[4,4,16,128]{3,2,1,0:T(8,128)(2,1)S(1)} %get-tuple-element.43), channel_id=1, source_target_pairs={{0,8},{4,12},{8,0},{12,4},{16,24},{20,28},{24,16},{28,20},{1,9},{5... | collective-permute-start | bytes 196616 | tf_op jit(solution)/shard_map/ppermute | solution.py:379
  21.2 0.0 collective-permute-done.5.incoming
  21.2 0.1 merge.9
  21.3 0.1 collective-permute-start.6
  21.4 0.0 collective-permute-done.8.incoming
  21.4 0.1 merge.11
  21.5 2.3 %collective-permute-start.9 = (s16[4,4,16,128]{3,2,1,0:T(8,128)(2,1)S(1)}, s16[4,4,16,128]{3,2,1,0:T(8,128)(2,1)S(1)}, u32[]{:S(2)}, u32[]{:S(2)}) collective-permute-start(s16[4,4,16,128]{3,2,1,0:T(8,128)(2,1)S(1)} %merge.11), channel_id=1, source_target_pairs={{0,16},{4,20},{8,24},{12,28},{16,0},{20,4},{24,8},{28,12},{1,17},{... | collective-permute-start | bytes 196616 | tf_op jit(solution)/shard_map/ppermute | solution.py:379
  23.8 0.1 collective-permute-done.3.incoming
  23.9 0.1 merge.8
  24.0 1.9 %collective-permute-start.4 = (s16[4,4,16,128]{3,2,1,0:T(8,128)(2,1)S(1)}, s16[4,4,16,128]{3,2,1,0:T(8,128)(2,1)S(1)}, u32[]{:S(2)}, u32[]{:S(2)}) collective-permute-start(s16[4,4,16,128]{3,2,1,0:T(8,128)(2,1)S(1)} %merge.8), channel_id=1, source_target_pairs={{0,16},{4,20},{8,24},{12,28},{16,0},{20,4},{24,8},{28,12},{1,17},{... | collective-permute-start | bytes 196616 | tf_op jit(solution)/shard_map/ppermute | solution.py:379
  25.9 0.0 collective-permute-done.1.refs_1_
  25.9 0.0 collective-permute-done.6.refs_4_
  25.9 0.7 %collective-permute-done.9.refs_5_ = s16[4,4,16,128]{3,2,1,0:T(8,128)(2,1)S(1)} collective-permute-done((s16[4,4,16,128]{3,2,1,0:T(8,128)(2,1)S(1)}, s16[4,4,16,128]{3,2,1,0:T(8,128)(2,1)S(1)}, u32[]{:S(2)}, u32[]{:S(2)}) %collective-permute-start.9) | collective-permute-done | bytes 65568 | tf_op jit(solution)/shard_map/ppermute | solution.py:379
  26.6 1.7 %collective-permute-done.4.refs_2_ = s16[4,4,16,128]{3,2,1,0:T(8,128)(2,1)S(1)} collective-permute-done((s16[4,4,16,128]{3,2,1,0:T(8,128)(2,1)S(1)}, s16[4,4,16,128]{3,2,1,0:T(8,128)(2,1)S(1)}, u32[]{:S(2)}, u32[]{:S(2)}) %collective-permute-start.4) | collective-permute-done | bytes 65568 | tf_op jit(solution)/shard_map/ppermute | solution.py:379
  28.3 1.0 %finish.1 = f32[2,4,32,256]{3,2,1,0:T(8,128)} custom-call(f32[16,8,128]{2,1,0:T(8,128)S(1)} %get-tuple-element.31.splats, f32[4,4,16,128]{3,2,1,0:T(8,128)S(1)} %get-tuple-element.42.refs_0_, s16[4,4,16,128]{3,2,1,0:T(8,128)(2,1)S(1)} %collective-permute-done.1.refs_1_, s16[4,4,16,128]{3,2,1,0:T(8,128)(2,1)S(1)} %collective-permute-done.4.refs_2_, ...), custom_call_target="tpu_custom_call" | custom-call | flops 6144000 | bytes 262144 | tf_op jit(solution)/shard_map/finish/pallas_call | solution.py:259
Async XLA Ops:
  9.8 6.1 %collective-permute-start.7 = (f32[8,4,16,128]{3,2,1,0:T(8,128)S(1)}, f32[8,4,16,128]{3,2,1,0:T(8,128)S(1)}, u32[]{:S(2)}, u32[]{:S(2)}) collective-permute-start(f32[8,4,16,128]{3,2,1,0:T(8,128)S(1)} %get-tuple-element.54), channel_id=1, source_target_pairs={{0,4},{4,0},{8,12},{12,8},{16,20},{20,16},{24,28},{28,24},{1,5},{5... | collective-permute-start | bytes 786440 | tf_op jit(solution)/shard_map/ppermute | solution.py:379
  10.3 8.6 %collective-permute-start.2 = (f32[8,4,16,128]{3,2,1,0:T(8,128)S(1)}, f32[8,4,16,128]{3,2,1,0:T(8,128)S(1)}, u32[]{:S(2)}, u32[]{:S(2)}) collective-permute-start(f32[8,4,16,128]{3,2,1,0:T(8,128)S(1)} %get-tuple-element.45), channel_id=1, source_target_pairs={{0,4},{4,0},{8,12},{12,8},{16,20},{20,16},{24,28},{28,24},{1,5},{5... | collective-permute-start | bytes 786440 | tf_op jit(solution)/shard_map/ppermute | solution.py:379
  13.2 5.9 %collective-permute-start = (f32[8,4,16,128]{3,2,1,0:T(8,128)S(1)}, f32[8,4,16,128]{3,2,1,0:T(8,128)S(1)}, u32[]{:S(2)}, u32[]{:S(2)}) collective-permute-start(f32[8,4,16,128]{3,2,1,0:T(8,128)S(1)} %get-tuple-element.41), channel_id=1, source_target_pairs={{0,4},{4,0},{8,12},{12,8},{16,20},{20,16},{24,28},{28,24},{1,5},{5... | collective-permute-start | bytes 786440 | tf_op jit(solution)/shard_map/ppermute | solution.py:379
  15.7 5.5 %collective-permute-start.5 = (f32[8,4,16,128]{3,2,1,0:T(8,128)S(1)}, f32[8,4,16,128]{3,2,1,0:T(8,128)S(1)}, u32[]{:S(2)}, u32[]{:S(2)}) collective-permute-start(f32[8,4,16,128]{3,2,1,0:T(8,128)S(1)} %get-tuple-element.50), channel_id=1, source_target_pairs={{0,4},{4,0},{8,12},{12,8},{16,20},{20,16},{24,28},{28,24},{1,5},{5... | collective-permute-start | bytes 786440 | tf_op jit(solution)/shard_map/ppermute | solution.py:379
  15.9 5.5 %collective-permute-start.8 = (s16[4,4,16,128]{3,2,1,0:T(8,128)(2,1)S(1)}, s16[4,4,16,128]{3,2,1,0:T(8,128)(2,1)S(1)}, u32[]{:S(2)}, u32[]{:S(2)}) collective-permute-start(s16[4,4,16,128]{3,2,1,0:T(8,128)(2,1)S(1)} %get-tuple-element.56), channel_id=1, source_target_pairs={{0,8},{4,12},{8,0},{12,4},{16,24},{20,28},{24,16},{28,20},{1,9},{5... | collective-permute-start | bytes 196616 | tf_op jit(solution)/shard_map/ppermute | solution.py:379
  19.0 4.9 %collective-permute-start.3 = (s16[4,4,16,128]{3,2,1,0:T(8,128)(2,1)S(1)}, s16[4,4,16,128]{3,2,1,0:T(8,128)(2,1)S(1)}, u32[]{:S(2)}, u32[]{:S(2)}) collective-permute-start(s16[4,4,16,128]{3,2,1,0:T(8,128)(2,1)S(1)} %get-tuple-element.47), channel_id=1, source_target_pairs={{0,8},{4,12},{8,0},{12,4},{16,24},{20,28},{24,16},{28,20},{1,9},{5... | collective-permute-start | bytes 196616 | tf_op jit(solution)/shard_map/ppermute | solution.py:379
  19.2 6.7 %collective-permute-start.1 = (s16[4,4,16,128]{3,2,1,0:T(8,128)(2,1)S(1)}, s16[4,4,16,128]{3,2,1,0:T(8,128)(2,1)S(1)}, u32[]{:S(2)}, u32[]{:S(2)}) collective-permute-start(s16[4,4,16,128]{3,2,1,0:T(8,128)(2,1)S(1)} %get-tuple-element.43), channel_id=1, source_target_pairs={{0,8},{4,12},{8,0},{12,4},{16,24},{20,28},{24,16},{28,20},{1,9},{5... | collective-permute-start | bytes 196616 | tf_op jit(solution)/shard_map/ppermute | solution.py:379
  21.3 4.6 %collective-permute-start.6 = (s16[4,4,16,128]{3,2,1,0:T(8,128)(2,1)S(1)}, s16[4,4,16,128]{3,2,1,0:T(8,128)(2,1)S(1)}, u32[]{:S(2)}, u32[]{:S(2)}) collective-permute-start(s16[4,4,16,128]{3,2,1,0:T(8,128)(2,1)S(1)} %get-tuple-element.52), channel_id=1, source_target_pairs={{0,8},{4,12},{8,0},{12,4},{16,24},{20,28},{24,16},{28,20},{1,9},{5... | collective-permute-start | bytes 196616 | tf_op jit(solution)/shard_map/ppermute | solution.py:379
  21.5 5.1 %collective-permute-start.9 = (s16[4,4,16,128]{3,2,1,0:T(8,128)(2,1)S(1)}, s16[4,4,16,128]{3,2,1,0:T(8,128)(2,1)S(1)}, u32[]{:S(2)}, u32[]{:S(2)}) collective-permute-start(s16[4,4,16,128]{3,2,1,0:T(8,128)(2,1)S(1)} %merge.11), channel_id=1, source_target_pairs={{0,16},{4,20},{8,24},{12,28},{16,0},{20,4},{24,8},{28,12},{1,17},{... | collective-permute-start | bytes 196616 | tf_op jit(solution)/shard_map/ppermute | solution.py:379
  24.0 4.3 %collective-permute-start.4 = (s16[4,4,16,128]{3,2,1,0:T(8,128)(2,1)S(1)}, s16[4,4,16,128]{3,2,1,0:T(8,128)(2,1)S(1)}, u32[]{:S(2)}, u32[]{:S(2)}) collective-permute-start(s16[4,4,16,128]{3,2,1,0:T(8,128)(2,1)S(1)} %merge.8), channel_id=1, source_target_pairs={{0,16},{4,20},{8,24},{12,28},{16,0},{20,4},{24,8},{28,12},{1,17},{... | collective-permute-start | bytes 196616 | tf_op jit(solution)/shard_map/ppermute | solution.py:379

commit v3 on v2

v3 whole, which is shorter than its diff:
```python
import functools
import math

import jax
import jax.numpy as jnp
import numpy as np
from jax import lax
from jax.experimental import pallas as pl
from jax.experimental.pallas import tpu as pltpu
from jax.sharding import PartitionSpec as P


BC = 16
LANES = 128
SUB = 8
SHEAR = (0.45, -0.3)
LOG2E = 1.0 / math.log(2.0)

CODE_RANGE = 32.0
CODE_STEP = 2047.0
CODE_BIAS = 32768.0


def shear_taps(brick_edge, view):
    f32 = np.float32
    slice_index = np.arange(brick_edge, dtype=f32)[:, None]
    position = np.arange(brick_edge, dtype=f32)[None, :] + f32(SHEAR[view]) * (
        slice_index - f32((brick_edge - 1) / 2.0)
    )
    anchor = np.floor(position)
    fraction = (position - anchor).astype(f32)
    low = (f32(1.0) - fraction).astype(jnp.bfloat16).astype(f32)
    high = fraction.astype(jnp.bfloat16).astype(f32)
    return anchor.astype(np.int32), low, high


def shear_lines(brick_edge, view):
    anchor, low, high = shear_taps(brick_edge, view)
    source = np.arange(brick_edge)[None, :, None]
    table = np.where(source == anchor[:, None, :], low[:, None, :], 0.0)
    return table + np.where(source == anchor[:, None, :] + 1, high[:, None, :], 0.0)


def shear_tables(edge):
    along_cols = shear_lines(edge, 0)
    along_rows = shear_lines(edge, 1)
    block = np.stack([np.kron(np.eye(LANES // edge), t) for t in along_cols])
    full = np.stack([np.kron(t, np.eye(edge)) for t in along_rows])
    lane = np.arange(LANES)
    turned = (-(lane // edge) % (LANES // edge)) * edge + lane % edge
    block = block[:, :, turned]
    full = full.reshape(edge, edge * edge, -1, LANES)[..., turned].reshape(full.shape)
    return block.astype(jnp.bfloat16), full.astype(jnp.bfloat16)


def encode(x):
    logs = jnp.log(jnp.maximum(x, 2.0**-CODE_RANGE))
    code = logs * (CODE_STEP * LOG2E) + (CODE_RANGE * CODE_STEP + 0.5)
    return (code.astype(jnp.int32) - int(CODE_BIAS)).astype(jnp.int16)


def decode(code):
    value = code.astype(jnp.int32).astype(jnp.float32)
    return jnp.exp2(value * (1.0 / CODE_STEP) + (CODE_BIAS / CODE_STEP - CODE_RANGE))


EXT_SLOPE, EXT_SHIFT, SLOPES, SHIFTS, FLIPS, FRONTS = 0, 1, 2, 5, 8, 10


def bit_of(value, bit):
    return lax.bitwise_and(lax.shift_right_logical(value, bit), 1)


def spread_bit(slot, position, bit):
    high = lax.shift_left(lax.shift_right_logical(slot, position), position + 1)
    low = lax.bitwise_and(slot, (1 << position) - 1)
    return high + low + bit * (1 << position)


def shade(item, bit, low_bits, v, samples, levels, splats, out):
    edge, halves = samples.shape[1], samples.shape[2]
    slot, group = item // 2, lax.rem(item, 2)
    unit = spread_bit(slot, low_bits, bit)
    h = lax.rem(unit, halves)
    start = pl.multiple_of((unit // halves) * BC + group * SUB, SUB)
    level = levels[pl.ds(start, SUB), :]
    flip = splats[FLIPS + v]
    ext_slope, ext_shift = splats[EXT_SLOPE], splats[EXT_SHIFT]
    shift = []
    for j in range(4):
        need = j + flip * (3 - 2 * j)
        shift.append(jnp.where(level > need, ext_shift, -1e30))
    clear = jnp.ones((SUB, LANES), jnp.float32)
    sums = [jnp.zeros((SUB, LANES), jnp.float32) for _ in range(3)]
    for k in range(edge):
        s = samples[v, k, h, pl.ds(start, SUB), :]
        passed = jnp.exp2(-jnp.exp2(s * ext_slope + shift[k // (edge // 4)]))
        beyond = clear * passed
        weight = clear - beyond
        clear = beyond
        for c in range(3):
            sums[c] = sums[c] + weight * jnp.tanh(s * splats[SLOPES + c] + splats[SHIFTS + c])
    opacity = 1.0 - clear
    place = pl.multiple_of(group * SUB, SUB)
    for c in range(3):
        out[slot, v, c, pl.ds(place, SUB), :] = (opacity + sums[c]) * 0.5
    out[slot, v, 3, pl.ds(place, SUB), :] = opacity


def to_slices(lines, r, perm, moved):
    edge = moved.shape[0]
    x = lines[r].reshape(BC * edge, lines.shape[-1])
    slices = jnp.dot(perm[...], x, preferred_element_type=jnp.float32).astype(jnp.bfloat16)
    for k in range(edge):
        place = r * BC if isinstance(r, int) else pl.multiple_of(r * BC, BC)
        moved[k, pl.ds(place, BC), :] = slices[k * BC : (k + 1) * BC, :]


def flips_of(splats):
    return [splats[FLIPS + v, 0, 0] > 0.5 for v in range(2)]


def resample(k, v, flips, moved, table, samples):
    edge, halves = samples.shape[1], samples.shape[2]
    result = jnp.dot(moved[k], table[k], preferred_element_type=jnp.float32)
    place = jnp.where(flips[v], edge - 1 - k, k)
    for h in range(halves):
        samples[v, place, h] = result[:, h * LANES : (h + 1) * LANES]


def beside(steps, items, jobs, item_fn, job_fn):
    def body(i, carry):
        for n in range(jobs // steps):
            job_fn(i * (jobs // steps) + n)
        for n in range(items // steps):
            item_fn(i * (items // steps) + n)
        return carry

    lax.fori_loop(0, steps, body, 0)


def first_kernel(
    rounds, low_bits,
    order, cgain, cbias, egain, ebias, cost, bricks, table0, table1,
    send, samples, moved_next, lines1, lines2, lines3, tab0, tab1, perm, levels, splats,
    lines0, moved, s_order, s_cgain, s_cbias, v_cost, sems,
):
    me = lax.axis_index("depth")
    rows, edge = lines0.shape[0], moved.shape[0]
    halves = samples.shape[2]
    chunk = rows * BC
    top, second = bit_of(me, rounds - 1), bit_of(me, rounds - 2)
    quarters = [
        (1 - top) * 2 + 1 - second, (1 - top) * 2 + second, top * 2 + 1 - second, top * 2 + second
    ]
    small = [(order, s_order), (cgain, s_cgain), (cbias, s_cbias), (cost, v_cost)]
    pairs = list(small)
    pairs.append((bricks.at[pl.ds(quarters[0] * rows, rows)], lines0))
    for h in range(halves):
        span = pl.ds(h * LANES, LANES)
        pairs.append((table0, tab0.at[:, span, span]))
    pairs.append((table1, tab1))
    for quarter, lines in zip(quarters[1:], (lines1, lines2, lines3)):
        pairs.append((bricks.at[pl.ds(quarter * rows, rows)], lines))
    copies = [pltpu.make_async_copy(a, b, sems.at[i]) for i, (a, b) in enumerate(pairs)]
    for copy in copies:
        copy.start()

    size = BC * edge
    out_row = lax.broadcasted_iota(jnp.int32, (size, size), 0)
    in_row = lax.broadcasted_iota(jnp.int32, (size, size), 1)
    wanted = lax.rem(out_row, BC) * edge + out_row // BC
    perm[...] = jnp.where(wanted == in_row, 1.0, 0.0).astype(jnp.bfloat16)
    zero = jnp.zeros((LANES, LANES), jnp.bfloat16)
    for k in range(edge):
        for a in range(halves):
            for b in range(halves):
                if a != b:
                    tab0[k, a * LANES : (a + 1) * LANES, b * LANES : (b + 1) * LANES] = zero

    for copy in copies[: len(small)]:
        copy.wait()

    def splat(value):
        return jnp.full((SUB, LANES), value, jnp.float32)

    splats[EXT_SLOPE] = splat(egain[0] * LOG2E)
    splats[EXT_SHIFT] = splat(ebias[0] * LOG2E + math.log2(LOG2E))
    for c in range(3):
        splats[SLOPES + c] = splat(s_cgain[c] * 0.5)
        splats[SHIFTS + c] = splat(s_cbias[c] * 0.5)
    flips = []
    for v in range(2):
        flips.append(s_order[v, 0] > s_order[v, order.shape[1] - 1])
        splats[FLIPS + v] = splat(jnp.where(flips[v], 1.0, 0.0))
        rank = lax.bitwise_xor(me, s_order[v, 0])
        for bit in range(rounds):
            splats[FRONTS + v * rounds + bit] = splat(bit_of(rank, bit).astype(jnp.float32))

    total = v_cost.shape[1]
    here = lax.broadcasted_iota(jnp.int32, (chunk, total), 0)
    there = lax.broadcasted_iota(jnp.int32, (chunk, total), 1)
    row = v_cost[...].astype(jnp.float32)
    ones = jnp.ones((total, LANES), jnp.bfloat16)
    for i, quarter in enumerate(quarters):
        picked = jnp.where(here + quarter * chunk == there, row, 0.0).astype(jnp.bfloat16)
        levels[i] = jnp.dot(picked, ones, preferred_element_type=jnp.float32)

    copies[len(small)].wait()
    for r in range(rows):
        to_slices(lines0, r, perm, moved)
    for h in range(halves):
        copies[len(small) + 1 + h].wait()
    for k in range(edge):
        resample(k, 0, flips, moved, tab0, samples)
    for copy in copies[len(small) + 1 + halves :]:
        copy.wait()

    mine = bit_of(me, 0)

    def item(v):
        return lambda i: shade(i, 1 - mine, low_bits, v, samples, levels.at[0], splats, send)

    count = chunk // SUB * halves // 2
    beside(2, count, edge, item(0), lambda k: resample(k, 1, flips, moved, tab1, samples))
    beside(2, count, rows, item(1), lambda r: to_slices(lines1, r, perm, moved_next))


def second_kernel(low_bits, samples, moved_next, tab0, tab1, levels, splats, kept, samples_next):
    mine = bit_of(lax.axis_index("depth"), 0)
    edge = samples.shape[1]
    count = samples.shape[3] // SUB * samples.shape[2] // 2
    flips = flips_of(splats)
    for v, table in enumerate((tab0, tab1)):
        beside(
            2, count, edge,
            lambda i: shade(i, mine, low_bits, v, samples, levels.at[0], splats, kept),
            lambda k: resample(k, v, flips, moved_next, table, samples_next),
        )


def quarter_kernel(low_bits, index, last, *refs):
    if last:
        samples, levels, splats, send, kept = refs
    else:
        samples, lines, tab0, tab1, perm, levels, splats, send, kept, samples_next, moved = refs
    mine = bit_of(lax.axis_index("depth"), 0)
    edge = samples.shape[1]
    count = samples.shape[3] // SUB * samples.shape[2] // 2
    flips = flips_of(splats)

    def items(v):
        def both(i):
            shade(i, 1 - mine, low_bits, v, samples, levels.at[index], splats, send)
            shade(i, mine, low_bits, v, samples, levels.at[index], splats, kept)

        return both

    def jobs(k):
        resample(k, 0, flips, moved, tab0, samples_next)
        resample(k, 1, flips, moved, tab1, samples_next)

    if last:
        beside(4, count, 0, items(0), None)
        beside(4, count, 0, items(1), None)
    else:
        rows = lines.shape[0]
        beside(4, count, rows, items(0), lambda r: to_slices(lines, r, perm, moved))
        beside(4, count, edge, items(1), jobs)


VMEM = pl.BlockSpec(memory_space=pltpu.VMEM)
HBM = pl.BlockSpec(memory_space=pltpu.HBM)


def call(kernel, ins, outs, cycles, scratch=(), limit=4 << 20, specs=None):
    outs = tuple(jax.ShapeDtypeStruct(shape, dtype) for shape, dtype in outs)
    return pl.pallas_call(
        kernel,
        out_shape=outs,
        in_specs=specs or [VMEM] * len(ins),
        out_specs=tuple(VMEM for _ in outs),
        scratch_shapes=list(scratch),
        compiler_params=pltpu.CompilerParams(vmem_limit_bytes=limit),
        cost_estimate=pl.CostEstimate(flops=cycles * 4096, bytes_accessed=1 << 18, transcendentals=0),
    )(*ins)


def render(rounds, low_bits, order, cgain, cbias, egain, ebias, cost, bricks, table0, table1):
    total, edge, plane = bricks.shape
    rows = total // BC // 4
    chunk, halves, size = rows * BC, plane // LANES, BC * edge
    f32, bf16 = jnp.float32, jnp.bfloat16
    part = ((rows * halves // 2, 2, 4, BC, LANES), f32)
    samples = ((2, edge, halves, chunk, LANES), f32)
    lines = ((rows, BC, edge, plane), bf16)
    moved = ((edge, chunk, plane), bf16)
    table = ((edge, plane, plane), bf16)
    square = ((size, size), bf16)
    levels = ((4, chunk, LANES), f32)
    splats = ((FRONTS + 2 * rounds, SUB, LANES), f32)
    bricks = bricks.reshape(total // BC, BC, edge, plane)
    far = lambda x: pltpu.with_memory_space_constraint(x, pltpu.HBM)
    ins = (far(order), far(cgain), far(cbias), egain, ebias, far(cost), far(bricks), far(table0), far(table1))
    specs = [HBM] * 3 + [pl.BlockSpec(memory_space=pltpu.SMEM)] * 2 + [HBM] * 4
    send0, samples0, moved1, _, lines2, lines3, tab0, tab1, perm, levels_, splats_ = call(
        functools.partial(first_kernel, rounds, low_bits), ins,
        (part, samples, moved, lines, lines, lines, table, table, square, levels, splats), 4000,
        [pltpu.VMEM(*lines), pltpu.VMEM(*moved),
         pltpu.SMEM(order.shape, order.dtype), pltpu.SMEM(cgain.shape, f32), pltpu.SMEM(cbias.shape, f32),
         pltpu.VMEM(cost.shape, cost.dtype), pltpu.SemaphoreType.DMA((9 + halves,))],
        20 << 20, specs,
    )
    kept0, samples1 = call(
        functools.partial(second_kernel, low_bits),
        (samples0, moved1, tab0, tab1, levels_, splats_), (part, samples), 1800, (), 14 << 20,
    )
    send1, kept1, samples2, _ = call(
        functools.partial(quarter_kernel, low_bits, 1, False),
        (samples1, lines2, tab0, tab1, perm, levels_, splats_), (part, part, samples, moved), 3500, (), 14 << 20,
    )
    send2, kept2, samples3, _ = call(
        functools.partial(quarter_kernel, low_bits, 2, False),
        (samples2, lines3, tab0, tab1, perm, levels_, splats_), (part, part, samples, moved), 3500, (), 14 << 20,
    )
    send3, kept3 = call(
        functools.partial(quarter_kernel, low_bits, 3, True),
        (samples3, levels_, splats_), (part, part), 3300, (), 8 << 20,
    )
    return splats_, [(send0, kept0), (send1, kept1), (send2, kept2), (send3, kept3)]


def merged_pair(front, kept, incoming):
    behind = 1.0 - front * incoming[3]
    ahead = 1.0 - (1.0 - front) * kept[3]
    return [kept[c] * behind + incoming[c] * ahead for c in range(4)]


def front_of(splats, v, rounds, bit):
    one = splats[FRONTS + v * rounds + bit]
    return jnp.concatenate([one] * (BC // SUB), axis=0)


def read(ref, unit, v):
    parts = [ref[unit, v, c] for c in range(4)]
    return [decode(x) for x in parts] if ref.dtype == jnp.int16 else parts


def merge_kernel(rounds, bit, many, low_bits, splats, kept, *refs):
    incoming, outs = refs[:many], refs[many:]
    mine = bit_of(lax.axis_index("depth"), bit + many)
    units = kept.shape[0]
    for v in range(2):
        for i, out in enumerate(outs):
            for slot in range(units // len(outs)):
                unit = slot
                if len(outs) > 1:
                    unit = spread_bit(slot, low_bits, 1 - mine if i == 0 else mine)
                done = read(kept, unit, v)
                for n, came in enumerate(incoming):
                    done = merged_pair(front_of(splats, v, rounds, bit + n), done, read(came, unit, v))
                for c in range(4):
                    out[slot, v, c] = encode(done[c]) if out.dtype == jnp.int16 else done[c]


def merge(rounds, bit, low_bits, types, splats, kept, incoming):
    units, tail = kept.shape[0], kept.shape[1:]
    outs = tuple(((units // len(types), *tail), t) for t in types)
    kernel = functools.partial(merge_kernel, rounds, bit, len(incoming), low_bits)
    return call(kernel, (splats, kept, *incoming), outs, 300)


def finish_kernel(rounds, bit, edge, splats, kept, *refs):
    incoming, out = refs[:-1], refs[-1]
    chunks = LANES // edge
    chunk_of = lax.broadcasted_iota(jnp.int32, (SUB, LANES), 1) // edge
    for v in range(2):
        for unit in range(kept.shape[0]):
            done = read(kept, unit, v)
            for n, came in enumerate(incoming):
                done = merged_pair(front_of(splats, v, rounds, bit + n), done, read(came, unit, v))
            for c in range(4):
                for g in range(BC // SUB):
                    x = done[c][g * SUB : (g + 1) * SUB, :]
                    x = pltpu.roll(x, 0, 1, stride=edge, stride_axis=0)
                    for step in range(3):
                        turned = pltpu.roll(x, SUB - (1 << step), 0)
                        x = jnp.where(bit_of(chunk_of, step) == 1, turned, x)
                    x = pltpu.roll(x, 0, 1, stride=edge, stride_axis=0)
                    out[v, c, unit * chunks : (unit + 1) * chunks, g * LANES : (g + 1) * LANES] = x


def finish(rounds, bit, edge, splats, kept, incoming):
    units = kept.shape[0]
    out = ((2, 4, units * LANES // edge, BC * edge), jnp.float32)
    return call(functools.partial(finish_kernel, rounds, bit, edge), (splats, kept, *incoming), (out,), 1500)[0]


def swapped(x, bit):
    count = lax.axis_size("depth")
    return lax.ppermute(x, "depth", [(i, i ^ 1 << bit) for i in range(count)])


def shards(bricks, cost, order, color_gain, color_bias, ext_gain, ext_bias):
    bricks = bricks[0]
    total, edge, plane = bricks.shape
    count = lax.axis_size("depth")
    rounds = count.bit_length() - 1
    units = total // BC * (plane // LANES)
    low_bits = (units // count).bit_length() - 1
    table0, table1 = (jnp.asarray(t) for t in shear_tables(edge))
    splats, parts = render(
        rounds, low_bits, order, color_gain, color_bias, ext_gain, ext_bias, cost, bricks, table0, table1
    )
    f32, i16 = jnp.float32, jnp.int16
    near = rounds - 2

    def close(index):
        send, kept = parts[index]
        for bit in range(near - 1):
            incoming = swapped(send, bit)
            send, kept = merge(rounds, bit, low_bits, (f32, f32), splats, kept, [incoming])
        return kept, swapped(send, near - 1)

    def leave(index):
        kept, incoming = close(index)
        (done,) = merge(rounds, near - 1, low_bits, (i16,), splats, kept, [incoming])
        return swapped(done, near)

    across = leave(0)
    kept, incoming = close(1)
    (done,) = merge(rounds, near - 1, low_bits, (i16,), splats, kept, [incoming, across])
    top = swapped(done, near + 1)
    across = leave(2)
    kept, incoming = close(3)
    return finish(rounds, near - 1, edge, splats, kept, [incoming, across, top])


def solution(mesh):
    in_specs = (P("depth", "image", None, None), P("depth", "image"), P(), P(), P(), P(), P())
    out_specs = P(None, None, "depth", "image")

    return jax.shard_map(shards, mesh=mesh, in_specs=in_specs, out_specs=out_specs, check_vma=False)
```

time: 29.5 us -> 28.6 us (0.969)
  starting transfers between devices: 10.7 us -> 6.13 us
  waiting for transfers between devices: 2.47 us -> 5.18 us
  Pallas kernels: 14.8 us -> 15.8 us
    ppermute x10 -> x7, starting transfers between devices: 10.7 us -> 6.13 us  [swapped(): return lax.ppermute(x, 'depth', [(i, i ^ 1 << bit) for i in range(count)])]
    ppermute x10 -> x7, waiting for transfers between devices: 2.47 us -> 5.18 us  [swapped(): return lax.ppermute(x, 'depth', [(i, i ^ 1 << bit) for i in range(count)])]
    pallas_call x11 -> x9, Pallas kernels: 14.8 us -> 15.8 us  [call(): pl.pallas_call(kernel, out_shape=outs, in_specs=specs or [VMEM] * len(ins...]
  transfers between devices with their start and end apart: 10 -> 7, of which waited for: 3 -> 3; matrix products, arithmetic and copies ran while one was open for 0% -> 0% of each run, Pallas kernels for 18% -> 34%
where the time goes in v3:
time: 28.6 us; the launch traced here: 28.4 us
  Pallas kernels  15.8 us (55%)
  starting transfers between devices  6.13 us (21%)
  waiting for transfers between devices  5.18 us (18%)
  between operations  1.34 us (5%)
    pallas_call x9, Pallas kernels, call(): pl.pallas_call(kernel, out_shape=outs, in_specs=specs or [VMEM] * len(ins...  15.8 us
    ppermute x7, starting transfers between devices, swapped(): return lax.ppermute(x, 'depth', [(i, i ^ 1 << bit) for i in range(count)])  6.13 us
    ppermute x7, waiting for transfers between devices, swapped(): return lax.ppermute(x, 'depth', [(i, i ^ 1 << bit) for i in range(count)])  5.18 us
  transfers between devices with their start and end apart: 7, of which 3 were waited for; matrix products, arithmetic and copies ran while one was open for 0% of the time, Pallas kernels for 34%

profile of v3, /device:TPU:0, one launch (start us, length us, event | category | flops | bytes accessed | tf_op | source)
XLA Modules:
  0.0 28.4 jit_solution(11813171173366754758)
XLA Ops:
  1.3 5.1 %shard_map.91 = (f32[4,2,4,16,128]{4,3,2,1,0:T(8,128)S(1)}, f32[2,16,2,64,128]{4,3,2,1,0:T(8,128)S(1)}, bf16[16,64,256]{2,1,0:T(8,128)(2,1)S(1)}, bf16[4,16,16,2...) custom-call(s32[2,8]{1,0:T(2,128)} %order.1, ...), custom_call_target="tpu_custom_call" | custom-call | flops 16384000 | bytes 262144 | tf_op jit(solution)/shard_map/pallas_call | solution.py:278
  6.4 0.6 %collective-permute-start.4 = (f32[4,2,4,16,128]{4,3,2,1,0:T(8,128)S(1)}, f32[4,2,4,16,128]{4,3,2,1,0:T(8,128)S(1)}, u32[]{:S(2)}, u32[]{:S(2)}) collective-permute-start(f32[4,2,4,16,128]{4,3,2,1,0:T(8,128)S(1)} %get-tuple-element.44), channel_id=1, source_target_pairs={{0,4},{4,0},{8,12},{12,8},{16,20},{20,16},{24,28},{28,24},{1,5},{5... | collective-permute-start | bytes 786440 | tf_op jit(solution)/shard_map/ppermute | solution.py:401
  6.9 1.2 %shard_map.92 = (f32[4,2,4,16,128]{4,3,2,1,0:T(8,128)S(1)}, f32[2,16,2,64,128]{4,3,2,1,0:T(8,128)S(1)}) custom-call(f32[2,16,2,64,128]{4,3,2,1,0:T(8,128)S(1)} %get-tuple-element.26.samples, bf16[16,64,256]{2,1,0:T(8,128)(2,1)S(1)} %get-tuple-element.27.moved_next, bf16[16,256,256]{2,1,0:T(8,128)(2,1)S(1)} %get-tuple-element.28.tab0.refs_2_, ...), custom_call_target="tpu_custom_call" | custom-call | flops 7372800 | bytes 262144 | tf_op jit(solution)/shard_map/pallas_call | solution.py:278
  8.2 3.1 %shard_map.93 = (f32[4,2,4,16,128]{4,3,2,1,0:T(8,128)S(1)}, f32[4,2,4,16,128]{4,3,2,1,0:T(8,128)S(1)}, f32[2,16,2,64,128]{4,3,2,1,0:T(8,128)S(1)}, bf16[16,64,256]{2,1,0:T(8,128)(2,1)}) custom-call(f32[2,16,2,64,128]{4,3,2,1,0:T(8,128)S(1)} %get-tuple-element.31.refs_0_, bf16[4,16,16,256]{3,2,1,0:T(8,128)(2,1)S(1)} %get-tuple-element.32.refs_1_, ...), custom_call_target="tpu_custom_call" | custom-call | flops 14336000 | bytes 262144 | tf_op jit(solution)/shard_map/pallas_call | solution.py:278
  11.3 3.1 %shard_map.94 = (f32[4,2,4,16,128]{4,3,2,1,0:T(8,128)S(1)}, f32[4,2,4,16,128]{4,3,2,1,0:T(8,128)S(1)}, f32[2,16,2,64,128]{4,3,2,1,0:T(8,128)S(1)}, bf16[16,64,256]{2,1,0:T(8,128)(2,1)}) custom-call(f32[2,16,2,64,128]{4,3,2,1,0:T(8,128)S(1)} %get-tuple-element.34.refs_0_, bf16[4,16,16,256]{3,2,1,0:T(8,128)(2,1)S(1)} %get-tuple-element.35.refs_1_, ...), custom_call_target="tpu_custom_call" | custom-call | flops 14336000 | bytes 262144 | tf_op jit(solution)/shard_map/pallas_call | solution.py:278
  14.4 0.0 collective-permute-start.1
  14.4 0.5 %collective-permute-start.3 = (f32[4,2,4,16,128]{4,3,2,1,0:T(8,128)S(1)}, f32[4,2,4,16,128]{4,3,2,1,0:T(8,128)S(1)}, u32[]{:S(2)}, u32[]{:S(2)}) collective-permute-start(f32[4,2,4,16,128]{4,3,2,1,0:T(8,128)S(1)} %get-tuple-element.42), channel_id=1, source_target_pairs={{0,4},{4,0},{8,12},{12,8},{16,20},{20,16},{24,28},{28,24},{1,5},{5... | collective-permute-start | bytes 786440 | tf_op jit(solution)/shard_map/ppermute | solution.py:401
  14.9 0.0 collective-permute-done.4.refs_0_
  14.9 0.1 shard_map.97
  15.1 2.6 %collective-permute-start.5 = (s16[4,2,4,16,128]{4,3,2,1,0:T(8,128)(2,1)S(1)}, s16[4,2,4,16,128]{4,3,2,1,0:T(8,128)(2,1)S(1)}, u32[]{:S(2)}, u32[]{:S(2)}) collective-permute-start(s16[4,2,4,16,128]{4,3,2,1,0:T(8,128)(2,1)S(1)} %shard_map.97), channel_id=1, source_target_pairs={{0,8},{4,12},{8,0},{12,4},{16,24},{20,28},{24,16},{28,20},{1,9},{5... | collective-permute-start | bytes 393224 | tf_op jit(solution)/shard_map/ppermute | solution.py:401
  17.6 1.7 %shard_map.95 = (f32[4,2,4,16,128]{4,3,2,1,0:T(8,128)S(1)}, f32[4,2,4,16,128]{4,3,2,1,0:T(8,128)S(1)}) custom-call(f32[2,16,2,64,128]{4,3,2,1,0:T(8,128)S(1)} %get-tuple-element.36.refs_0_, f32[4,64,128]{2,1,0:T(8,128)S(1)} %get-tuple-element.30.levels.refs_5_.refs_1_, f32[16,8,128]{2,1,0:T(8,128)S(1)} %get-tuple-element.25.splats.refs_6_.refs_2_), custom_call_target="tpu_custom_call" | custom-call | flops 13516800 | bytes 262144 | tf_op jit(solution)/shard_map/pallas_call | solution.py:278
  19.4 0.3 collective-permute-start
  19.6 0.0 collective-permute-done.1.refs_0_
  19.6 0.1 shard_map.96
  19.8 0.4 %collective-permute-start.2 = (s16[4,2,4,16,128]{4,3,2,1,0:T(8,128)(2,1)S(1)}, s16[4,2,4,16,128]{4,3,2,1,0:T(8,128)(2,1)S(1)}, u32[]{:S(2)}, u32[]{:S(2)}) collective-permute-start(s16[4,2,4,16,128]{4,3,2,1,0:T(8,128)(2,1)S(1)} %shard_map.96), channel_id=1, source_target_pairs={{0,8},{4,12},{8,0},{12,4},{16,24},{20,28},{24,16},{28,20},{1,9},{5... | collective-permute-start | bytes 393224 | tf_op jit(solution)/shard_map/ppermute | solution.py:401
  20.1 0.0 collective-permute-done.3.refs_0_
  20.2 1.6 %collective-permute-done.5.refs_1_ = s16[4,2,4,16,128]{4,3,2,1,0:T(8,128)(2,1)S(1)} collective-permute-done((s16[4,2,4,16,128]{4,3,2,1,0:T(8,128)(2,1)S(1)}, s16[4,2,4,16,128]{4,3,2,1,0:T(8,128)(2,1)S(1)}, u32[]{:S(2)}, u32[]{:S(2)}) %collective-permute-start.5) | collective-permute-done | bytes 131104 | tf_op jit(solution)/shard_map/ppermute | solution.py:401
  21.8 0.2 shard_map.98
  22.0 1.8 %collective-permute-start.6 = (s16[4,2,4,16,128]{4,3,2,1,0:T(8,128)(2,1)S(1)}, s16[4,2,4,16,128]{4,3,2,1,0:T(8,128)(2,1)S(1)}, u32[]{:S(2)}, u32[]{:S(2)}) collective-permute-start(s16[4,2,4,16,128]{4,3,2,1,0:T(8,128)(2,1)S(1)} %shard_map.98), channel_id=1, source_target_pairs={{0,16},{4,20},{8,24},{12,28},{16,0},{20,4},{24,8},{28,12},{1,17},{... | collective-permute-start | bytes 393224 | tf_op jit(solution)/shard_map/ppermute | solution.py:401
  23.8 0.0 collective-permute-done.refs_0_
  23.8 1.7 %collective-permute-done.2.refs_1_ = s16[4,2,4,16,128]{4,3,2,1,0:T(8,128)(2,1)S(1)} collective-permute-done((s16[4,2,4,16,128]{4,3,2,1,0:T(8,128)(2,1)S(1)}, s16[4,2,4,16,128]{4,3,2,1,0:T(8,128)(2,1)S(1)}, u32[]{:S(2)}, u32[]{:S(2)}) %collective-permute-start.2) | collective-permute-done | bytes 131104 | tf_op jit(solution)/shard_map/ppermute | solution.py:401
  25.5 1.8 %collective-permute-done.6.refs_2_ = s16[4,2,4,16,128]{4,3,2,1,0:T(8,128)(2,1)S(1)} collective-permute-done((s16[4,2,4,16,128]{4,3,2,1,0:T(8,128)(2,1)S(1)}, s16[4,2,4,16,128]{4,3,2,1,0:T(8,128)(2,1)S(1)}, u32[]{:S(2)}, u32[]{:S(2)}) %collective-permute-start.6) | collective-permute-done | bytes 131104 | tf_op jit(solution)/shard_map/ppermute | solution.py:401
  27.4 1.1 %shard_map.99 = f32[2,4,32,256]{3,2,1,0:T(8,128)} custom-call(f32[16,8,128]{2,1,0:T(8,128)S(1)} %get-tuple-element.25.splats.refs_6_.refs_2_, f32[4,2,4,16,128]{4,3,2,1,0:T(8,128)S(1)} %get-tuple-element.37.kept, f32[4,2,4,16,128]{4,3,2,1,0:T(8,128)S(1)} %collective-permute-done.refs_0_, s16[4,2,4,16,128]{4,3,2,1,0:T(8,128)(2,1)S(1)} %collective-permute-done.2.refs_1_, ...), custom_call_target="tpu_custom_call" | custom-call | flops 6144000 | bytes 262144 | tf_op jit(solution)/shard_map/pallas_call | solution.py:278
Async XLA Ops:
  6.4 8.6 %collective-permute-start.4 = (f32[4,2,4,16,128]{4,3,2,1,0:T(8,128)S(1)}, f32[4,2,4,16,128]{4,3,2,1,0:T(8,128)S(1)}, u32[]{:S(2)}, u32[]{:S(2)}) collective-permute-start(f32[4,2,4,16,128]{4,3,2,1,0:T(8,128)S(1)} %get-tuple-element.44), channel_id=1, source_target_pairs={{0,4},{4,0},{8,12},{12,8},{16,20},{20,16},{24,28},{28,24},{1,5},{5... | collective-permute-start | bytes 786440 | tf_op jit(solution)/shard_map/ppermute | solution.py:401
  14.4 5.2 %collective-permute-start.1 = (f32[4,2,4,16,128]{4,3,2,1,0:T(8,128)S(1)}, f32[4,2,4,16,128]{4,3,2,1,0:T(8,128)S(1)}, u32[]{:S(2)}, u32[]{:S(2)}) collective-permute-start(f32[4,2,4,16,128]{4,3,2,1,0:T(8,128)S(1)} %get-tuple-element.40), channel_id=1, source_target_pairs={{0,4},{4,0},{8,12},{12,8},{16,20},{20,16},{24,28},{28,24},{1,5},{5... | collective-permute-start | bytes 786440 | tf_op jit(solution)/shard_map/ppermute | solution.py:401
  14.4 5.7 %collective-permute-start.3 = (f32[4,2,4,16,128]{4,3,2,1,0:T(8,128)S(1)}, f32[4,2,4,16,128]{4,3,2,1,0:T(8,128)S(1)}, u32[]{:S(2)}, u32[]{:S(2)}) collective-permute-start(f32[4,2,4,16,128]{4,3,2,1,0:T(8,128)S(1)} %get-tuple-element.42), channel_id=1, source_target_pairs={{0,4},{4,0},{8,12},{12,8},{16,20},{20,16},{24,28},{28,24},{1,5},{5... | collective-permute-start | bytes 786440 | tf_op jit(solution)/shard_map/ppermute | solution.py:401
  15.1 6.7 %collective-permute-start.5 = (s16[4,2,4,16,128]{4,3,2,1,0:T(8,128)(2,1)S(1)}, s16[4,2,4,16,128]{4,3,2,1,0:T(8,128)(2,1)S(1)}, u32[]{:S(2)}, u32[]{:S(2)}) collective-permute-start(s16[4,2,4,16,128]{4,3,2,1,0:T(8,128)(2,1)S(1)} %shard_map.97), channel_id=1, source_target_pairs={{0,8},{4,12},{8,0},{12,4},{16,24},{20,28},{24,16},{28,20},{1,9},{5... | collective-permute-start | bytes 393224 | tf_op jit(solution)/shard_map/ppermute | solution.py:401
  19.4 4.5 %collective-permute-start = (f32[4,2,4,16,128]{4,3,2,1,0:T(8,128)S(1)}, f32[4,2,4,16,128]{4,3,2,1,0:T(8,128)S(1)}, u32[]{:S(2)}, u32[]{:S(2)}) collective-permute-start(f32[4,2,4,16,128]{4,3,2,1,0:T(8,128)S(1)} %get-tuple-element.38), channel_id=1, source_target_pairs={{0,4},{4,0},{8,12},{12,8},{16,20},{20,16},{24,28},{28,24},{1,5},{5... | collective-permute-start | bytes 786440 | tf_op jit(solution)/shard_map/ppermute | solution.py:401
  19.8 5.8 %collective-permute-start.2 = (s16[4,2,4,16,128]{4,3,2,1,0:T(8,128)(2,1)S(1)}, s16[4,2,4,16,128]{4,3,2,1,0:T(8,128)(2,1)S(1)}, u32[]{:S(2)}, u32[]{:S(2)}) collective-permute-start(s16[4,2,4,16,128]{4,3,2,1,0:T(8,128)(2,1)S(1)} %shard_map.96), channel_id=1, source_target_pairs={{0,8},{4,12},{8,0},{12,4},{16,24},{20,28},{24,16},{28,20},{1,9},{5... | collective-permute-start | bytes 393224 | tf_op jit(solution)/shard_map/ppermute | solution.py:401
  22.0 5.4 %collective-permute-start.6 = (s16[4,2,4,16,128]{4,3,2,1,0:T(8,128)(2,1)S(1)}, s16[4,2,4,16,128]{4,3,2,1,0:T(8,128)(2,1)S(1)}, u32[]{:S(2)}, u32[]{:S(2)}) collective-permute-start(s16[4,2,4,16,128]{4,3,2,1,0:T(8,128)(2,1)S(1)} %shard_map.98), channel_id=1, source_target_pairs={{0,16},{4,20},{8,24},{12,28},{16,0},{20,4},{24,8},{28,12},{1,17},{... | collective-permute-start | bytes 393224 | tf_op jit(solution)/shard_map/ppermute | solution.py:401

commit v4 on v3

--- a/solution.py
+++ b/solution.py
@@ -41,16 +41,13 @@
     return table + np.where(source == anchor[:, None, :] + 1, high[:, None, :], 0.0)
 
 
-def shear_tables(edge):
-    along_cols = shear_lines(edge, 0)
-    along_rows = shear_lines(edge, 1)
-    block = np.stack([np.kron(np.eye(LANES // edge), t) for t in along_cols])
-    full = np.stack([np.kron(t, np.eye(edge)) for t in along_rows])
+def shear_weights(edge):
     lane = np.arange(LANES)
     turned = (-(lane // edge) % (LANES // edge)) * edge + lane % edge
-    block = block[:, :, turned]
-    full = full.reshape(edge, edge * edge, -1, LANES)[..., turned].reshape(full.shape)
-    return block.astype(jnp.bfloat16), full.astype(jnp.bfloat16)
+    cols = np.tile(shear_lines(edge, 0), (1, 1, LANES // edge))
+    rows = np.repeat(shear_lines(edge, 1), edge, axis=2)
+    rows = rows.reshape(edge, edge, -1, LANES)[..., turned].transpose(0, 2, 1, 3)
+    return cols.astype(np.float32), rows.astype(np.float32)
 
 
 def encode(x):
@@ -107,13 +104,18 @@
     out[slot, v, 3, pl.ds(place, SUB), :] = opacity
 
 
+def wide(ref, *index):
+    return jnp.concatenate([ref[(*index, h)] for h in range(ref.shape[len(index)])], axis=-1)
+
+
 def to_slices(lines, r, perm, moved):
-    edge = moved.shape[0]
-    x = lines[r].reshape(BC * edge, lines.shape[-1])
-    slices = jnp.dot(perm[...], x, preferred_element_type=jnp.float32).astype(jnp.bfloat16)
+    edge, halves = moved.shape[0], moved.shape[1]
+    x = jnp.concatenate([lines[r, h].reshape(BC * edge, LANES) for h in range(halves)], axis=-1)
+    slices = jnp.dot(wide(perm), x, preferred_element_type=jnp.float32).astype(jnp.bfloat16)
+    place = r * BC if isinstance(r, int) else pl.multiple_of(r * BC, BC)
     for k in range(edge):
-        place = r * BC if isinstance(r, int) else pl.multiple_of(r * BC, BC)
-        moved[k, pl.ds(place, BC), :] = slices[k * BC : (k + 1) * BC, :]
+        for h in range(halves):
+            moved[k, h, pl.ds(place, BC), :] = slices[k * BC : (k + 1) * BC, h * LANES : (h + 1) * LANES]
 
 
 def flips_of(splats):
@@ -122,7 +124,7 @@
 
 def resample(k, v, flips, moved, table, samples):
     edge, halves = samples.shape[1], samples.shape[2]
-    result = jnp.dot(moved[k], table[k], preferred_element_type=jnp.float32)
+    result = jnp.dot(wide(moved, k), wide(table, k), preferred_element_type=jnp.float32)
     place = jnp.where(flips[v], edge - 1 - k, k)
     for h in range(halves):
         samples[v, place, h] = result[:, h * LANES : (h + 1) * LANES]
@@ -141,9 +143,9 @@
 
 def first_kernel(
     rounds, low_bits,
-    order, cgain, cbias, egain, ebias, cost, bricks, table0, table1,
+    order, cgain, cbias, egain, ebias, cost, bricks, weights0, weights1,
     send, samples, moved_next, lines1, lines2, lines3, tab0, tab1, perm, levels, splats,
-    lines0, moved, s_order, s_cgain, s_cbias, v_cost, sems,
+    lines0, moved, w0, w1, s_order, s_cgain, s_cbias, v_cost, sems,
 ):
     me = lax.axis_index("depth")
     rows, edge = lines0.shape[0], moved.shape[0]
@@ -153,30 +155,23 @@
     quarters = [
         (1 - top) * 2 + 1 - second, (1 - top) * 2 + second, top * 2 + 1 - second, top * 2 + second
     ]
-    small = [(order, s_order), (cgain, s_cgain), (cbias, s_cbias), (cost, v_cost)]
+    small = [(weights0, w0), (weights1, w1), (order, s_order), (cgain, s_cgain), (cbias, s_cbias), (cost, v_cost)]
     pairs = list(small)
-    pairs.append((bricks.at[pl.ds(quarters[0] * rows, rows)], lines0))
-    for h in range(halves):
-        span = pl.ds(h * LANES, LANES)
-        pairs.append((table0, tab0.at[:, span, span]))
-    pairs.append((table1, tab1))
-    for quarter, lines in zip(quarters[1:], (lines1, lines2, lines3)):
-        pairs.append((bricks.at[pl.ds(quarter * rows, rows)], lines))
+    for quarter, lines in zip(quarters, (lines0, lines1, lines2, lines3)):
+        for h in range(halves):
+            span = pl.ds(h * LANES, LANES)
+            pairs.append((bricks.at[pl.ds(quarter * rows, rows), :, :, span], lines.at[:, h]))
     copies = [pltpu.make_async_copy(a, b, sems.at[i]) for i, (a, b) in enumerate(pairs)]
     for copy in copies:
         copy.start()
+    ready = [copies[len(small) + q * halves : len(small) + (q + 1) * halves] for q in range(4)]
 
     size = BC * edge
-    out_row = lax.broadcasted_iota(jnp.int32, (size, size), 0)
-    in_row = lax.broadcasted_iota(jnp.int32, (size, size), 1)
-    wanted = lax.rem(out_row, BC) * edge + out_row // BC
-    perm[...] = jnp.where(wanted == in_row, 1.0, 0.0).astype(jnp.bfloat16)
-    zero = jnp.zeros((LANES, LANES), jnp.bfloat16)
-    for k in range(edge):
-        for a in range(halves):
-            for b in range(halves):
-                if a != b:
-                    tab0[k, a * LANES : (a + 1) * LANES, b * LANES : (b + 1) * LANES] = zero
+    for h in range(halves):
+        out_row = lax.broadcasted_iota(jnp.int32, (size, LANES), 0)
+        in_row = lax.broadcasted_iota(jnp.int32, (size, LANES), 1) + h * LANES
+        wanted = lax.rem(out_row, BC) * edge + out_row // BC
+        perm[h] = jnp.where(wanted == in_row, 1.0, 0.0).astype(jnp.bfloat16)
 
     for copy in copies[: len(small)]:
         copy.wait()
@@ -206,15 +201,31 @@
         picked = jnp.where(here + quarter * chunk == there, row, 0.0).astype(jnp.bfloat16)
         levels[i] = jnp.dot(picked, ones, preferred_element_type=jnp.float32)
 
-    copies[len(small)].wait()
+    tile = LANES // edge
+    lane = lax.broadcasted_iota(jnp.int32, (edge, LANES), 1)
+    source = lax.broadcasted_iota(jnp.int32, (edge, LANES), 0)
+    masks = [jnp.where(lane // edge == (-y) % tile, 1.0, 0.0) for y in range(tile)]
+    column = jnp.where(lax.rem(lane, edge) == source, 1.0, 0.0)
+    blank = jnp.zeros((edge, LANES), jnp.bfloat16)
+
+    def build(k, carry):
+        cols = w0[k]
+        blocks = [(cols * masks[y]).astype(jnp.bfloat16) for y in range(tile)]
+        for y in range(edge):
+            for h in range(halves):
+                span = pl.ds(y * edge, edge)
+                tab0[k, h, span, :] = blocks[y % tile] if y // tile == h else blank
+                tab1[k, h, span, :] = (column * w1[k, h, y : y + 1, :]).astype(jnp.bfloat16)
+        return carry
+
+    lax.fori_loop(0, edge, build, 0)
+
+    for copy in ready[0]:
+        copy.wait()
     for r in range(rows):
         to_slices(lines0, r, perm, moved)
-    for h in range(halves):
-        copies[len(small) + 1 + h].wait()
     for k in range(edge):
         resample(k, 0, flips, moved, tab0, samples)
-    for copy in copies[len(small) + 1 + halves :]:
-        copy.wait()
 
     mine = bit_of(me, 0)
 
@@ -223,7 +234,11 @@
 
     count = chunk // SUB * halves // 2
     beside(2, count, edge, item(0), lambda k: resample(k, 1, flips, moved, tab1, samples))
+    for copy in ready[1]:
+        copy.wait()
     beside(2, count, rows, item(1), lambda r: to_slices(lines1, r, perm, moved_next))
+    for copy in ready[2] + ready[3]:
+        copy.wait()
 
 
 def second_kernel(low_bits, samples, moved_next, tab0, tab1, levels, splats, kept, samples_next):
@@ -286,29 +301,29 @@
     )(*ins)
 
 
-def render(rounds, low_bits, order, cgain, cbias, egain, ebias, cost, bricks, table0, table1):
+def render(rounds, low_bits, order, cgain, cbias, egain, ebias, cost, bricks, weights0, weights1):
     total, edge, plane = bricks.shape
     rows = total // BC // 4
     chunk, halves, size = rows * BC, plane // LANES, BC * edge
     f32, bf16 = jnp.float32, jnp.bfloat16
     part = ((rows * halves // 2, 2, 4, BC, LANES), f32)
     samples = ((2, edge, halves, chunk, LANES), f32)
-    lines = ((rows, BC, edge, plane), bf16)
-    moved = ((edge, chunk, plane), bf16)
-    table = ((edge, plane, plane), bf16)
-    square = ((size, size), bf16)
+    lines = ((rows, halves, BC, edge, LANES), bf16)
+    moved = ((edge, halves, chunk, LANES), bf16)
+    table = ((edge, halves, plane, LANES), bf16)
+    square = ((size // LANES, size, LANES), bf16)
     levels = ((4, chunk, LANES), f32)
     splats = ((FRONTS + 2 * rounds, SUB, LANES), f32)
     bricks = bricks.reshape(total // BC, BC, edge, plane)
     far = lambda x: pltpu.with_memory_space_constraint(x, pltpu.HBM)
-    ins = (far(order), far(cgain), far(cbias), egain, ebias, far(cost), far(bricks), far(table0), far(table1))
+    ins = (far(order), far(cgain), far(cbias), egain, ebias, far(cost), far(bricks), far(weights0), far(weights1))
     specs = [HBM] * 3 + [pl.BlockSpec(memory_space=pltpu.SMEM)] * 2 + [HBM] * 4
     send0, samples0, moved1, _, lines2, lines3, tab0, tab1, perm, levels_, splats_ = call(
         functools.partial(first_kernel, rounds, low_bits), ins,
         (part, samples, moved, lines, lines, lines, table, table, square, levels, splats), 4000,
-        [pltpu.VMEM(*lines), pltpu.VMEM(*moved),
+        [pltpu.VMEM(*lines), pltpu.VMEM(*moved), pltpu.VMEM(weights0.shape, f32), pltpu.VMEM(weights1.shape, f32),
          pltpu.SMEM(order.shape, order.dtype), pltpu.SMEM(cgain.shape, f32), pltpu.SMEM(cbias.shape, f32),
-         pltpu.VMEM(cost.shape, cost.dtype), pltpu.SemaphoreType.DMA((9 + halves,))],
+         pltpu.VMEM(cost.shape, cost.dtype), pltpu.SemaphoreType.DMA((6 + 4 * halves,))],
         20 << 20, specs,
     )
     kept0, samples1 = call(
@@ -408,9 +423,9 @@
     rounds = count.bit_length() - 1
     units = total // BC * (plane // LANES)
     low_bits = (units // count).bit_length() - 1
-    table0, table1 = (jnp.asarray(t) for t in shear_tables(edge))
+    weights0, weights1 = (jnp.asarray(t) for t in shear_weights(edge))
     splats, parts = render(
-        rounds, low_bits, order, color_gain, color_bias, ext_gain, ext_bias, cost, bricks, table0, table1
+        rounds, low_bits, order, color_gain, color_bias, ext_gain, ext_bias, cost, bricks, weights0, weights1
     )
     f32, i16 = jnp.float32, jnp.int16
     near = rounds - 2

time: 28.6 us -> 28.7 us (level)
  transfers between devices with their start and end apart: 7 -> 7, of which waited for: 3 -> 3; matrix products, arithmetic and copies ran while one was open for 0% -> 0% of each run, Pallas kernels for 34% -> 35%
where the time goes in v4:
time: 28.7 us; the launch traced here: 28.5 us
  Pallas kernels  15.9 us (55%)
  starting transfers between devices  6.12 us (21%)
  waiting for transfers between devices  5.17 us (18%)
  between operations  1.34 us (5%)
    pallas_call x9, Pallas kernels, call(): pl.pallas_call(kernel, out_shape=outs, in_specs=specs or [VMEM] * len(ins...  15.9 us
    ppermute x7, starting transfers between devices, swapped(): return lax.ppermute(x, 'depth', [(i, i ^ 1 << bit) for i in range(count)])  6.12 us
    ppermute x7, waiting for transfers between devices, swapped(): return lax.ppermute(x, 'depth', [(i, i ^ 1 << bit) for i in range(count)])  5.17 us
  transfers between devices with their start and end apart: 7, of which 3 were waited for; matrix products, arithmetic and copies ran while one was open for 0% of the time, Pallas kernels for 35%

profile of v4, /device:TPU:0, one launch (start us, length us, event | category | flops | bytes accessed | tf_op | source)
XLA Modules:
  0.0 28.5 jit_solution(4426599923600345217)
XLA Ops:
  1.3 5.0 %shard_map.91 = (f32[4,2,4,16,128]{4,3,2,1,0:T(8,128)S(1)}, f32[2,16,2,64,128]{4,3,2,1,0:T(8,128)S(1)}, bf16[16,2,64,128]{3,2,1,0:T(8,128)(2,1)S(1)}, bf16[4,2,1...) custom-call(s32[2,8]{1,0:T(2,128)} %order.1, ...), custom_call_target="tpu_custom_call" | custom-call | flops 16384000 | bytes 262144 | tf_op jit(solution)/shard_map/pallas_call | solution.py:293
  6.3 0.6 %collective-permute-start.4 = (f32[4,2,4,16,128]{4,3,2,1,0:T(8,128)S(1)}, f32[4,2,4,16,128]{4,3,2,1,0:T(8,128)S(1)}, u32[]{:S(2)}, u32[]{:S(2)}) collective-permute-start(f32[4,2,4,16,128]{4,3,2,1,0:T(8,128)S(1)} %get-tuple-element.44), channel_id=1, source_target_pairs={{0,4},{4,0},{8,12},{12,8},{16,20},{20,16},{24,28},{28,24},{1,5},{5... | collective-permute-start | bytes 786440 | tf_op jit(solution)/shard_map/ppermute | solution.py:416
  6.8 1.3 %shard_map.92 = (f32[4,2,4,16,128]{4,3,2,1,0:T(8,128)S(1)}, f32[2,16,2,64,128]{4,3,2,1,0:T(8,128)S(1)}) custom-call(f32[2,16,2,64,128]{4,3,2,1,0:T(8,128)S(1)} %get-tuple-element.26.samples, bf16[16,2,64,128]{3,2,1,0:T(8,128)(2,1)S(1)} %get-tuple-element.27.moved_next, bf16[16,2,256,128]{3,2,1,0:T(8,128)(2,1)S(1)} %get-tuple-element.28.tab0.refs_2_, ...), custom_call_target="tpu_custom_call" | custom-call | flops 7372800 | bytes 262144 | tf_op jit(solution)/shard_map/pallas_call | solution.py:293
  8.1 3.2 %shard_map.93 = (f32[4,2,4,16,128]{4,3,2,1,0:T(8,128)S(1)}, f32[4,2,4,16,128]{4,3,2,1,0:T(8,128)S(1)}, f32[2,16,2,64,128]{4,3,2,1,0:T(8,128)S(1)}, bf16[16,2,64,128]{3,2,1,0:T(8,128)(2,1)}) custom-call(f32[2,16,2,64,128]{4,3,2,1,0:T(8,128)S(1)} %get-tuple-element.31.refs_0_, bf16[4,2,16,16,128]{4,3,2,1,0:T(8,128)(2,1)S(1)} %get-tuple-element.32.refs_1_, ...), custom_call_target="tpu_custom_call" | custom-call | flops 14336000 | bytes 262144 | tf_op jit(solution)/shard_map/pallas_call | solution.py:293
  11.3 3.2 %shard_map.94 = (f32[4,2,4,16,128]{4,3,2,1,0:T(8,128)S(1)}, f32[4,2,4,16,128]{4,3,2,1,0:T(8,128)S(1)}, f32[2,16,2,64,128]{4,3,2,1,0:T(8,128)S(1)}, bf16[16,2,64,128]{3,2,1,0:T(8,128)(2,1)}) custom-call(f32[2,16,2,64,128]{4,3,2,1,0:T(8,128)S(1)} %get-tuple-element.34.refs_0_, bf16[4,2,16,16,128]{4,3,2,1,0:T(8,128)(2,1)S(1)} %get-tuple-element.35.refs_1_, ...), custom_call_target="tpu_custom_call" | custom-call | flops 14336000 | bytes 262144 | tf_op jit(solution)/shard_map/pallas_call | solution.py:293
  14.5 0.0 collective-permute-start.1
  14.5 0.5 %collective-permute-start.3 = (f32[4,2,4,16,128]{4,3,2,1,0:T(8,128)S(1)}, f32[4,2,4,16,128]{4,3,2,1,0:T(8,128)S(1)}, u32[]{:S(2)}, u32[]{:S(2)}) collective-permute-start(f32[4,2,4,16,128]{4,3,2,1,0:T(8,128)S(1)} %get-tuple-element.42), channel_id=1, source_target_pairs={{0,4},{4,0},{8,12},{12,8},{16,20},{20,16},{24,28},{28,24},{1,5},{5... | collective-permute-start | bytes 786440 | tf_op jit(solution)/shard_map/ppermute | solution.py:416
  15.0 0.0 collective-permute-done.4.refs_0_
  15.0 0.1 shard_map.97
  15.2 2.5 %collective-permute-start.5 = (s16[4,2,4,16,128]{4,3,2,1,0:T(8,128)(2,1)S(1)}, s16[4,2,4,16,128]{4,3,2,1,0:T(8,128)(2,1)S(1)}, u32[]{:S(2)}, u32[]{:S(2)}) collective-permute-start(s16[4,2,4,16,128]{4,3,2,1,0:T(8,128)(2,1)S(1)} %shard_map.97), channel_id=1, source_target_pairs={{0,8},{4,12},{8,0},{12,4},{16,24},{20,28},{24,16},{28,20},{1,9},{5... | collective-permute-start | bytes 393224 | tf_op jit(solution)/shard_map/ppermute | solution.py:416
  17.7 1.7 %shard_map.95 = (f32[4,2,4,16,128]{4,3,2,1,0:T(8,128)S(1)}, f32[4,2,4,16,128]{4,3,2,1,0:T(8,128)S(1)}) custom-call(f32[2,16,2,64,128]{4,3,2,1,0:T(8,128)S(1)} %get-tuple-element.36.refs_0_, f32[4,64,128]{2,1,0:T(8,128)S(1)} %get-tuple-element.30.levels.refs_5_.refs_1_, f32[16,8,128]{2,1,0:T(8,128)S(1)} %get-tuple-element.25.splats.refs_6_.refs_2_), custom_call_target="tpu_custom_call" | custom-call | flops 13516800 | bytes 262144 | tf_op jit(solution)/shard_map/pallas_call | solution.py:293
  19.5 0.3 collective-permute-start
  19.7 0.0 collective-permute-done.1.refs_0_
  19.7 0.1 shard_map.96
  19.9 0.4 %collective-permute-start.2 = (s16[4,2,4,16,128]{4,3,2,1,0:T(8,128)(2,1)S(1)}, s16[4,2,4,16,128]{4,3,2,1,0:T(8,128)(2,1)S(1)}, u32[]{:S(2)}, u32[]{:S(2)}) collective-permute-start(s16[4,2,4,16,128]{4,3,2,1,0:T(8,128)(2,1)S(1)} %shard_map.96), channel_id=1, source_target_pairs={{0,8},{4,12},{8,0},{12,4},{16,24},{20,28},{24,16},{28,20},{1,9},{5... | collective-permute-start | bytes 393224 | tf_op jit(solution)/shard_map/ppermute | solution.py:416
  20.3 0.0 collective-permute-done.3.refs_0_
  20.3 1.6 %collective-permute-done.5.refs_1_ = s16[4,2,4,16,128]{4,3,2,1,0:T(8,128)(2,1)S(1)} collective-permute-done((s16[4,2,4,16,128]{4,3,2,1,0:T(8,128)(2,1)S(1)}, s16[4,2,4,16,128]{4,3,2,1,0:T(8,128)(2,1)S(1)}, u32[]{:S(2)}, u32[]{:S(2)}) %collective-permute-start.5) | collective-permute-done | bytes 131104 | tf_op jit(solution)/shard_map/ppermute | solution.py:416
  21.9 0.2 shard_map.98
  22.1 1.8 %collective-permute-start.6 = (s16[4,2,4,16,128]{4,3,2,1,0:T(8,128)(2,1)S(1)}, s16[4,2,4,16,128]{4,3,2,1,0:T(8,128)(2,1)S(1)}, u32[]{:S(2)}, u32[]{:S(2)}) collective-permute-start(s16[4,2,4,16,128]{4,3,2,1,0:T(8,128)(2,1)S(1)} %shard_map.98), channel_id=1, source_target_pairs={{0,16},{4,20},{8,24},{12,28},{16,0},{20,4},{24,8},{28,12},{1,17},{... | collective-permute-start | bytes 393224 | tf_op jit(solution)/shard_map/ppermute | solution.py:416
  23.9 0.0 collective-permute-done.refs_0_
  23.9 1.7 %collective-permute-done.2.refs_1_ = s16[4,2,4,16,128]{4,3,2,1,0:T(8,128)(2,1)S(1)} collective-permute-done((s16[4,2,4,16,128]{4,3,2,1,0:T(8,128)(2,1)S(1)}, s16[4,2,4,16,128]{4,3,2,1,0:T(8,128)(2,1)S(1)}, u32[]{:S(2)}, u32[]{:S(2)}) %collective-permute-start.2) | collective-permute-done | bytes 131104 | tf_op jit(solution)/shard_map/ppermute | solution.py:416
  25.6 1.8 %collective-permute-done.6.refs_2_ = s16[4,2,4,16,128]{4,3,2,1,0:T(8,128)(2,1)S(1)} collective-permute-done((s16[4,2,4,16,128]{4,3,2,1,0:T(8,128)(2,1)S(1)}, s16[4,2,4,16,128]{4,3,2,1,0:T(8,128)(2,1)S(1)}, u32[]{:S(2)}, u32[]{:S(2)}) %collective-permute-start.6) | collective-permute-done | bytes 131104 | tf_op jit(solution)/shard_map/ppermute | solution.py:416
  27.5 1.1 %shard_map.99 = f32[2,4,32,256]{3,2,1,0:T(8,128)} custom-call(f32[16,8,128]{2,1,0:T(8,128)S(1)} %get-tuple-element.25.splats.refs_6_.refs_2_, f32[4,2,4,16,128]{4,3,2,1,0:T(8,128)S(1)} %get-tuple-element.37.kept, f32[4,2,4,16,128]{4,3,2,1,0:T(8,128)S(1)} %collective-permute-done.refs_0_, s16[4,2,4,16,128]{4,3,2,1,0:T(8,128)(2,1)S(1)} %collective-permute-done.2.refs_1_, ...), custom_call_target="tpu_custom_call" | custom-call | flops 6144000 | bytes 262144 | tf_op jit(solution)/shard_map/pallas_call | solution.py:293
Async XLA Ops:
  6.3 8.8 %collective-permute-start.4 = (f32[4,2,4,16,128]{4,3,2,1,0:T(8,128)S(1)}, f32[4,2,4,16,128]{4,3,2,1,0:T(8,128)S(1)}, u32[]{:S(2)}, u32[]{:S(2)}) collective-permute-start(f32[4,2,4,16,128]{4,3,2,1,0:T(8,128)S(1)} %get-tuple-element.44), channel_id=1, source_target_pairs={{0,4},{4,0},{8,12},{12,8},{16,20},{20,16},{24,28},{28,24},{1,5},{5... | collective-permute-start | bytes 786440 | tf_op jit(solution)/shard_map/ppermute | solution.py:416
  14.5 5.2 %collective-permute-start.1 = (f32[4,2,4,16,128]{4,3,2,1,0:T(8,128)S(1)}, f32[4,2,4,16,128]{4,3,2,1,0:T(8,128)S(1)}, u32[]{:S(2)}, u32[]{:S(2)}) collective-permute-start(f32[4,2,4,16,128]{4,3,2,1,0:T(8,128)S(1)} %get-tuple-element.40), channel_id=1, source_target_pairs={{0,4},{4,0},{8,12},{12,8},{16,20},{20,16},{24,28},{28,24},{1,5},{5... | collective-permute-start | bytes 786440 | tf_op jit(solution)/shard_map/ppermute | solution.py:416
  14.5 5.7 %collective-permute-start.3 = (f32[4,2,4,16,128]{4,3,2,1,0:T(8,128)S(1)}, f32[4,2,4,16,128]{4,3,2,1,0:T(8,128)S(1)}, u32[]{:S(2)}, u32[]{:S(2)}) collective-permute-start(f32[4,2,4,16,128]{4,3,2,1,0:T(8,128)S(1)} %get-tuple-element.42), channel_id=1, source_target_pairs={{0,4},{4,0},{8,12},{12,8},{16,20},{20,16},{24,28},{28,24},{1,5},{5... | collective-permute-start | bytes 786440 | tf_op jit(solution)/shard_map/ppermute | solution.py:416
  15.2 6.7 %collective-permute-start.5 = (s16[4,2,4,16,128]{4,3,2,1,0:T(8,128)(2,1)S(1)}, s16[4,2,4,16,128]{4,3,2,1,0:T(8,128)(2,1)S(1)}, u32[]{:S(2)}, u32[]{:S(2)}) collective-permute-start(s16[4,2,4,16,128]{4,3,2,1,0:T(8,128)(2,1)S(1)} %shard_map.97), channel_id=1, source_target_pairs={{0,8},{4,12},{8,0},{12,4},{16,24},{20,28},{24,16},{28,20},{1,9},{5... | collective-permute-start | bytes 393224 | tf_op jit(solution)/shard_map/ppermute | solution.py:416
  19.5 4.5 %collective-permute-start = (f32[4,2,4,16,128]{4,3,2,1,0:T(8,128)S(1)}, f32[4,2,4,16,128]{4,3,2,1,0:T(8,128)S(1)}, u32[]{:S(2)}, u32[]{:S(2)}) collective-permute-start(f32[4,2,4,16,128]{4,3,2,1,0:T(8,128)S(1)} %get-tuple-element.38), channel_id=1, source_target_pairs={{0,4},{4,0},{8,12},{12,8},{16,20},{20,16},{24,28},{28,24},{1,5},{5... | collective-permute-start | bytes 786440 | tf_op jit(solution)/shard_map/ppermute | solution.py:416
  19.9 5.8 %collective-permute-start.2 = (s16[4,2,4,16,128]{4,3,2,1,0:T(8,128)(2,1)S(1)}, s16[4,2,4,16,128]{4,3,2,1,0:T(8,128)(2,1)S(1)}, u32[]{:S(2)}, u32[]{:S(2)}) collective-permute-start(s16[4,2,4,16,128]{4,3,2,1,0:T(8,128)(2,1)S(1)} %shard_map.96), channel_id=1, source_target_pairs={{0,8},{4,12},{8,0},{12,4},{16,24},{20,28},{24,16},{28,20},{1,9},{5... | collective-permute-start | bytes 393224 | tf_op jit(solution)/shard_map/ppermute | solution.py:416
  22.1 5.4 %collective-permute-start.6 = (s16[4,2,4,16,128]{4,3,2,1,0:T(8,128)(2,1)S(1)}, s16[4,2,4,16,128]{4,3,2,1,0:T(8,128)(2,1)S(1)}, u32[]{:S(2)}, u32[]{:S(2)}) collective-permute-start(s16[4,2,4,16,128]{4,3,2,1,0:T(8,128)(2,1)S(1)} %shard_map.98), channel_id=1, source_target_pairs={{0,16},{4,20},{8,24},{12,28},{16,0},{20,4},{24,8},{28,12},{1,17},{... | collective-permute-start | bytes 393224 | tf_op jit(solution)/shard_map/ppermute | solution.py:416

commit v5 on v4

--- a/solution.py
+++ b/solution.py
@@ -144,8 +144,8 @@
 def first_kernel(
     rounds, low_bits,
     order, cgain, cbias, egain, ebias, cost, bricks, weights0, weights1,
-    send, samples, moved_next, lines1, lines2, lines3, tab0, tab1, perm, levels, splats,
-    lines0, moved, w0, w1, s_order, s_cgain, s_cbias, v_cost, sems,
+    send, samples, moved1, moved2, lines3, tab0, tab1, perm, levels, splats,
+    lines0, lines1, lines2, moved, w0, w1, s_order, s_cgain, s_cbias, v_cost, sems,
 ):
     me = lax.axis_index("depth")
     rows, edge = lines0.shape[0], moved.shape[0]
@@ -234,10 +234,15 @@
 
     count = chunk // SUB * halves // 2
     beside(2, count, edge, item(0), lambda k: resample(k, 1, flips, moved, tab1, samples))
-    for copy in ready[1]:
+    for copy in ready[1] + ready[2]:
         copy.wait()
-    beside(2, count, rows, item(1), lambda r: to_slices(lines1, r, perm, moved_next))
-    for copy in ready[2] + ready[3]:
+
+    def slices(r):
+        to_slices(lines1, r, perm, moved1)
+        to_slices(lines2, r, perm, moved2)
+
+    beside(2, count, rows, item(1), slices)
+    for copy in ready[3]:
         copy.wait()
 
 
@@ -254,34 +259,32 @@
         )
 
 
-def quarter_kernel(low_bits, index, last, *refs):
-    if last:
-        samples, levels, splats, send, kept = refs
+def quarter_kernel(low_bits, index, *refs):
+    levels, splats, samples, *refs = refs
+    if index == 1:
+        moved, tab0, tab1, lines, perm, send, kept, samples_next, moved_next = refs
+    elif index == 2:
+        moved, tab0, tab1, send, kept, samples_next = refs
     else:
-        samples, lines, tab0, tab1, perm, levels, splats, send, kept, samples_next, moved = refs
+        send, kept = refs
     mine = bit_of(lax.axis_index("depth"), 0)
     edge = samples.shape[1]
     count = samples.shape[3] // SUB * samples.shape[2] // 2
+    rows = samples.shape[3] // BC
     flips = flips_of(splats)
-
-    def items(v):
-        def both(i):
+    for v in range(2):
+
+        def items(i):
             shade(i, 1 - mine, low_bits, v, samples, levels.at[index], splats, send)
             shade(i, mine, low_bits, v, samples, levels.at[index], splats, kept)
 
-        return both
-
-    def jobs(k):
-        resample(k, 0, flips, moved, tab0, samples_next)
-        resample(k, 1, flips, moved, tab1, samples_next)
-
-    if last:
-        beside(4, count, 0, items(0), None)
-        beside(4, count, 0, items(1), None)
-    else:
-        rows = lines.shape[0]
-        beside(4, count, rows, items(0), lambda r: to_slices(lines, r, perm, moved))
-        beside(4, count, edge, items(1), jobs)
+        def jobs(r):
+            for n in range(edge // rows):
+                resample(r * (edge // rows) + n, v, flips, moved, tab1 if v else tab0, samples_next)
+            if index == 1 and v == 0:
+                to_slices(lines, r, perm, moved_next)
+
+        beside(rows, count, rows if index < 3 else 0, items, jobs)
 
 
 VMEM = pl.BlockSpec(memory_space=pltpu.VMEM)
@@ -318,10 +321,11 @@
     far = lambda x: pltpu.with_memory_space_constraint(x, pltpu.HBM)
     ins = (far(order), far(cgain), far(cbias), egain, ebias, far(cost), far(bricks), far(weights0), far(weights1))
     specs = [HBM] * 3 + [pl.BlockSpec(memory_space=pltpu.SMEM)] * 2 + [HBM] * 4
-    send0, samples0, moved1, _, lines2, lines3, tab0, tab1, perm, levels_, splats_ = call(
+    send0, samples0, moved1, moved2, lines3, tab0, tab1, perm, levels_, splats_ = call(
         functools.partial(first_kernel, rounds, low_bits), ins,
-        (part, samples, moved, lines, lines, lines, table, table, square, levels, splats), 4000,
-        [pltpu.VMEM(*lines), pltpu.VMEM(*moved), pltpu.VMEM(weights0.shape, f32), pltpu.VMEM(weights1.shape, f32),
+        (part, samples, moved, moved, lines, table, table, square, levels, splats), 4000,
+        [pltpu.VMEM(*lines), pltpu.VMEM(*lines), pltpu.VMEM(*lines), pltpu.VMEM(*moved),
+         pltpu.VMEM(weights0.shape, f32), pltpu.VMEM(weights1.shape, f32),
          pltpu.SMEM(order.shape, order.dtype), pltpu.SMEM(cgain.shape, f32), pltpu.SMEM(cbias.shape, f32),
          pltpu.VMEM(cost.shape, cost.dtype), pltpu.SemaphoreType.DMA((6 + 4 * halves,))],
         20 << 20, specs,
@@ -330,17 +334,17 @@
         functools.partial(second_kernel, low_bits),
         (samples0, moved1, tab0, tab1, levels_, splats_), (part, samples), 1800, (), 14 << 20,
     )
-    send1, kept1, samples2, _ = call(
-        functools.partial(quarter_kernel, low_bits, 1, False),
-        (samples1, lines2, tab0, tab1, perm, levels_, splats_), (part, part, samples, moved), 3500, (), 14 << 20,
-    )
-    send2, kept2, samples3, _ = call(
-        functools.partial(quarter_kernel, low_bits, 2, False),
-        (samples2, lines3, tab0, tab1, perm, levels_, splats_), (part, part, samples, moved), 3500, (), 14 << 20,
+    send1, kept1, samples2, moved3 = call(
+        functools.partial(quarter_kernel, low_bits, 1),
+        (levels_, splats_, samples1, moved2, tab0, tab1, lines3, perm), (part, part, samples, moved), 3500, (), 14 << 20,
+    )
+    send2, kept2, samples3 = call(
+        functools.partial(quarter_kernel, low_bits, 2),
+        (levels_, splats_, samples2, moved3, tab0, tab1), (part, part, samples), 3500, (), 14 << 20,
     )
     send3, kept3 = call(
-        functools.partial(quarter_kernel, low_bits, 3, True),
-        (samples3, levels_, splats_), (part, part), 3300, (), 8 << 20,
+        functools.partial(quarter_kernel, low_bits, 3),
+        (levels_, splats_, samples3), (part, part), 3300, (), 8 << 20,
     )
     return splats_, [(send0, kept0), (send1, kept1), (send2, kept2), (send3, kept3)]
 

time: 28.7 us -> 26.1 us (0.909)
  Pallas kernels: 15.9 us -> 13.3 us
    pallas_call x9, Pallas kernels: 15.9 us -> 13.3 us  [call(): pl.pallas_call(kernel, out_shape=outs, in_specs=specs or [VMEM] * len(ins...]
  transfers between devices with their start and end apart: 7 -> 7, of which waited for: 3 -> 3; matrix products, arithmetic and copies ran while one was open for 0% -> 0% of each run, Pallas kernels for 35% -> 31%
where the time goes in v5:
time: 26.1 us; the launch traced here: 26 us
  Pallas kernels  13.3 us (51%)
  starting transfers between devices  6.19 us (24%)
  waiting for transfers between devices  5.11 us (20%)
  between operations  1.35 us (5%)
    pallas_call x9, Pallas kernels, call(): pl.pallas_call(kernel, out_shape=outs, in_specs=specs or [VMEM] * len(ins...  13.3 us
    ppermute x7, starting transfers between devices, swapped(): return lax.ppermute(x, 'depth', [(i, i ^ 1 << bit) for i in range(count)])  6.19 us
    ppermute x7, waiting for transfers between devices, swapped(): return lax.ppermute(x, 'depth', [(i, i ^ 1 << bit) for i in range(count)])  5.11 us
  transfers between devices with their start and end apart: 7, of which 3 were waited for; matrix products, arithmetic and copies ran while one was open for 0% of the time, Pallas kernels for 31%

profile of v5, /device:TPU:0, one launch (start us, length us, event | category | flops | bytes accessed | tf_op | source)
XLA Modules:
  0.0 26.0 jit_solution(1698871016790675965)
XLA Ops:
  1.3 4.3 %shard_map.91 = (f32[4,2,4,16,128]{4,3,2,1,0:T(8,128)S(1)}, f32[2,16,2,64,128]{4,3,2,1,0:T(8,128)S(1)}, bf16[16,2,64,128]{3,2,1,0:T(8,128)(2,1)S(1)}, bf16[16,2,...) custom-call(s32[2,8]{1,0:T(2,128)} %order.1, ...), custom_call_target="tpu_custom_call" | custom-call | flops 16384000 | bytes 262144 | tf_op jit(solution)/shard_map/pallas_call | solution.py:296
  5.6 0.6 %collective-permute-start.4 = (f32[4,2,4,16,128]{4,3,2,1,0:T(8,128)S(1)}, f32[4,2,4,16,128]{4,3,2,1,0:T(8,128)S(1)}, u32[]{:S(2)}, u32[]{:S(2)}) collective-permute-start(f32[4,2,4,16,128]{4,3,2,1,0:T(8,128)S(1)} %get-tuple-element.46), channel_id=1, source_target_pairs={{0,4},{4,0},{8,12},{12,8},{16,20},{20,16},{24,28},{28,24},{1,5},{5... | collective-permute-start | bytes 786440 | tf_op jit(solution)/shard_map/ppermute | solution.py:420
  6.1 1.3 %shard_map.92 = (f32[4,2,4,16,128]{4,3,2,1,0:T(8,128)S(1)}, f32[2,16,2,64,128]{4,3,2,1,0:T(8,128)S(1)}) custom-call(f32[2,16,2,64,128]{4,3,2,1,0:T(8,128)S(1)} %get-tuple-element.28.samples, bf16[16,2,64,128]{3,2,1,0:T(8,128)(2,1)S(1)} %get-tuple-element.29.moved_next, bf16[16,2,256,128]{3,2,1,0:T(8,128)(2,1)S(1)} %get-tuple-element.30.tab0.refs_4_, ...), custom_call_target="tpu_custom_call" | custom-call | flops 7372800 | bytes 262144 | tf_op jit(solution)/shard_map/pallas_call | solution.py:296
  7.4 2.5 %shard_map.93 = (f32[4,2,4,16,128]{4,3,2,1,0:T(8,128)S(1)}, f32[4,2,4,16,128]{4,3,2,1,0:T(8,128)S(1)}, f32[2,16,2,64,128]{4,3,2,1,0:T(8,128)S(1)}, bf16[16,2,64,128]{3,2,1,0:T(8,128)(2,1)S(1)}) custom-call(f32[4,64,128]{2,1,0:T(8,128)S(1)} %get-tuple-element.27.levels.refs_0_, f32[16,8,128]{2,1,0:T(8,128)S(1)} %get-tuple-element.26.splats.refs_1_, ...), custom_call_target="tpu_custom_call" | custom-call | flops 14336000 | bytes 262144 | tf_op jit(solution)/shard_map/pallas_call | solution.py:296
  10.0 2.0 %shard_map.94 = (f32[4,2,4,16,128]{4,3,2,1,0:T(8,128)S(1)}, f32[4,2,4,16,128]{4,3,2,1,0:T(8,128)S(1)}, f32[2,16,2,64,128]{4,3,2,1,0:T(8,128)S(1)}) custom-call(f32[4,64,128]{2,1,0:T(8,128)S(1)} %get-tuple-element.27.levels.refs_0_, f32[16,8,128]{2,1,0:T(8,128)S(1)} %get-tuple-element.26.splats.refs_1_, f32[2,16,2,64,128]{4,3,2,1,0:T(8,128)S(1)} %get-tuple-element.36.refs_2_, ...), custom_call_target="tpu_custom_call" | custom-call | flops 14336000 | bytes 262144 | tf_op jit(solution)/shard_map/pallas_call | solution.py:296
  12.0 0.1 collective-permute-start.1
  12.1 0.5 %collective-permute-start.3 = (f32[4,2,4,16,128]{4,3,2,1,0:T(8,128)S(1)}, f32[4,2,4,16,128]{4,3,2,1,0:T(8,128)S(1)}, u32[]{:S(2)}, u32[]{:S(2)}) collective-permute-start(f32[4,2,4,16,128]{4,3,2,1,0:T(8,128)S(1)} %get-tuple-element.44), channel_id=1, source_target_pairs={{0,4},{4,0},{8,12},{12,8},{16,20},{20,16},{24,28},{28,24},{1,5},{5... | collective-permute-start | bytes 786440 | tf_op jit(solution)/shard_map/ppermute | solution.py:420
  12.5 0.0 collective-permute-done.4.refs_0_
  12.6 0.1 shard_map.97
  12.7 2.6 %collective-permute-start.5 = (s16[4,2,4,16,128]{4,3,2,1,0:T(8,128)(2,1)S(1)}, s16[4,2,4,16,128]{4,3,2,1,0:T(8,128)(2,1)S(1)}, u32[]{:S(2)}, u32[]{:S(2)}) collective-permute-start(s16[4,2,4,16,128]{4,3,2,1,0:T(8,128)(2,1)S(1)} %shard_map.97), channel_id=1, source_target_pairs={{0,8},{4,12},{8,0},{12,4},{16,24},{20,28},{24,16},{28,20},{1,9},{5... | collective-permute-start | bytes 393224 | tf_op jit(solution)/shard_map/ppermute | solution.py:420
  15.3 1.7 %shard_map.95 = (f32[4,2,4,16,128]{4,3,2,1,0:T(8,128)S(1)}, f32[4,2,4,16,128]{4,3,2,1,0:T(8,128)S(1)}) custom-call(f32[4,64,128]{2,1,0:T(8,128)S(1)} %get-tuple-element.27.levels.refs_0_, f32[16,8,128]{2,1,0:T(8,128)S(1)} %get-tuple-element.26.splats.refs_1_, f32[2,16,2,64,128]{4,3,2,1,0:T(8,128)S(1)} %get-tuple-element.38.refs_2_), custom_call_target="tpu_custom_call" | custom-call | flops 13516800 | bytes 262144 | tf_op jit(solution)/shard_map/pallas_call | solution.py:296
  17.0 0.2 collective-permute-start
  17.2 0.0 collective-permute-done.1.refs_0_
  17.3 0.1 shard_map.96
  17.4 0.4 %collective-permute-start.2 = (s16[4,2,4,16,128]{4,3,2,1,0:T(8,128)(2,1)S(1)}, s16[4,2,4,16,128]{4,3,2,1,0:T(8,128)(2,1)S(1)}, u32[]{:S(2)}, u32[]{:S(2)}) collective-permute-start(s16[4,2,4,16,128]{4,3,2,1,0:T(8,128)(2,1)S(1)} %shard_map.96), channel_id=1, source_target_pairs={{0,8},{4,12},{8,0},{12,4},{16,24},{20,28},{24,16},{28,20},{1,9},{5... | collective-permute-start | bytes 393224 | tf_op jit(solution)/shard_map/ppermute | solution.py:420
  17.8 0.0 collective-permute-done.3.refs_0_
  17.8 1.6 %collective-permute-done.5.refs_1_ = s16[4,2,4,16,128]{4,3,2,1,0:T(8,128)(2,1)S(1)} collective-permute-done((s16[4,2,4,16,128]{4,3,2,1,0:T(8,128)(2,1)S(1)}, s16[4,2,4,16,128]{4,3,2,1,0:T(8,128)(2,1)S(1)}, u32[]{:S(2)}, u32[]{:S(2)}) %collective-permute-start.5) | collective-permute-done | bytes 131104 | tf_op jit(solution)/shard_map/ppermute | solution.py:420
  19.4 0.2 shard_map.98
  19.6 1.8 %collective-permute-start.6 = (s16[4,2,4,16,128]{4,3,2,1,0:T(8,128)(2,1)S(1)}, s16[4,2,4,16,128]{4,3,2,1,0:T(8,128)(2,1)S(1)}, u32[]{:S(2)}, u32[]{:S(2)}) collective-permute-start(s16[4,2,4,16,128]{4,3,2,1,0:T(8,128)(2,1)S(1)} %shard_map.98), channel_id=1, source_target_pairs={{0,16},{4,20},{8,24},{12,28},{16,0},{20,4},{24,8},{28,12},{1,17},{... | collective-permute-start | bytes 393224 | tf_op jit(solution)/shard_map/ppermute | solution.py:420
  21.4 0.0 collective-permute-done.refs_0_
  21.4 1.8 %collective-permute-done.2.refs_1_ = s16[4,2,4,16,128]{4,3,2,1,0:T(8,128)(2,1)S(1)} collective-permute-done((s16[4,2,4,16,128]{4,3,2,1,0:T(8,128)(2,1)S(1)}, s16[4,2,4,16,128]{4,3,2,1,0:T(8,128)(2,1)S(1)}, u32[]{:S(2)}, u32[]{:S(2)}) %collective-permute-start.2) | collective-permute-done | bytes 131104 | tf_op jit(solution)/shard_map/ppermute | solution.py:420
  23.2 1.7 %collective-permute-done.6.refs_2_ = s16[4,2,4,16,128]{4,3,2,1,0:T(8,128)(2,1)S(1)} collective-permute-done((s16[4,2,4,16,128]{4,3,2,1,0:T(8,128)(2,1)S(1)}, s16[4,2,4,16,128]{4,3,2,1,0:T(8,128)(2,1)S(1)}, u32[]{:S(2)}, u32[]{:S(2)}) %collective-permute-start.6) | collective-permute-done | bytes 131104 | tf_op jit(solution)/shard_map/ppermute | solution.py:420
  24.9 1.1 %shard_map.99 = f32[2,4,32,256]{3,2,1,0:T(8,128)} custom-call(f32[16,8,128]{2,1,0:T(8,128)S(1)} %get-tuple-element.26.splats.refs_1_, f32[4,2,4,16,128]{4,3,2,1,0:T(8,128)S(1)} %get-tuple-element.39.kept, f32[4,2,4,16,128]{4,3,2,1,0:T(8,128)S(1)} %collective-permute-done.refs_0_, s16[4,2,4,16,128]{4,3,2,1,0:T(8,128)(2,1)S(1)} %collective-permute-done.2.refs_1_, ...), custom_call_target="tpu_custom_call" | custom-call | flops 6144000 | bytes 262144 | tf_op jit(solution)/shard_map/pallas_call | solution.py:296
Async XLA Ops:
  5.6 7.0 %collective-permute-start.4 = (f32[4,2,4,16,128]{4,3,2,1,0:T(8,128)S(1)}, f32[4,2,4,16,128]{4,3,2,1,0:T(8,128)S(1)}, u32[]{:S(2)}, u32[]{:S(2)}) collective-permute-start(f32[4,2,4,16,128]{4,3,2,1,0:T(8,128)S(1)} %get-tuple-element.46), channel_id=1, source_target_pairs={{0,4},{4,0},{8,12},{12,8},{16,20},{20,16},{24,28},{28,24},{1,5},{5... | collective-permute-start | bytes 786440 | tf_op jit(solution)/shard_map/ppermute | solution.py:420
  12.0 5.3 %collective-permute-start.1 = (f32[4,2,4,16,128]{4,3,2,1,0:T(8,128)S(1)}, f32[4,2,4,16,128]{4,3,2,1,0:T(8,128)S(1)}, u32[]{:S(2)}, u32[]{:S(2)}) collective-permute-start(f32[4,2,4,16,128]{4,3,2,1,0:T(8,128)S(1)} %get-tuple-element.42), channel_id=1, source_target_pairs={{0,4},{4,0},{8,12},{12,8},{16,20},{20,16},{24,28},{28,24},{1,5},{5... | collective-permute-start | bytes 786440 | tf_op jit(solution)/shard_map/ppermute | solution.py:420
  12.1 5.7 %collective-permute-start.3 = (f32[4,2,4,16,128]{4,3,2,1,0:T(8,128)S(1)}, f32[4,2,4,16,128]{4,3,2,1,0:T(8,128)S(1)}, u32[]{:S(2)}, u32[]{:S(2)}) collective-permute-start(f32[4,2,4,16,128]{4,3,2,1,0:T(8,128)S(1)} %get-tuple-element.44), channel_id=1, source_target_pairs={{0,4},{4,0},{8,12},{12,8},{16,20},{20,16},{24,28},{28,24},{1,5},{5... | collective-permute-start | bytes 786440 | tf_op jit(solution)/shard_map/ppermute | solution.py:420
  12.7 6.7 %collective-permute-start.5 = (s16[4,2,4,16,128]{4,3,2,1,0:T(8,128)(2,1)S(1)}, s16[4,2,4,16,128]{4,3,2,1,0:T(8,128)(2,1)S(1)}, u32[]{:S(2)}, u32[]{:S(2)}) collective-permute-start(s16[4,2,4,16,128]{4,3,2,1,0:T(8,128)(2,1)S(1)} %shard_map.97), channel_id=1, source_target_pairs={{0,8},{4,12},{8,0},{12,4},{16,24},{20,28},{24,16},{28,20},{1,9},{5... | collective-permute-start | bytes 393224 | tf_op jit(solution)/shard_map/ppermute | solution.py:420
  17.0 4.4 %collective-permute-start = (f32[4,2,4,16,128]{4,3,2,1,0:T(8,128)S(1)}, f32[4,2,4,16,128]{4,3,2,1,0:T(8,128)S(1)}, u32[]{:S(2)}, u32[]{:S(2)}) collective-permute-start(f32[4,2,4,16,128]{4,3,2,1,0:T(8,128)S(1)} %get-tuple-element.40), channel_id=1, source_target_pairs={{0,4},{4,0},{8,12},{12,8},{16,20},{20,16},{24,28},{28,24},{1,5},{5... | collective-permute-start | bytes 786440 | tf_op jit(solution)/shard_map/ppermute | solution.py:420
  17.4 5.8 %collective-permute-start.2 = (s16[4,2,4,16,128]{4,3,2,1,0:T(8,128)(2,1)S(1)}, s16[4,2,4,16,128]{4,3,2,1,0:T(8,128)(2,1)S(1)}, u32[]{:S(2)}, u32[]{:S(2)}) collective-permute-start(s16[4,2,4,16,128]{4,3,2,1,0:T(8,128)(2,1)S(1)} %shard_map.96), channel_id=1, source_target_pairs={{0,8},{4,12},{8,0},{12,4},{16,24},{20,28},{24,16},{28,20},{1,9},{5... | collective-permute-start | bytes 393224 | tf_op jit(solution)/shard_map/ppermute | solution.py:420
  19.6 5.3 %collective-permute-start.6 = (s16[4,2,4,16,128]{4,3,2,1,0:T(8,128)(2,1)S(1)}, s16[4,2,4,16,128]{4,3,2,1,0:T(8,128)(2,1)S(1)}, u32[]{:S(2)}, u32[]{:S(2)}) collective-permute-start(s16[4,2,4,16,128]{4,3,2,1,0:T(8,128)(2,1)S(1)} %shard_map.98), channel_id=1, source_target_pairs={{0,16},{4,20},{8,24},{12,28},{16,0},{20,4},{24,8},{28,12},{1,17},{... | collective-permute-start | bytes 393224 | tf_op jit(solution)/shard_map/ppermute | solution.py:420

commit v6 on v5

--- a/solution.py
+++ b/solution.py
@@ -3,7 +3,6 @@
 
 import jax
 import jax.numpy as jnp
-import numpy as np
 from jax import lax
 from jax.experimental import pallas as pl
 from jax.experimental.pallas import tpu as pltpu
@@ -21,35 +20,6 @@
 CODE_BIAS = 32768.0
 
 
-def shear_taps(brick_edge, view):
-    f32 = np.float32
-    slice_index = np.arange(brick_edge, dtype=f32)[:, None]
-    position = np.arange(brick_edge, dtype=f32)[None, :] + f32(SHEAR[view]) * (
-        slice_index - f32((brick_edge - 1) / 2.0)
-    )
-    anchor = np.floor(position)
-    fraction = (position - anchor).astype(f32)
-    low = (f32(1.0) - fraction).astype(jnp.bfloat16).astype(f32)
-    high = fraction.astype(jnp.bfloat16).astype(f32)
-    return anchor.astype(np.int32), low, high
-
-
-def shear_lines(brick_edge, view):
-    anchor, low, high = shear_taps(brick_edge, view)
-    source = np.arange(brick_edge)[None, :, None]
-    table = np.where(source == anchor[:, None, :], low[:, None, :], 0.0)
-    return table + np.where(source == anchor[:, None, :] + 1, high[:, None, :], 0.0)
-
-
-def shear_weights(edge):
-    lane = np.arange(LANES)
-    turned = (-(lane // edge) % (LANES // edge)) * edge + lane % edge
-    cols = np.tile(shear_lines(edge, 0), (1, 1, LANES // edge))
-    rows = np.repeat(shear_lines(edge, 1), edge, axis=2)
-    rows = rows.reshape(edge, edge, -1, LANES)[..., turned].transpose(0, 2, 1, 3)
-    return cols.astype(np.float32), rows.astype(np.float32)
-
-
 def encode(x):
     logs = jnp.log(jnp.maximum(x, 2.0**-CODE_RANGE))
     code = logs * (CODE_STEP * LOG2E) + (CODE_RANGE * CODE_STEP + 0.5)
@@ -75,7 +45,7 @@
 
 
 def shade(item, bit, low_bits, v, samples, levels, splats, out):
-    edge, halves = samples.shape[1], samples.shape[2]
+    edge, halves = samples[v].shape[0], samples[v].shape[1]
     slot, group = item // 2, lax.rem(item, 2)
     unit = spread_bit(slot, low_bits, bit)
     h = lax.rem(unit, halves)
@@ -88,11 +58,12 @@
         need = j + flip * (3 - 2 * j)
         shift.append(jnp.where(level > need, ext_shift, -1e30))
     clear = jnp.ones((SUB, LANES), jnp.float32)
+    depth = jnp.zeros((SUB, LANES), jnp.float32)
     sums = [jnp.zeros((SUB, LANES), jnp.float32) for _ in range(3)]
     for k in range(edge):
-        s = samples[v, k, h, pl.ds(start, SUB), :]
-        passed = jnp.exp2(-jnp.exp2(s * ext_slope + shift[k // (edge // 4)]))
-        beyond = clear * passed
+        s = samples[v][k, h, pl.ds(start, SUB), :]
+        depth = depth - jnp.exp2(s * ext_slope + shift[k // (edge // 4)])
+        beyond = jnp.exp2(depth)
         weight = clear - beyond
         clear = beyond
         for c in range(3):
@@ -123,11 +94,11 @@
 
 
 def resample(k, v, flips, moved, table, samples):
-    edge, halves = samples.shape[1], samples.shape[2]
+    edge, halves = samples[v].shape[0], samples[v].shape[1]
     result = jnp.dot(wide(moved, k), wide(table, k), preferred_element_type=jnp.float32)
     place = jnp.where(flips[v], edge - 1 - k, k)
     for h in range(halves):
-        samples[v, place, h] = result[:, h * LANES : (h + 1) * LANES]
+        samples[v][place, h] = result[:, h * LANES : (h + 1) * LANES]
 
 
 def beside(steps, items, jobs, item_fn, job_fn):
@@ -143,19 +114,20 @@
 
 def first_kernel(
     rounds, low_bits,
-    order, cgain, cbias, egain, ebias, cost, bricks, weights0, weights1,
-    send, samples, moved1, moved2, lines3, tab0, tab1, perm, levels, splats,
-    lines0, lines1, lines2, moved, w0, w1, s_order, s_cgain, s_cbias, v_cost, sems,
+    order, cgain, cbias, egain, ebias, cost, bricks,
+    send, samples0, samples1, moved1, moved2, lines3, tab0, tab1, perm, levels, splats,
+    lines0, lines1, lines2, moved, s_order, s_cgain, s_cbias, v_cost, sems,
 ):
     me = lax.axis_index("depth")
     rows, edge = lines0.shape[0], moved.shape[0]
-    halves = samples.shape[2]
+    samples = (samples0, samples1)
+    halves = samples0.shape[1]
     chunk = rows * BC
     top, second = bit_of(me, rounds - 1), bit_of(me, rounds - 2)
     quarters = [
         (1 - top) * 2 + 1 - second, (1 - top) * 2 + second, top * 2 + 1 - second, top * 2 + second
     ]
-    small = [(weights0, w0), (weights1, w1), (order, s_order), (cgain, s_cgain), (cbias, s_cbias), (cost, v_cost)]
+    small = [(order, s_order), (cgain, s_cgain), (cbias, s_cbias), (cost, v_cost)]
     pairs = list(small)
     for quarter, lines in zip(quarters, (lines0, lines1, lines2, lines3)):
         for h in range(halves):
@@ -172,6 +144,41 @@
         in_row = lax.broadcasted_iota(jnp.int32, (size, LANES), 1) + h * LANES
         wanted = lax.rem(out_row, BC) * edge + out_row // BC
         perm[h] = jnp.where(wanted == in_row, 1.0, 0.0).astype(jnp.bfloat16)
+
+    tile = LANES // edge
+    lane = lax.broadcasted_iota(jnp.int32, (edge, LANES), 1)
+    source = lax.broadcasted_iota(jnp.int32, (edge, LANES), 0)
+    masks = [jnp.where(lane // edge == (-y) % tile, 1.0, 0.0) for y in range(tile)]
+    same_column = lax.rem(lane, edge) == source
+    blank = jnp.zeros((edge, LANES), jnp.bfloat16)
+    target_col = lax.rem(lane, edge).astype(jnp.float32)
+    target_row = [(lax.rem(tile - lane // edge, tile) + h * tile).astype(jnp.float32) for h in range(halves)]
+    source = source.astype(jnp.float32)
+
+    def taps(target, view, k):
+        position = target + SHEAR[view] * (k.astype(jnp.float32) - (edge - 1) / 2.0)
+        anchor = jnp.floor(position)
+        high = position - anchor
+        return anchor, 1.0 - high, high
+
+    def weigh(source, anchor, low, high):
+        return jnp.where(source == anchor, low, 0.0) + jnp.where(source == anchor + 1.0, high, 0.0)
+
+    def build(k, carry):
+        cols = weigh(source, *taps(target_col, 0, k))
+        blocks = [(cols * masks[y]).astype(jnp.bfloat16) for y in range(tile)]
+        lines = []
+        for h in range(halves):
+            anchor, low, high = taps(target_row[h], 1, k)
+            lines.append((anchor, jnp.where(same_column, low, 0.0), jnp.where(same_column, high, 0.0)))
+        for y in range(edge):
+            for h in range(halves):
+                span = pl.ds(y * edge, edge)
+                tab0[k, h, span, :] = blocks[y % tile] if y // tile == h else blank
+                tab1[k, h, span, :] = weigh(float(y), *lines[h]).astype(jnp.bfloat16)
+        return carry
+
+    lax.fori_loop(0, edge, build, 0)
 
     for copy in copies[: len(small)]:
         copy.wait()
@@ -201,25 +208,6 @@
         picked = jnp.where(here + quarter * chunk == there, row, 0.0).astype(jnp.bfloat16)
         levels[i] = jnp.dot(picked, ones, preferred_element_type=jnp.float32)
 
-    tile = LANES // edge
-    lane = lax.broadcasted_iota(jnp.int32, (edge, LANES), 1)
-    source = lax.broadcasted_iota(jnp.int32, (edge, LANES), 0)
-    masks = [jnp.where(lane // edge == (-y) % tile, 1.0, 0.0) for y in range(tile)]
-    column = jnp.where(lax.rem(lane, edge) == source, 1.0, 0.0)
-    blank = jnp.zeros((edge, LANES), jnp.bfloat16)
-
-    def build(k, carry):
-        cols = w0[k]
-        blocks = [(cols * masks[y]).astype(jnp.bfloat16) for y in range(tile)]
-        for y in range(edge):
-            for h in range(halves):
-                span = pl.ds(y * edge, edge)
-                tab0[k, h, span, :] = blocks[y % tile] if y // tile == h else blank
-                tab1[k, h, span, :] = (column * w1[k, h, y : y + 1, :]).astype(jnp.bfloat16)
-        return carry
-
-    lax.fori_loop(0, edge, build, 0)
-
     for copy in ready[0]:
         copy.wait()
     for r in range(rows):
@@ -246,10 +234,11 @@
         copy.wait()
 
 
-def second_kernel(low_bits, samples, moved_next, tab0, tab1, levels, splats, kept, samples_next):
+def second_kernel(low_bits, here0, here1, moved_next, tab0, tab1, levels, splats, kept, next0, next1):
     mine = bit_of(lax.axis_index("depth"), 0)
-    edge = samples.shape[1]
-    count = samples.shape[3] // SUB * samples.shape[2] // 2
+    samples, samples_next = (here0, here1), (next0, next1)
+    edge, halves, chunk, _ = here0.shape
+    count = chunk // SUB * halves // 2
     flips = flips_of(splats)
     for v, table in enumerate((tab0, tab1)):
         beside(
@@ -260,17 +249,18 @@
 
 
 def quarter_kernel(low_bits, index, *refs):
-    levels, splats, samples, *refs = refs
+    levels, splats, here0, here1, *refs = refs
+    samples = (here0, here1)
     if index == 1:
-        moved, tab0, tab1, lines, perm, send, kept, samples_next, moved_next = refs
+        moved, tab0, tab1, lines, perm, send, kept, *samples_next, moved_next = refs
     elif index == 2:
-        moved, tab0, tab1, send, kept, samples_next = refs
+        moved, tab0, tab1, send, kept, *samples_next = refs
     else:
         send, kept = refs
     mine = bit_of(lax.axis_index("depth"), 0)
-    edge = samples.shape[1]
-    count = samples.shape[3] // SUB * samples.shape[2] // 2
-    rows = samples.shape[3] // BC
+    edge, halves, chunk, _ = here0.shape
+    count = chunk // SUB * halves // 2
+    rows = chunk // BC
     flips = flips_of(splats)
     for v in range(2):
 
@@ -304,13 +294,13 @@
     )(*ins)
 
 
-def render(rounds, low_bits, order, cgain, cbias, egain, ebias, cost, bricks, weights0, weights1):
+def render(rounds, low_bits, order, cgain, cbias, egain, ebias, cost, bricks):
     total, edge, plane = bricks.shape
     rows = total // BC // 4
     chunk, halves, size = rows * BC, plane // LANES, BC * edge
     f32, bf16 = jnp.float32, jnp.bfloat16
     part = ((rows * halves // 2, 2, 4, BC, LANES), f32)
-    samples = ((2, edge, halves, chunk, LANES), f32)
+    samples = ((edge, halves, chunk, LANES), f32)
     lines = ((rows, halves, BC, edge, LANES), bf16)
     moved = ((edge, halves, chunk, LANES), bf16)
     table = ((edge, halves, plane, LANES), bf16)
@@ -319,32 +309,31 @@
     splats = ((FRONTS + 2 * rounds, SUB, LANES), f32)
     bricks = bricks.reshape(total // BC, BC, edge, plane)
     far = lambda x: pltpu.with_memory_space_constraint(x, pltpu.HBM)
-    ins = (far(order), far(cgain), far(cbias), egain, ebias, far(cost), far(bricks), far(weights0), far(weights1))
-    specs = [HBM] * 3 + [pl.BlockSpec(memory_space=pltpu.SMEM)] * 2 + [HBM] * 4
-    send0, samples0, moved1, moved2, lines3, tab0, tab1, perm, levels_, splats_ = call(
+    ins = (far(order), far(cgain), far(cbias), egain, ebias, far(cost), far(bricks))
+    specs = [HBM] * 3 + [pl.BlockSpec(memory_space=pltpu.SMEM)] * 2 + [HBM] * 2
+    send0, *samples0, moved1, moved2, lines3, tab0, tab1, perm, levels_, splats_ = call(
         functools.partial(first_kernel, rounds, low_bits), ins,
-        (part, samples, moved, moved, lines, table, table, square, levels, splats), 4000,
+        (part, samples, samples, moved, moved, lines, table, table, square, levels, splats), 4000,
         [pltpu.VMEM(*lines), pltpu.VMEM(*lines), pltpu.VMEM(*lines), pltpu.VMEM(*moved),
-         pltpu.VMEM(weights0.shape, f32), pltpu.VMEM(weights1.shape, f32),
          pltpu.SMEM(order.shape, order.dtype), pltpu.SMEM(cgain.shape, f32), pltpu.SMEM(cbias.shape, f32),
-         pltpu.VMEM(cost.shape, cost.dtype), pltpu.SemaphoreType.DMA((6 + 4 * halves,))],
+         pltpu.VMEM(cost.shape, cost.dtype), pltpu.SemaphoreType.DMA((4 + 4 * halves,))],
         20 << 20, specs,
     )
-    kept0, samples1 = call(
+    kept0, *samples1 = call(
         functools.partial(second_kernel, low_bits),
-        (samples0, moved1, tab0, tab1, levels_, splats_), (part, samples), 1800, (), 14 << 20,
-    )
-    send1, kept1, samples2, moved3 = call(
+        (*samples0, moved1, tab0, tab1, levels_, splats_), (part, samples, samples), 1800, (), 14 << 20,
+    )
+    send1, kept1, *samples2, moved3 = call(
         functools.partial(quarter_kernel, low_bits, 1),
-        (levels_, splats_, samples1, moved2, tab0, tab1, lines3, perm), (part, part, samples, moved), 3500, (), 14 << 20,
-    )
-    send2, kept2, samples3 = call(
+        (levels_, splats_, *samples1, moved2, tab0, tab1, lines3, perm), (part, part, samples, samples, moved), 3500, (), 14 << 20,
+    )
+    send2, kept2, *samples3 = call(
         functools.partial(quarter_kernel, low_bits, 2),
-        (levels_, splats_, samples2, moved3, tab0, tab1), (part, part, samples), 3500, (), 14 << 20,
+        (levels_, splats_, *samples2, moved3, tab0, tab1), (part, part, samples, samples), 3500, (), 14 << 20,
     )
     send3, kept3 = call(
         functools.partial(quarter_kernel, low_bits, 3),
-        (levels_, splats_, samples3), (part, part), 3300, (), 8 << 20,
+        (levels_, splats_, *samples3), (part, part), 3300, (), 8 << 20,
     )
     return splats_, [(send0, kept0), (send1, kept1), (send2, kept2), (send3, kept3)]
 
@@ -427,9 +416,8 @@
     rounds = count.bit_length() - 1
     units = total // BC * (plane // LANES)
     low_bits = (units // count).bit_length() - 1
-    weights0, weights1 = (jnp.asarray(t) for t in shear_weights(edge))
     splats, parts = render(
-        rounds, low_bits, order, color_gain, color_bias, ext_gain, ext_bias, cost, bricks, weights0, weights1
+        rounds, low_bits, order, color_gain, color_bias, ext_gain, ext_bias, cost, bricks
     )
     f32, i16 = jnp.float32, jnp.int16
     near = rounds - 2

time: 26.1 us -> 25.1 us (0.962)
  Pallas kernels: 13.3 us -> 12.2 us
    pallas_call x9, Pallas kernels: 13.3 us -> 12.2 us  [call(): pl.pallas_call(kernel, out_shape=outs, in_specs=specs or [VMEM] * len(ins...]
where the time goes in v6:
time: 25.1 us; the launch traced here: 24.9 us
  Pallas kernels  12.2 us (49%)
  starting transfers between devices  6.19 us (25%)
  waiting for transfers between devices  5.18 us (21%)
  between operations  1.35 us (5%)
    pallas_call x9, Pallas kernels, call(): pl.pallas_call(kernel, out_shape=outs, in_specs=specs or [VMEM] * len(ins...  12.2 us
    ppermute x7, starting transfers between devices, swapped(): return lax.ppermute(x, 'depth', [(i, i ^ 1 << bit) for i in range(count)])  6.19 us
    ppermute x7, waiting for transfers between devices, swapped(): return lax.ppermute(x, 'depth', [(i, i ^ 1 << bit) for i in range(count)])  5.18 us
  transfers between devices with their start and end apart: 7, of which 3 were waited for; matrix products, arithmetic and copies ran while one was open for 0% of the time, Pallas kernels for 31%

profile of v6, /device:TPU:0, one launch (start us, length us, event | category | flops | bytes accessed | tf_op | source)
XLA Modules:
  0.0 24.9 jit_solution(15700784866539397107)
XLA Ops:
  1.3 3.4 %shard_map.73 = (f32[4,2,4,16,128]{4,3,2,1,0:T(8,128)S(1)}, f32[16,2,64,128]{3,2,1,0:T(8,128)S(1)}, f32[16,2,64,128]{3,2,1,0:T(8,128)S(1)}, bf16[16,2,64,128]{3,...) custom-call(s32[2,8]{1,0:T(2,128)} %order.1, ...), custom_call_target="tpu_custom_call" | custom-call | flops 16384000 | bytes 262144 | tf_op jit(solution)/shard_map/pallas_call | solution.py:286
  4.7 0.6 %collective-permute-start.4 = (f32[4,2,4,16,128]{4,3,2,1,0:T(8,128)S(1)}, f32[4,2,4,16,128]{4,3,2,1,0:T(8,128)S(1)}, u32[]{:S(2)}, u32[]{:S(2)}) collective-permute-start(f32[4,2,4,16,128]{4,3,2,1,0:T(8,128)S(1)} %get-tuple-element.54), channel_id=1, source_target_pairs={{0,4},{4,0},{8,12},{12,8},{16,20},{20,16},{24,28},{28,24},{1,5},{5... | collective-permute-start | bytes 786440 | tf_op jit(solution)/shard_map/ppermute | solution.py:409
  5.2 1.3 %shard_map.74 = (f32[4,2,4,16,128]{4,3,2,1,0:T(8,128)S(1)}, f32[16,2,64,128]{3,2,1,0:T(8,128)S(1)}, f32[16,2,64,128]{3,2,1,0:T(8,128)S(1)}) custom-call(f32[16,2,64,128]{3,2,1,0:T(8,128)S(1)} %get-tuple-element.32.here0, f32[16,2,64,128]{3,2,1,0:T(8,128)S(1)} %get-tuple-element.33.here1, bf16[16,2,64,128]{3,2,1,0:T(8,128)(2,1)S(1)} %get-tuple-element.34.moved_next, ...), custom_call_target="tpu_custom_call" | custom-call | flops 7372800 | bytes 262144 | tf_op jit(solution)/shard_map/pallas_call | solution.py:286
  6.6 2.5 %shard_map.75 = (f32[4,2,4,16,128]{4,3,2,1,0:T(8,128)S(1)}, f32[4,2,4,16,128]{4,3,2,1,0:T(8,128)S(1)}, f32[16,2,64,128]{3,2,1,0:T(8,128)S(1)}, f32[16,2,64,128]{...) custom-call(f32[4,64,128]{2,1,0:T(8,128)S(1)} %get-tuple-element.31.levels.refs_0_, ...), custom_call_target="tpu_custom_call" | custom-call | flops 14336000 | bytes 262144 | tf_op jit(solution)/shard_map/pallas_call | solution.py:286
  9.0 1.9 %shard_map.76 = (f32[4,2,4,16,128]{4,3,2,1,0:T(8,128)S(1)}, f32[4,2,4,16,128]{4,3,2,1,0:T(8,128)S(1)}, f32[16,2,64,128]{3,2,1,0:T(8,128)S(1)}, f32[16,2,64,128]{3,2,1,0:T(8,128)S(1)}) custom-call(f32[4,64,128]{2,1,0:T(8,128)S(1)} %get-tuple-element.31.levels.refs_0_, f32[16,8,128]{2,1,0:T(8,128)S(1)} %get-tuple-element.30.splats.refs_1_, ...), custom_call_target="tpu_custom_call" | custom-call | flops 14336000 | bytes 262144 | tf_op jit(solution)/shard_map/pallas_call | solution.py:286
  10.9 0.1 collective-permute-start.1
  11.0 0.5 %collective-permute-start.3 = (f32[4,2,4,16,128]{4,3,2,1,0:T(8,128)S(1)}, f32[4,2,4,16,128]{4,3,2,1,0:T(8,128)S(1)}, u32[]{:S(2)}, u32[]{:S(2)}) collective-permute-start(f32[4,2,4,16,128]{4,3,2,1,0:T(8,128)S(1)} %get-tuple-element.52), channel_id=1, source_target_pairs={{0,4},{4,0},{8,12},{12,8},{16,20},{20,16},{24,28},{28,24},{1,5},{5... | collective-permute-start | bytes 786440 | tf_op jit(solution)/shard_map/ppermute | solution.py:409
  11.5 0.0 collective-permute-done.4.refs_0_
  11.5 0.1 shard_map.79
  11.6 2.6 %collective-permute-start.5 = (s16[4,2,4,16,128]{4,3,2,1,0:T(8,128)(2,1)S(1)}, s16[4,2,4,16,128]{4,3,2,1,0:T(8,128)(2,1)S(1)}, u32[]{:S(2)}, u32[]{:S(2)}) collective-permute-start(s16[4,2,4,16,128]{4,3,2,1,0:T(8,128)(2,1)S(1)} %shard_map.79), channel_id=1, source_target_pairs={{0,8},{4,12},{8,0},{12,4},{16,24},{20,28},{24,16},{28,20},{1,9},{5... | collective-permute-start | bytes 393224 | tf_op jit(solution)/shard_map/ppermute | solution.py:409
  14.2 1.7 %shard_map.77 = (f32[4,2,4,16,128]{4,3,2,1,0:T(8,128)S(1)}, f32[4,2,4,16,128]{4,3,2,1,0:T(8,128)S(1)}) custom-call(f32[4,64,128]{2,1,0:T(8,128)S(1)} %get-tuple-element.31.levels.refs_0_, f32[16,8,128]{2,1,0:T(8,128)S(1)} %get-tuple-element.30.splats.refs_1_, f32[16,2,64,128]{3,2,1,0:T(8,128)S(1)} %get-tuple-element.45.refs_2_, ...), custom_call_target="tpu_custom_call" | custom-call | flops 13516800 | bytes 262144 | tf_op jit(solution)/shard_map/pallas_call | solution.py:286
  15.9 0.2 collective-permute-start
  16.1 0.0 collective-permute-done.1.refs_0_
  16.1 0.1 shard_map.78
  16.3 0.4 %collective-permute-start.2 = (s16[4,2,4,16,128]{4,3,2,1,0:T(8,128)(2,1)S(1)}, s16[4,2,4,16,128]{4,3,2,1,0:T(8,128)(2,1)S(1)}, u32[]{:S(2)}, u32[]{:S(2)}) collective-permute-start(s16[4,2,4,16,128]{4,3,2,1,0:T(8,128)(2,1)S(1)} %shard_map.78), channel_id=1, source_target_pairs={{0,8},{4,12},{8,0},{12,4},{16,24},{20,28},{24,16},{28,20},{1,9},{5... | collective-permute-start | bytes 393224 | tf_op jit(solution)/shard_map/ppermute | solution.py:409
  16.6 0.0 collective-permute-done.3.refs_0_
  16.6 1.7 %collective-permute-done.5.refs_1_ = s16[4,2,4,16,128]{4,3,2,1,0:T(8,128)(2,1)S(1)} collective-permute-done((s16[4,2,4,16,128]{4,3,2,1,0:T(8,128)(2,1)S(1)}, s16[4,2,4,16,128]{4,3,2,1,0:T(8,128)(2,1)S(1)}, u32[]{:S(2)}, u32[]{:S(2)}) %collective-permute-start.5) | collective-permute-done | bytes 131104 | tf_op jit(solution)/shard_map/ppermute | solution.py:409
  18.3 0.2 shard_map.80
  18.5 1.8 %collective-permute-start.6 = (s16[4,2,4,16,128]{4,3,2,1,0:T(8,128)(2,1)S(1)}, s16[4,2,4,16,128]{4,3,2,1,0:T(8,128)(2,1)S(1)}, u32[]{:S(2)}, u32[]{:S(2)}) collective-permute-start(s16[4,2,4,16,128]{4,3,2,1,0:T(8,128)(2,1)S(1)} %shard_map.80), channel_id=1, source_target_pairs={{0,16},{4,20},{8,24},{12,28},{16,0},{20,4},{24,8},{28,12},{1,17},{... | collective-permute-start | bytes 393224 | tf_op jit(solution)/shard_map/ppermute | solution.py:409
  20.4 0.0 collective-permute-done.refs_0_
  20.4 1.7 %collective-permute-done.2.refs_1_ = s16[4,2,4,16,128]{4,3,2,1,0:T(8,128)(2,1)S(1)} collective-permute-done((s16[4,2,4,16,128]{4,3,2,1,0:T(8,128)(2,1)S(1)}, s16[4,2,4,16,128]{4,3,2,1,0:T(8,128)(2,1)S(1)}, u32[]{:S(2)}, u32[]{:S(2)}) %collective-permute-start.2) | collective-permute-done | bytes 131104 | tf_op jit(solution)/shard_map/ppermute | solution.py:409
  22.1 1.8 %collective-permute-done.6.refs_2_ = s16[4,2,4,16,128]{4,3,2,1,0:T(8,128)(2,1)S(1)} collective-permute-done((s16[4,2,4,16,128]{4,3,2,1,0:T(8,128)(2,1)S(1)}, s16[4,2,4,16,128]{4,3,2,1,0:T(8,128)(2,1)S(1)}, u32[]{:S(2)}, u32[]{:S(2)}) %collective-permute-start.6) | collective-permute-done | bytes 131104 | tf_op jit(solution)/shard_map/ppermute | solution.py:409
  23.9 1.1 %shard_map.81 = f32[2,4,32,256]{3,2,1,0:T(8,128)} custom-call(f32[16,8,128]{2,1,0:T(8,128)S(1)} %get-tuple-element.30.splats.refs_1_, f32[4,2,4,16,128]{4,3,2,1,0:T(8,128)S(1)} %get-tuple-element.47.kept, f32[4,2,4,16,128]{4,3,2,1,0:T(8,128)S(1)} %collective-permute-done.refs_0_, s16[4,2,4,16,128]{4,3,2,1,0:T(8,128)(2,1)S(1)} %collective-permute-done.2.refs_1_, ...), custom_call_target="tpu_custom_call" | custom-call | flops 6144000 | bytes 262144 | tf_op jit(solution)/shard_map/pallas_call | solution.py:286
Async XLA Ops:
  4.7 6.8 %collective-permute-start.4 = (f32[4,2,4,16,128]{4,3,2,1,0:T(8,128)S(1)}, f32[4,2,4,16,128]{4,3,2,1,0:T(8,128)S(1)}, u32[]{:S(2)}, u32[]{:S(2)}) collective-permute-start(f32[4,2,4,16,128]{4,3,2,1,0:T(8,128)S(1)} %get-tuple-element.54), channel_id=1, source_target_pairs={{0,4},{4,0},{8,12},{12,8},{16,20},{20,16},{24,28},{28,24},{1,5},{5... | collective-permute-start | bytes 786440 | tf_op jit(solution)/shard_map/ppermute | solution.py:409
  10.9 5.2 %collective-permute-start.1 = (f32[4,2,4,16,128]{4,3,2,1,0:T(8,128)S(1)}, f32[4,2,4,16,128]{4,3,2,1,0:T(8,128)S(1)}, u32[]{:S(2)}, u32[]{:S(2)}) collective-permute-start(f32[4,2,4,16,128]{4,3,2,1,0:T(8,128)S(1)} %get-tuple-element.50), channel_id=1, source_target_pairs={{0,4},{4,0},{8,12},{12,8},{16,20},{20,16},{24,28},{28,24},{1,5},{5... | collective-permute-start | bytes 786440 | tf_op jit(solution)/shard_map/ppermute | solution.py:409
  11.0 5.6 %collective-permute-start.3 = (f32[4,2,4,16,128]{4,3,2,1,0:T(8,128)S(1)}, f32[4,2,4,16,128]{4,3,2,1,0:T(8,128)S(1)}, u32[]{:S(2)}, u32[]{:S(2)}) collective-permute-start(f32[4,2,4,16,128]{4,3,2,1,0:T(8,128)S(1)} %get-tuple-element.52), channel_id=1, source_target_pairs={{0,4},{4,0},{8,12},{12,8},{16,20},{20,16},{24,28},{28,24},{1,5},{5... | collective-permute-start | bytes 786440 | tf_op jit(solution)/shard_map/ppermute | solution.py:409
  11.6 6.7 %collective-permute-start.5 = (s16[4,2,4,16,128]{4,3,2,1,0:T(8,128)(2,1)S(1)}, s16[4,2,4,16,128]{4,3,2,1,0:T(8,128)(2,1)S(1)}, u32[]{:S(2)}, u32[]{:S(2)}) collective-permute-start(s16[4,2,4,16,128]{4,3,2,1,0:T(8,128)(2,1)S(1)} %shard_map.79), channel_id=1, source_target_pairs={{0,8},{4,12},{8,0},{12,4},{16,24},{20,28},{24,16},{28,20},{1,9},{5... | collective-permute-start | bytes 393224 | tf_op jit(solution)/shard_map/ppermute | solution.py:409
  15.9 4.5 %collective-permute-start = (f32[4,2,4,16,128]{4,3,2,1,0:T(8,128)S(1)}, f32[4,2,4,16,128]{4,3,2,1,0:T(8,128)S(1)}, u32[]{:S(2)}, u32[]{:S(2)}) collective-permute-start(f32[4,2,4,16,128]{4,3,2,1,0:T(8,128)S(1)} %get-tuple-element.48), channel_id=1, source_target_pairs={{0,4},{4,0},{8,12},{12,8},{16,20},{20,16},{24,28},{28,24},{1,5},{5... | collective-permute-start | bytes 786440 | tf_op jit(solution)/shard_map/ppermute | solution.py:409
  16.3 5.8 %collective-permute-start.2 = (s16[4,2,4,16,128]{4,3,2,1,0:T(8,128)(2,1)S(1)}, s16[4,2,4,16,128]{4,3,2,1,0:T(8,128)(2,1)S(1)}, u32[]{:S(2)}, u32[]{:S(2)}) collective-permute-start(s16[4,2,4,16,128]{4,3,2,1,0:T(8,128)(2,1)S(1)} %shard_map.78), channel_id=1, source_target_pairs={{0,8},{4,12},{8,0},{12,4},{16,24},{20,28},{24,16},{28,20},{1,9},{5... | collective-permute-start | bytes 393224 | tf_op jit(solution)/shard_map/ppermute | solution.py:409
  18.5 5.3 %collective-permute-start.6 = (s16[4,2,4,16,128]{4,3,2,1,0:T(8,128)(2,1)S(1)}, s16[4,2,4,16,128]{4,3,2,1,0:T(8,128)(2,1)S(1)}, u32[]{:S(2)}, u32[]{:S(2)}) collective-permute-start(s16[4,2,4,16,128]{4,3,2,1,0:T(8,128)(2,1)S(1)} %shard_map.80), channel_id=1, source_target_pairs={{0,16},{4,20},{8,24},{12,28},{16,0},{20,4},{24,8},{28,12},{1,17},{... | collective-permute-start | bytes 393224 | tf_op jit(solution)/shard_map/ppermute | solution.py:409

commit v7 on v6

--- a/solution.py
+++ b/solution.py
@@ -103,10 +103,10 @@
 
 def beside(steps, items, jobs, item_fn, job_fn):
     def body(i, carry):
+        for n in range(items // steps):
+            item_fn(i * (items // steps) + n)
         for n in range(jobs // steps):
             job_fn(i * (jobs // steps) + n)
-        for n in range(items // steps):
-            item_fn(i * (items // steps) + n)
         return carry
 
     lax.fori_loop(0, steps, body, 0)
@@ -115,8 +115,8 @@
 def first_kernel(
     rounds, low_bits,
     order, cgain, cbias, egain, ebias, cost, bricks,
-    send, samples0, samples1, moved1, moved2, lines3, tab0, tab1, perm, levels, splats,
-    lines0, lines1, lines2, moved, s_order, s_cgain, s_cbias, v_cost, sems,
+    send, samples0, samples1, moved1, moved2, moved3, tab0, tab1, levels, splats,
+    lines0, lines1, lines2, lines3, perm, moved, s_order, s_cgain, s_cbias, v_cost, sems,
 ):
     me = lax.axis_index("depth")
     rows, edge = lines0.shape[0], moved.shape[0]
@@ -125,7 +125,7 @@
     chunk = rows * BC
     top, second = bit_of(me, rounds - 1), bit_of(me, rounds - 2)
     quarters = [
-        (1 - top) * 2 + 1 - second, (1 - top) * 2 + second, top * 2 + 1 - second, top * 2 + second
+        (1 - top) * 2 + 1 - second, top * 2 + 1 - second, (1 - top) * 2 + second, top * 2 + second
     ]
     small = [(order, s_order), (cgain, s_cgain), (cbias, s_cbias), (cost, v_cost)]
     pairs = list(small)
@@ -134,7 +134,8 @@
             span = pl.ds(h * LANES, LANES)
             pairs.append((bricks.at[pl.ds(quarter * rows, rows), :, :, span], lines.at[:, h]))
     copies = [pltpu.make_async_copy(a, b, sems.at[i]) for i, (a, b) in enumerate(pairs)]
-    for copy in copies:
+    early = len(small) + halves
+    for copy in copies[:early]:
         copy.start()
     ready = [copies[len(small) + q * halves : len(small) + (q + 1) * halves] for q in range(4)]
 
@@ -148,7 +149,7 @@
     tile = LANES // edge
     lane = lax.broadcasted_iota(jnp.int32, (edge, LANES), 1)
     source = lax.broadcasted_iota(jnp.int32, (edge, LANES), 0)
-    masks = [jnp.where(lane // edge == (-y) % tile, 1.0, 0.0) for y in range(tile)]
+    masks = [jnp.where(lane // edge == (-y) % tile, 1.0, 0.0).astype(jnp.bfloat16) for y in range(tile)]
     same_column = lax.rem(lane, edge) == source
     blank = jnp.zeros((edge, LANES), jnp.bfloat16)
     target_col = lax.rem(lane, edge).astype(jnp.float32)
@@ -165,17 +166,19 @@
         return jnp.where(source == anchor, low, 0.0) + jnp.where(source == anchor + 1.0, high, 0.0)
 
     def build(k, carry):
-        cols = weigh(source, *taps(target_col, 0, k))
-        blocks = [(cols * masks[y]).astype(jnp.bfloat16) for y in range(tile)]
-        lines = []
+        cols = weigh(source, *taps(target_col, 0, k)).astype(jnp.bfloat16)
+        blocks = [cols * masks[y] for y in range(tile)]
         for h in range(halves):
             anchor, low, high = taps(target_row[h], 1, k)
-            lines.append((anchor, jnp.where(same_column, low, 0.0), jnp.where(same_column, high, 0.0)))
-        for y in range(edge):
-            for h in range(halves):
+            low = jnp.where(same_column, low, 0.0).astype(jnp.bfloat16)
+            high = jnp.where(same_column, high, 0.0).astype(jnp.bfloat16)
+            after = (anchor + 1.0).astype(jnp.bfloat16)
+            anchor = anchor.astype(jnp.bfloat16)
+            for y in range(edge):
                 span = pl.ds(y * edge, edge)
+                line = jnp.full((), y, jnp.bfloat16)
                 tab0[k, h, span, :] = blocks[y % tile] if y // tile == h else blank
-                tab1[k, h, span, :] = weigh(float(y), *lines[h]).astype(jnp.bfloat16)
+                tab1[k, h, span, :] = jnp.where(anchor == line, low, jnp.where(after == line, high, blank))
         return carry
 
     lax.fori_loop(0, edge, build, 0)
@@ -199,6 +202,15 @@
         for bit in range(rounds):
             splats[FRONTS + v * rounds + bit] = splat(bit_of(rank, bit).astype(jnp.float32))
 
+    for copy in ready[0]:
+        copy.wait()
+    for copy in copies[early:]:
+        copy.start()
+    for r in range(rows):
+        to_slices(lines0, r, perm, moved)
+    for k in range(edge):
+        resample(k, 0, flips, moved, tab0, samples)
+
     total = v_cost.shape[1]
     here = lax.broadcasted_iota(jnp.int32, (chunk, total), 0)
     there = lax.broadcasted_iota(jnp.int32, (chunk, total), 1)
@@ -208,13 +220,6 @@
         picked = jnp.where(here + quarter * chunk == there, row, 0.0).astype(jnp.bfloat16)
         levels[i] = jnp.dot(picked, ones, preferred_element_type=jnp.float32)
 
-    for copy in ready[0]:
-        copy.wait()
-    for r in range(rows):
-        to_slices(lines0, r, perm, moved)
-    for k in range(edge):
-        resample(k, 0, flips, moved, tab0, samples)
-
     mine = bit_of(me, 0)
 
     def item(v):
@@ -222,45 +227,40 @@
 
     count = chunk // SUB * halves // 2
     beside(2, count, edge, item(0), lambda k: resample(k, 1, flips, moved, tab1, samples))
-    for copy in ready[1] + ready[2]:
+    for copy in ready[1] + ready[2] + ready[3]:
         copy.wait()
 
     def slices(r):
         to_slices(lines1, r, perm, moved1)
         to_slices(lines2, r, perm, moved2)
+        to_slices(lines3, r, perm, moved3)
 
     beside(2, count, rows, item(1), slices)
-    for copy in ready[3]:
-        copy.wait()
-
-
-def second_kernel(low_bits, here0, here1, moved_next, tab0, tab1, levels, splats, kept, next0, next1):
+
+
+def second_kernel(low_bits, here0, here1, moved_next, tab0, levels, splats, kept, next0):
     mine = bit_of(lax.axis_index("depth"), 0)
-    samples, samples_next = (here0, here1), (next0, next1)
+    samples = (here0, here1)
     edge, halves, chunk, _ = here0.shape
     count = chunk // SUB * halves // 2
     flips = flips_of(splats)
-    for v, table in enumerate((tab0, tab1)):
+    for v in range(2):
         beside(
-            2, count, edge,
+            2, count, edge // 2,
             lambda i: shade(i, mine, low_bits, v, samples, levels.at[0], splats, kept),
-            lambda k: resample(k, v, flips, moved_next, table, samples_next),
+            lambda k: resample(v * (edge // 2) + k, 0, flips, moved_next, tab0, (next0,)),
         )
 
 
-def quarter_kernel(low_bits, index, *refs):
-    levels, splats, here0, here1, *refs = refs
+def quarter_kernel(low_bits, index, levels, splats, here0, moved, tab1, *refs):
+    if index < 3:
+        moved_next, tab0, send, kept, next0, here1 = refs
+    else:
+        send, kept, here1 = refs
     samples = (here0, here1)
-    if index == 1:
-        moved, tab0, tab1, lines, perm, send, kept, *samples_next, moved_next = refs
-    elif index == 2:
-        moved, tab0, tab1, send, kept, *samples_next = refs
-    else:
-        send, kept = refs
     mine = bit_of(lax.axis_index("depth"), 0)
     edge, halves, chunk, _ = here0.shape
     count = chunk // SUB * halves // 2
-    rows = chunk // BC
     flips = flips_of(splats)
     for v in range(2):
 
@@ -268,13 +268,13 @@
             shade(i, 1 - mine, low_bits, v, samples, levels.at[index], splats, send)
             shade(i, mine, low_bits, v, samples, levels.at[index], splats, kept)
 
-        def jobs(r):
-            for n in range(edge // rows):
-                resample(r * (edge // rows) + n, v, flips, moved, tab1 if v else tab0, samples_next)
-            if index == 1 and v == 0:
-                to_slices(lines, r, perm, moved_next)
-
-        beside(rows, count, rows if index < 3 else 0, items, jobs)
+        def jobs(k):
+            if v == 0:
+                resample(k, 1, flips, moved, tab1, samples)
+            else:
+                resample(k, 0, flips, moved_next, tab0, (next0,))
+
+        beside(4, count, edge if index < 3 or v == 0 else 0, items, jobs)
 
 
 VMEM = pl.BlockSpec(memory_space=pltpu.VMEM)
@@ -311,29 +311,30 @@
     far = lambda x: pltpu.with_memory_space_constraint(x, pltpu.HBM)
     ins = (far(order), far(cgain), far(cbias), egain, ebias, far(cost), far(bricks))
     specs = [HBM] * 3 + [pl.BlockSpec(memory_space=pltpu.SMEM)] * 2 + [HBM] * 2
-    send0, *samples0, moved1, moved2, lines3, tab0, tab1, perm, levels_, splats_ = call(
+    send0, *samples0, moved1, moved2, moved3, tab0, tab1, levels_, splats_ = call(
         functools.partial(first_kernel, rounds, low_bits), ins,
-        (part, samples, samples, moved, moved, lines, table, table, square, levels, splats), 4000,
-        [pltpu.VMEM(*lines), pltpu.VMEM(*lines), pltpu.VMEM(*lines), pltpu.VMEM(*moved),
+        (part, samples, samples, moved, moved, moved, table, table, levels, splats), 4000,
+        [*[pltpu.VMEM(*lines)] * 4, pltpu.VMEM(*square), pltpu.VMEM(*moved),
          pltpu.SMEM(order.shape, order.dtype), pltpu.SMEM(cgain.shape, f32), pltpu.SMEM(cbias.shape, f32),
          pltpu.VMEM(cost.shape, cost.dtype), pltpu.SemaphoreType.DMA((4 + 4 * halves,))],
         20 << 20, specs,
     )
-    kept0, *samples1 = call(
+    kept0, samples1 = call(
         functools.partial(second_kernel, low_bits),
-        (*samples0, moved1, tab0, tab1, levels_, splats_), (part, samples, samples), 1800, (), 14 << 20,
-    )
-    send1, kept1, *samples2, moved3 = call(
+        (*samples0, moved1, tab0, levels_, splats_), (part, samples), 1800, (), 14 << 20,
+    )
+    scratch = [pltpu.VMEM(*samples)]
+    send1, kept1, samples2 = call(
         functools.partial(quarter_kernel, low_bits, 1),
-        (levels_, splats_, *samples1, moved2, tab0, tab1, lines3, perm), (part, part, samples, samples, moved), 3500, (), 14 << 20,
-    )
-    send2, kept2, *samples3 = call(
+        (levels_, splats_, samples1, moved1, tab1, moved2, tab0), (part, part, samples), 3500, scratch, 14 << 20,
+    )
+    send2, kept2, samples3 = call(
         functools.partial(quarter_kernel, low_bits, 2),
-        (levels_, splats_, *samples2, moved3, tab0, tab1), (part, part, samples, samples), 3500, (), 14 << 20,
+        (levels_, splats_, samples2, moved2, tab1, moved3, tab0), (part, part, samples), 3500, scratch, 14 << 20,
     )
     send3, kept3 = call(
         functools.partial(quarter_kernel, low_bits, 3),
-        (levels_, splats_, *samples3), (part, part), 3300, (), 8 << 20,
+        (levels_, splats_, samples3, moved3, tab1), (part, part), 3300, scratch, 8 << 20,
     )
     return splats_, [(send0, kept0), (send1, kept1), (send2, kept2), (send3, kept3)]
 
@@ -434,11 +435,11 @@
         (done,) = merge(rounds, near - 1, low_bits, (i16,), splats, kept, [incoming])
         return swapped(done, near)
 
-    across = leave(0)
-    kept, incoming = close(1)
-    (done,) = merge(rounds, near - 1, low_bits, (i16,), splats, kept, [incoming, across])
+    far = leave(0)
+    across = leave(1)
+    kept, incoming = close(2)
+    (done,) = merge(rounds, near - 1, low_bits, (i16,), splats, kept, [incoming, far])
     top = swapped(done, near + 1)
-    across = leave(2)
     kept, incoming = close(3)
     return finish(rounds, near - 1, edge, splats, kept, [incoming, across, top])
 

time: 25.1 us -> 24.5 us (0.976)
  Pallas kernels: 12.2 us -> 11.6 us
    pallas_call x9, Pallas kernels: 12.2 us -> 11.6 us  [call(): pl.pallas_call(kernel, out_shape=outs, in_specs=specs or [VMEM] * len(ins...]
  transfers between devices with their start and end apart: 7 -> 7, of which waited for: 3 -> 3; matrix products, arithmetic and copies ran while one was open for 0% -> 0% of each run, Pallas kernels for 31% -> 30%
where the time goes in v7:
time: 24.5 us; the launch traced here: 24.3 us
  Pallas kernels  11.6 us (47%)
  starting transfers between devices  6.23 us (25%)
  waiting for transfers between devices  5.12 us (21%)
  between operations  1.35 us (6%)
    pallas_call x9, Pallas kernels, call(): pl.pallas_call(kernel, out_shape=outs, in_specs=specs or [VMEM] * len(ins...  11.6 us
    ppermute x7, starting transfers between devices, swapped(): return lax.ppermute(x, 'depth', [(i, i ^ 1 << bit) for i in range(count)])  6.23 us
    ppermute x7, waiting for transfers between devices, swapped(): return lax.ppermute(x, 'depth', [(i, i ^ 1 << bit) for i in range(count)])  5.12 us
  transfers between devices with their start and end apart: 7, of which 3 were waited for; matrix products, arithmetic and copies ran while one was open for 0% of the time, Pallas kernels for 30%

profile of v7, /device:TPU:0, one launch (start us, length us, event | category | flops | bytes accessed | tf_op | source)
XLA Modules:
  0.0 24.3 jit_solution(4222571907912701396)
XLA Ops:
  1.3 3.3 %shard_map.73 = (f32[4,2,4,16,128]{4,3,2,1,0:T(8,128)S(1)}, f32[16,2,64,128]{3,2,1,0:T(8,128)S(1)}, f32[16,2,64,128]{3,2,1,0:T(8,128)S(1)}, bf16[16,2,64,128]{3,...) custom-call(s32[2,8]{1,0:T(2,128)} %order.1, ...), custom_call_target="tpu_custom_call" | custom-call | flops 16384000 | bytes 262144 | tf_op jit(solution)/shard_map/pallas_call | solution.py:286
  4.6 0.6 %collective-permute-start.4 = (f32[4,2,4,16,128]{4,3,2,1,0:T(8,128)S(1)}, f32[4,2,4,16,128]{4,3,2,1,0:T(8,128)S(1)}, u32[]{:S(2)}, u32[]{:S(2)}) collective-permute-start(f32[4,2,4,16,128]{4,3,2,1,0:T(8,128)S(1)} %get-tuple-element.44), channel_id=1, source_target_pairs={{0,4},{4,0},{8,12},{12,8},{16,20},{20,16},{24,28},{28,24},{1,5},{5... | collective-permute-start | bytes 786440 | tf_op jit(solution)/shard_map/ppermute | solution.py:410
  5.2 1.2 %shard_map.74 = (f32[4,2,4,16,128]{4,3,2,1,0:T(8,128)S(1)}, f32[16,2,64,128]{3,2,1,0:T(8,128)S(1)}) custom-call(f32[16,2,64,128]{3,2,1,0:T(8,128)S(1)} %get-tuple-element.27.here0, f32[16,2,64,128]{3,2,1,0:T(8,128)S(1)} %get-tuple-element.28.here1, bf16[16,2,64,128]{3,2,1,0:T(8,128)(2,1)S(1)} %get-tuple-element.29.moved_next.moved, ...), custom_call_target="tpu_custom_call" | custom-call | flops 7372800 | bytes 262144 | tf_op jit(solution)/shard_map/pallas_call | solution.py:286
  6.4 1.9 %shard_map.75 = (f32[4,2,4,16,128]{4,3,2,1,0:T(8,128)S(1)}, f32[4,2,4,16,128]{4,3,2,1,0:T(8,128)S(1)}, f32[16,2,64,128]{3,2,1,0:T(8,128)S(1)}) custom-call(f32[4,64,128]{2,1,0:T(8,128)S(1)} %get-tuple-element.26.levels, f32[16,8,128]{2,1,0:T(8,128)S(1)} %get-tuple-element.25.splats, f32[16,2,64,128]{3,2,1,0:T(8,128)S(1)} %get-tuple-element.31.here0, ...), custom_call_target="tpu_custom_call" | custom-call | flops 14336000 | bytes 262144 | tf_op jit(solution)/shard_map/pallas_call | solution.py:286
  8.3 0.1 collective-permute-start.1
  8.4 1.9 %shard_map.76 = (f32[4,2,4,16,128]{4,3,2,1,0:T(8,128)S(1)}, f32[4,2,4,16,128]{4,3,2,1,0:T(8,128)S(1)}, f32[16,2,64,128]{3,2,1,0:T(8,128)S(1)}) custom-call(f32[4,64,128]{2,1,0:T(8,128)S(1)} %get-tuple-element.26.levels, f32[16,8,128]{2,1,0:T(8,128)S(1)} %get-tuple-element.25.splats, f32[16,2,64,128]{3,2,1,0:T(8,128)S(1)} %get-tuple-element.34.here0, ...), custom_call_target="tpu_custom_call" | custom-call | flops 14336000 | bytes 262144 | tf_op jit(solution)/shard_map/pallas_call | solution.py:286
  10.3 0.6 %collective-permute-start.3 = (f32[4,2,4,16,128]{4,3,2,1,0:T(8,128)S(1)}, f32[4,2,4,16,128]{4,3,2,1,0:T(8,128)S(1)}, u32[]{:S(2)}, u32[]{:S(2)}) collective-permute-start(f32[4,2,4,16,128]{4,3,2,1,0:T(8,128)S(1)} %get-tuple-element.42), channel_id=1, source_target_pairs={{0,4},{4,0},{8,12},{12,8},{16,20},{20,16},{24,28},{28,24},{1,5},{5... | collective-permute-start | bytes 786440 | tf_op jit(solution)/shard_map/ppermute | solution.py:410
  10.8 0.0 collective-permute-done.4.refs_0_
  10.9 0.1 shard_map.79
  11.0 2.6 %collective-permute-start.5 = (s16[4,2,4,16,128]{4,3,2,1,0:T(8,128)(2,1)S(1)}, s16[4,2,4,16,128]{4,3,2,1,0:T(8,128)(2,1)S(1)}, u32[]{:S(2)}, u32[]{:S(2)}) collective-permute-start(s16[4,2,4,16,128]{4,3,2,1,0:T(8,128)(2,1)S(1)} %shard_map.79), channel_id=1, source_target_pairs={{0,8},{4,12},{8,0},{12,4},{16,24},{20,28},{24,16},{28,20},{1,9},{5... | collective-permute-start | bytes 393224 | tf_op jit(solution)/shard_map/ppermute | solution.py:410
  13.5 1.8 %shard_map.77 = (f32[4,2,4,16,128]{4,3,2,1,0:T(8,128)S(1)}, f32[4,2,4,16,128]{4,3,2,1,0:T(8,128)S(1)}) custom-call(f32[4,64,128]{2,1,0:T(8,128)S(1)} %get-tuple-element.26.levels, f32[16,8,128]{2,1,0:T(8,128)S(1)} %get-tuple-element.25.splats, f32[16,2,64,128]{3,2,1,0:T(8,128)S(1)} %get-tuple-element.36.here0, ...), custom_call_target="tpu_custom_call" | custom-call | flops 13516800 | bytes 262144 | tf_op jit(solution)/shard_map/pallas_call | solution.py:286
  15.3 0.3 %collective-permute-start = (f32[4,2,4,16,128]{4,3,2,1,0:T(8,128)S(1)}, f32[4,2,4,16,128]{4,3,2,1,0:T(8,128)S(1)}, u32[]{:S(2)}, u32[]{:S(2)}) collective-permute-start(f32[4,2,4,16,128]{4,3,2,1,0:T(8,128)S(1)} %get-tuple-element.38), channel_id=1, source_target_pairs={{0,4},{4,0},{8,12},{12,8},{16,20},{20,16},{24,28},{28,24},{1,5},{5... | collective-permute-start | bytes 786440 | tf_op jit(solution)/shard_map/ppermute | solution.py:410
  15.6 0.0 collective-permute-done.1.refs_0_
  15.6 0.1 shard_map.78
  15.7 0.4 %collective-permute-start.2 = (s16[4,2,4,16,128]{4,3,2,1,0:T(8,128)(2,1)S(1)}, s16[4,2,4,16,128]{4,3,2,1,0:T(8,128)(2,1)S(1)}, u32[]{:S(2)}, u32[]{:S(2)}) collective-permute-start(s16[4,2,4,16,128]{4,3,2,1,0:T(8,128)(2,1)S(1)} %shard_map.78), channel_id=1, source_target_pairs={{0,8},{4,12},{8,0},{12,4},{16,24},{20,28},{24,16},{28,20},{1,9},{5... | collective-permute-start | bytes 393224 | tf_op jit(solution)/shard_map/ppermute | solution.py:410
  16.1 0.0 collective-permute-done.3.refs_0_
  16.1 1.6 %collective-permute-done.5.refs_1_ = s16[4,2,4,16,128]{4,3,2,1,0:T(8,128)(2,1)S(1)} collective-permute-done((s16[4,2,4,16,128]{4,3,2,1,0:T(8,128)(2,1)S(1)}, s16[4,2,4,16,128]{4,3,2,1,0:T(8,128)(2,1)S(1)}, u32[]{:S(2)}, u32[]{:S(2)}) %collective-permute-start.5) | collective-permute-done | bytes 131104 | tf_op jit(solution)/shard_map/ppermute | solution.py:410
  17.7 0.2 shard_map.80
  17.9 1.8 %collective-permute-start.6 = (s16[4,2,4,16,128]{4,3,2,1,0:T(8,128)(2,1)S(1)}, s16[4,2,4,16,128]{4,3,2,1,0:T(8,128)(2,1)S(1)}, u32[]{:S(2)}, u32[]{:S(2)}) collective-permute-start(s16[4,2,4,16,128]{4,3,2,1,0:T(8,128)(2,1)S(1)} %shard_map.80), channel_id=1, source_target_pairs={{0,16},{4,20},{8,24},{12,28},{16,0},{20,4},{24,8},{28,12},{1,17},{... | collective-permute-start | bytes 393224 | tf_op jit(solution)/shard_map/ppermute | solution.py:410
  19.7 0.0 collective-permute-done.refs_0_
  19.7 1.8 %collective-permute-done.2.refs_1_ = s16[4,2,4,16,128]{4,3,2,1,0:T(8,128)(2,1)S(1)} collective-permute-done((s16[4,2,4,16,128]{4,3,2,1,0:T(8,128)(2,1)S(1)}, s16[4,2,4,16,128]{4,3,2,1,0:T(8,128)(2,1)S(1)}, u32[]{:S(2)}, u32[]{:S(2)}) %collective-permute-start.2) | collective-permute-done | bytes 131104 | tf_op jit(solution)/shard_map/ppermute | solution.py:410
  21.5 1.7 %collective-permute-done.6.refs_2_ = s16[4,2,4,16,128]{4,3,2,1,0:T(8,128)(2,1)S(1)} collective-permute-done((s16[4,2,4,16,128]{4,3,2,1,0:T(8,128)(2,1)S(1)}, s16[4,2,4,16,128]{4,3,2,1,0:T(8,128)(2,1)S(1)}, u32[]{:S(2)}, u32[]{:S(2)}) %collective-permute-start.6) | collective-permute-done | bytes 131104 | tf_op jit(solution)/shard_map/ppermute | solution.py:410
  23.3 1.1 %shard_map.81 = f32[2,4,32,256]{3,2,1,0:T(8,128)} custom-call(f32[16,8,128]{2,1,0:T(8,128)S(1)} %get-tuple-element.25.splats, f32[4,2,4,16,128]{4,3,2,1,0:T(8,128)S(1)} %get-tuple-element.37.kept, f32[4,2,4,16,128]{4,3,2,1,0:T(8,128)S(1)} %collective-permute-done.refs_0_, s16[4,2,4,16,128]{4,3,2,1,0:T(8,128)(2,1)S(1)} %collective-permute-done.2.refs_1_, ...), custom_call_target="tpu_custom_call" | custom-call | flops 6144000 | bytes 262144 | tf_op jit(solution)/shard_map/pallas_call | solution.py:286
Async XLA Ops:
  4.6 6.2 %collective-permute-start.4 = (f32[4,2,4,16,128]{4,3,2,1,0:T(8,128)S(1)}, f32[4,2,4,16,128]{4,3,2,1,0:T(8,128)S(1)}, u32[]{:S(2)}, u32[]{:S(2)}) collective-permute-start(f32[4,2,4,16,128]{4,3,2,1,0:T(8,128)S(1)} %get-tuple-element.44), channel_id=1, source_target_pairs={{0,4},{4,0},{8,12},{12,8},{16,20},{20,16},{24,28},{28,24},{1,5},{5... | collective-permute-start | bytes 786440 | tf_op jit(solution)/shard_map/ppermute | solution.py:410
  8.3 7.3 %collective-permute-start.1 = (f32[4,2,4,16,128]{4,3,2,1,0:T(8,128)S(1)}, f32[4,2,4,16,128]{4,3,2,1,0:T(8,128)S(1)}, u32[]{:S(2)}, u32[]{:S(2)}) collective-permute-start(f32[4,2,4,16,128]{4,3,2,1,0:T(8,128)S(1)} %get-tuple-element.40), channel_id=1, source_target_pairs={{0,4},{4,0},{8,12},{12,8},{16,20},{20,16},{24,28},{28,24},{1,5},{5... | collective-permute-start | bytes 786440 | tf_op jit(solution)/shard_map/ppermute | solution.py:410
  10.3 5.8 %collective-permute-start.3 = (f32[4,2,4,16,128]{4,3,2,1,0:T(8,128)S(1)}, f32[4,2,4,16,128]{4,3,2,1,0:T(8,128)S(1)}, u32[]{:S(2)}, u32[]{:S(2)}) collective-permute-start(f32[4,2,4,16,128]{4,3,2,1,0:T(8,128)S(1)} %get-tuple-element.42), channel_id=1, source_target_pairs={{0,4},{4,0},{8,12},{12,8},{16,20},{20,16},{24,28},{28,24},{1,5},{5... | collective-permute-start | bytes 786440 | tf_op jit(solution)/shard_map/ppermute | solution.py:410
  11.0 6.7 %collective-permute-start.5 = (s16[4,2,4,16,128]{4,3,2,1,0:T(8,128)(2,1)S(1)}, s16[4,2,4,16,128]{4,3,2,1,0:T(8,128)(2,1)S(1)}, u32[]{:S(2)}, u32[]{:S(2)}) collective-permute-start(s16[4,2,4,16,128]{4,3,2,1,0:T(8,128)(2,1)S(1)} %shard_map.79), channel_id=1, source_target_pairs={{0,8},{4,12},{8,0},{12,4},{16,24},{20,28},{24,16},{28,20},{1,9},{5... | collective-permute-start | bytes 393224 | tf_op jit(solution)/shard_map/ppermute | solution.py:410
  15.3 4.4 %collective-permute-start = (f32[4,2,4,16,128]{4,3,2,1,0:T(8,128)S(1)}, f32[4,2,4,16,128]{4,3,2,1,0:T(8,128)S(1)}, u32[]{:S(2)}, u32[]{:S(2)}) collective-permute-start(f32[4,2,4,16,128]{4,3,2,1,0:T(8,128)S(1)} %get-tuple-element.38), channel_id=1, source_target_pairs={{0,4},{4,0},{8,12},{12,8},{16,20},{20,16},{24,28},{28,24},{1,5},{5... | collective-permute-start | bytes 786440 | tf_op jit(solution)/shard_map/ppermute | solution.py:410
  15.7 5.8 %collective-permute-start.2 = (s16[4,2,4,16,128]{4,3,2,1,0:T(8,128)(2,1)S(1)}, s16[4,2,4,16,128]{4,3,2,1,0:T(8,128)(2,1)S(1)}, u32[]{:S(2)}, u32[]{:S(2)}) collective-permute-start(s16[4,2,4,16,128]{4,3,2,1,0:T(8,128)(2,1)S(1)} %shard_map.78), channel_id=1, source_target_pairs={{0,8},{4,12},{8,0},{12,4},{16,24},{20,28},{24,16},{28,20},{1,9},{5... | collective-permute-start | bytes 393224 | tf_op jit(solution)/shard_map/ppermute | solution.py:410
  17.9 5.4 %collective-permute-start.6 = (s16[4,2,4,16,128]{4,3,2,1,0:T(8,128)(2,1)S(1)}, s16[4,2,4,16,128]{4,3,2,1,0:T(8,128)(2,1)S(1)}, u32[]{:S(2)}, u32[]{:S(2)}) collective-permute-start(s16[4,2,4,16,128]{4,3,2,1,0:T(8,128)(2,1)S(1)} %shard_map.80), channel_id=1, source_target_pairs={{0,16},{4,20},{8,24},{12,28},{16,0},{20,4},{24,8},{28,12},{1,17},{... | collective-permute-start | bytes 393224 | tf_op jit(solution)/shard_map/ppermute | solution.py:410

commit v8 on v7

--- a/solution.py
+++ b/solution.py
@@ -125,7 +125,7 @@
     chunk = rows * BC
     top, second = bit_of(me, rounds - 1), bit_of(me, rounds - 2)
     quarters = [
-        (1 - top) * 2 + 1 - second, top * 2 + 1 - second, (1 - top) * 2 + second, top * 2 + second
+        (1 - top) * 2 + 1 - second, (1 - top) * 2 + second, top * 2 + 1 - second, top * 2 + second
     ]
     small = [(order, s_order), (cgain, s_cgain), (cbias, s_cbias), (cost, v_cost)]
     pairs = list(small)
@@ -238,29 +238,31 @@
     beside(2, count, rows, item(1), slices)
 
 
-def second_kernel(low_bits, here0, here1, moved_next, tab0, levels, splats, kept, next0):
+def second_kernel(low_bits, here0, here1, moved_next, tab0, tab1, levels, splats, kept, next0, next1):
     mine = bit_of(lax.axis_index("depth"), 0)
-    samples = (here0, here1)
+    samples, samples_next = (here0, here1), (next0, next1)
     edge, halves, chunk, _ = here0.shape
     count = chunk // SUB * halves // 2
     flips = flips_of(splats)
-    for v in range(2):
+    for v, table in enumerate((tab0, tab1)):
         beside(
-            2, count, edge // 2,
+            1, count, edge,
             lambda i: shade(i, mine, low_bits, v, samples, levels.at[0], splats, kept),
-            lambda k: resample(v * (edge // 2) + k, 0, flips, moved_next, tab0, (next0,)),
+            lambda k: resample(k, v, flips, moved_next, table, samples_next),
         )
 
 
-def quarter_kernel(low_bits, index, levels, splats, here0, moved, tab1, *refs):
+def quarter_kernel(low_bits, index, *refs):
+    levels, splats, here0, here1, *refs = refs
+    samples = (here0, here1)
     if index < 3:
-        moved_next, tab0, send, kept, next0, here1 = refs
+        moved, tab0, tab1, send, kept, *samples_next = refs
     else:
-        send, kept, here1 = refs
-    samples = (here0, here1)
+        send, kept = refs
     mine = bit_of(lax.axis_index("depth"), 0)
     edge, halves, chunk, _ = here0.shape
     count = chunk // SUB * halves // 2
+    rows = chunk // BC
     flips = flips_of(splats)
     for v in range(2):
 
@@ -268,13 +270,11 @@
             shade(i, 1 - mine, low_bits, v, samples, levels.at[index], splats, send)
             shade(i, mine, low_bits, v, samples, levels.at[index], splats, kept)
 
-        def jobs(k):
-            if v == 0:
-                resample(k, 1, flips, moved, tab1, samples)
-            else:
-                resample(k, 0, flips, moved_next, tab0, (next0,))
-
-        beside(4, count, edge if index < 3 or v == 0 else 0, items, jobs)
+        def jobs(r):
+            for n in range(edge // rows):
+                resample(r * (edge // rows) + n, v, flips, moved, tab1 if v else tab0, samples_next)
+
+        beside(2, count, rows if index < 3 else 0, items, jobs)
 
 
 VMEM = pl.BlockSpec(memory_space=pltpu.VMEM)
@@ -319,22 +319,21 @@
          pltpu.VMEM(cost.shape, cost.dtype), pltpu.SemaphoreType.DMA((4 + 4 * halves,))],
         20 << 20, specs,
     )
-    kept0, samples1 = call(
+    kept0, *samples1 = call(
         functools.partial(second_kernel, low_bits),
-        (*samples0, moved1, tab0, levels_, splats_), (part, samples), 1800, (), 14 << 20,
-    )
-    scratch = [pltpu.VMEM(*samples)]
-    send1, kept1, samples2 = call(
+        (*samples0, moved1, tab0, tab1, levels_, splats_), (part, samples, samples), 1800, (), 14 << 20,
+    )
+    send1, kept1, *samples2 = call(
         functools.partial(quarter_kernel, low_bits, 1),
-        (levels_, splats_, samples1, moved1, tab1, moved2, tab0), (part, part, samples), 3500, scratch, 14 << 20,
-    )
-    send2, kept2, samples3 = call(
+        (levels_, splats_, *samples1, moved2, tab0, tab1), (part, part, samples, samples), 3500, (), 14 << 20,
+    )
+    send2, kept2, *samples3 = call(
         functools.partial(quarter_kernel, low_bits, 2),
-        (levels_, splats_, samples2, moved2, tab1, moved3, tab0), (part, part, samples), 3500, scratch, 14 << 20,
+        (levels_, splats_, *samples2, moved3, tab0, tab1), (part, part, samples, samples), 3500, (), 14 << 20,
     )
     send3, kept3 = call(
         functools.partial(quarter_kernel, low_bits, 3),
-        (levels_, splats_, samples3, moved3, tab1), (part, part), 3300, scratch, 8 << 20,
+        (levels_, splats_, *samples3), (part, part), 3300, (), 8 << 20,
     )
     return splats_, [(send0, kept0), (send1, kept1), (send2, kept2), (send3, kept3)]
 
@@ -435,11 +434,11 @@
         (done,) = merge(rounds, near - 1, low_bits, (i16,), splats, kept, [incoming])
         return swapped(done, near)
 
-    far = leave(0)
-    across = leave(1)
-    kept, incoming = close(2)
-    (done,) = merge(rounds, near - 1, low_bits, (i16,), splats, kept, [incoming, far])
+    across = leave(0)
+    kept, incoming = close(1)
+    (done,) = merge(rounds, near - 1, low_bits, (i16,), splats, kept, [incoming, across])
     top = swapped(done, near + 1)
+    across = leave(2)
     kept, incoming = close(3)
     return finish(rounds, near - 1, edge, splats, kept, [incoming, across, top])
 

time: 24.5 us -> 23.9 us (0.976)
  Pallas kernels: 11.6 us -> 10.9 us
    pallas_call x9, Pallas kernels: 11.6 us -> 10.9 us  [call(): pl.pallas_call(kernel, out_shape=outs, in_specs=specs or [VMEM] * len(ins...]
  transfers between devices with their start and end apart: 7 -> 7, of which waited for: 3 -> 3; matrix products, arithmetic and copies ran while one was open for 0% -> 0% of each run, Pallas kernels for 30% -> 27%
where the time goes in v8:
time: 23.9 us; the launch traced here: 23.7 us
  Pallas kernels  10.9 us (46%)
  starting transfers between devices  6.2 us (26%)
  waiting for transfers between devices  5.26 us (22%)
  between operations  1.34 us (6%)
    pallas_call x9, Pallas kernels, call(): pl.pallas_call(kernel, out_shape=outs, in_specs=specs or [VMEM] * len(ins...  10.9 us
    ppermute x7, starting transfers between devices, swapped(): return lax.ppermute(x, 'depth', [(i, i ^ 1 << bit) for i in range(count)])  6.2 us
    ppermute x7, waiting for transfers between devices, swapped(): return lax.ppermute(x, 'depth', [(i, i ^ 1 << bit) for i in range(count)])  5.26 us
  transfers between devices with their start and end apart: 7, of which 3 were waited for; matrix products, arithmetic and copies ran while one was open for 0% of the time, Pallas kernels for 27%

profile of v8, /device:TPU:0, one launch (start us, length us, event | category | flops | bytes accessed | tf_op | source)
XLA Modules:
  0.0 23.7 jit_solution(16391009386774175737)
XLA Ops:
  1.3 3.3 %shard_map.73 = (f32[4,2,4,16,128]{4,3,2,1,0:T(8,128)S(1)}, f32[16,2,64,128]{3,2,1,0:T(8,128)S(1)}, f32[16,2,64,128]{3,2,1,0:T(8,128)S(1)}, bf16[16,2,64,128]{3,...) custom-call(s32[2,8]{1,0:T(2,128)} %order.1, ...), custom_call_target="tpu_custom_call" | custom-call | flops 16384000 | bytes 262144 | tf_op jit(solution)/shard_map/pallas_call | solution.py:286
  4.6 0.6 %collective-permute-start.4 = (f32[4,2,4,16,128]{4,3,2,1,0:T(8,128)S(1)}, f32[4,2,4,16,128]{4,3,2,1,0:T(8,128)S(1)}, u32[]{:S(2)}, u32[]{:S(2)}) collective-permute-start(f32[4,2,4,16,128]{4,3,2,1,0:T(8,128)S(1)} %get-tuple-element.50), channel_id=1, source_target_pairs={{0,4},{4,0},{8,12},{12,8},{16,20},{20,16},{24,28},{28,24},{1,5},{5... | collective-permute-start | bytes 786440 | tf_op jit(solution)/shard_map/ppermute | solution.py:409
  5.2 1.0 %shard_map.74 = (f32[4,2,4,16,128]{4,3,2,1,0:T(8,128)S(1)}, f32[16,2,64,128]{3,2,1,0:T(8,128)S(1)}, f32[16,2,64,128]{3,2,1,0:T(8,128)S(1)}) custom-call(f32[16,2,64,128]{3,2,1,0:T(8,128)S(1)} %get-tuple-element.30.here0, f32[16,2,64,128]{3,2,1,0:T(8,128)S(1)} %get-tuple-element.31.here1, bf16[16,2,64,128]{3,2,1,0:T(8,128)(2,1)S(1)} %get-tuple-element.32.moved_next, ...), custom_call_target="tpu_custom_call" | custom-call | flops 7372800 | bytes 262144 | tf_op jit(solution)/shard_map/pallas_call | solution.py:286
  6.2 1.7 %shard_map.75 = (f32[4,2,4,16,128]{4,3,2,1,0:T(8,128)S(1)}, f32[4,2,4,16,128]{4,3,2,1,0:T(8,128)S(1)}, f32[16,2,64,128]{3,2,1,0:T(8,128)S(1)}, f32[16,2,64,128]{3,2,1,0:T(8,128)S(1)}) custom-call(f32[4,64,128]{2,1,0:T(8,128)S(1)} %get-tuple-element.29.levels.refs_0_, f32[16,8,128]{2,1,0:T(8,128)S(1)} %get-tuple-element.28.splats.refs_1_, ...), custom_call_target="tpu_custom_call" | custom-call | flops 14336000 | bytes 262144 | tf_op jit(solution)/shard_map/pallas_call | solution.py:286
  8.0 1.7 %shard_map.76 = (f32[4,2,4,16,128]{4,3,2,1,0:T(8,128)S(1)}, f32[4,2,4,16,128]{4,3,2,1,0:T(8,128)S(1)}, f32[16,2,64,128]{3,2,1,0:T(8,128)S(1)}, f32[16,2,64,128]{3,2,1,0:T(8,128)S(1)}) custom-call(f32[4,64,128]{2,1,0:T(8,128)S(1)} %get-tuple-element.29.levels.refs_0_, f32[16,8,128]{2,1,0:T(8,128)S(1)} %get-tuple-element.28.splats.refs_1_, ...), custom_call_target="tpu_custom_call" | custom-call | flops 14336000 | bytes 262144 | tf_op jit(solution)/shard_map/pallas_call | solution.py:286
  9.7 0.1 collective-permute-start.1
  9.8 0.5 %collective-permute-start.3 = (f32[4,2,4,16,128]{4,3,2,1,0:T(8,128)S(1)}, f32[4,2,4,16,128]{4,3,2,1,0:T(8,128)S(1)}, u32[]{:S(2)}, u32[]{:S(2)}) collective-permute-start(f32[4,2,4,16,128]{4,3,2,1,0:T(8,128)S(1)} %get-tuple-element.48), channel_id=1, source_target_pairs={{0,4},{4,0},{8,12},{12,8},{16,20},{20,16},{24,28},{28,24},{1,5},{5... | collective-permute-start | bytes 786440 | tf_op jit(solution)/shard_map/ppermute | solution.py:409
  10.3 0.0 collective-permute-done.4.refs_0_
  10.3 0.1 shard_map.79
  10.4 2.6 %collective-permute-start.5 = (s16[4,2,4,16,128]{4,3,2,1,0:T(8,128)(2,1)S(1)}, s16[4,2,4,16,128]{4,3,2,1,0:T(8,128)(2,1)S(1)}, u32[]{:S(2)}, u32[]{:S(2)}) collective-permute-start(s16[4,2,4,16,128]{4,3,2,1,0:T(8,128)(2,1)S(1)} %shard_map.79), channel_id=1, source_target_pairs={{0,8},{4,12},{8,0},{12,4},{16,24},{20,28},{24,16},{28,20},{1,9},{5... | collective-permute-start | bytes 393224 | tf_op jit(solution)/shard_map/ppermute | solution.py:409
  13.0 1.6 %shard_map.77 = (f32[4,2,4,16,128]{4,3,2,1,0:T(8,128)S(1)}, f32[4,2,4,16,128]{4,3,2,1,0:T(8,128)S(1)}) custom-call(f32[4,64,128]{2,1,0:T(8,128)S(1)} %get-tuple-element.29.levels.refs_0_, f32[16,8,128]{2,1,0:T(8,128)S(1)} %get-tuple-element.28.splats.refs_1_, f32[16,2,64,128]{3,2,1,0:T(8,128)S(1)} %get-tuple-element.41.refs_2_, ...), custom_call_target="tpu_custom_call" | custom-call | flops 13516800 | bytes 262144 | tf_op jit(solution)/shard_map/pallas_call | solution.py:286
  14.6 0.2 collective-permute-start
  14.8 0.0 collective-permute-done.1.refs_0_
  14.8 0.1 shard_map.78
  15.0 0.4 %collective-permute-start.2 = (s16[4,2,4,16,128]{4,3,2,1,0:T(8,128)(2,1)S(1)}, s16[4,2,4,16,128]{4,3,2,1,0:T(8,128)(2,1)S(1)}, u32[]{:S(2)}, u32[]{:S(2)}) collective-permute-start(s16[4,2,4,16,128]{4,3,2,1,0:T(8,128)(2,1)S(1)} %shard_map.78), channel_id=1, source_target_pairs={{0,8},{4,12},{8,0},{12,4},{16,24},{20,28},{24,16},{28,20},{1,9},{5... | collective-permute-start | bytes 393224 | tf_op jit(solution)/shard_map/ppermute | solution.py:409
  15.3 0.0 collective-permute-done.3.refs_0_
  15.3 1.8 %collective-permute-done.5.refs_1_ = s16[4,2,4,16,128]{4,3,2,1,0:T(8,128)(2,1)S(1)} collective-permute-done((s16[4,2,4,16,128]{4,3,2,1,0:T(8,128)(2,1)S(1)}, s16[4,2,4,16,128]{4,3,2,1,0:T(8,128)(2,1)S(1)}, u32[]{:S(2)}, u32[]{:S(2)}) %collective-permute-start.5) | collective-permute-done | bytes 131104 | tf_op jit(solution)/shard_map/ppermute | solution.py:409
  17.1 0.2 shard_map.80
  17.3 1.8 %collective-permute-start.6 = (s16[4,2,4,16,128]{4,3,2,1,0:T(8,128)(2,1)S(1)}, s16[4,2,4,16,128]{4,3,2,1,0:T(8,128)(2,1)S(1)}, u32[]{:S(2)}, u32[]{:S(2)}) collective-permute-start(s16[4,2,4,16,128]{4,3,2,1,0:T(8,128)(2,1)S(1)} %shard_map.80), channel_id=1, source_target_pairs={{0,16},{4,20},{8,24},{12,28},{16,0},{20,4},{24,8},{28,12},{1,17},{... | collective-permute-start | bytes 393224 | tf_op jit(solution)/shard_map/ppermute | solution.py:409
  19.1 0.0 collective-permute-done.refs_0_
  19.2 1.6 %collective-permute-done.2.refs_1_ = s16[4,2,4,16,128]{4,3,2,1,0:T(8,128)(2,1)S(1)} collective-permute-done((s16[4,2,4,16,128]{4,3,2,1,0:T(8,128)(2,1)S(1)}, s16[4,2,4,16,128]{4,3,2,1,0:T(8,128)(2,1)S(1)}, u32[]{:S(2)}, u32[]{:S(2)}) %collective-permute-start.2) | collective-permute-done | bytes 131104 | tf_op jit(solution)/shard_map/ppermute | solution.py:409
  20.8 1.9 %collective-permute-done.6.refs_2_ = s16[4,2,4,16,128]{4,3,2,1,0:T(8,128)(2,1)S(1)} collective-permute-done((s16[4,2,4,16,128]{4,3,2,1,0:T(8,128)(2,1)S(1)}, s16[4,2,4,16,128]{4,3,2,1,0:T(8,128)(2,1)S(1)}, u32[]{:S(2)}, u32[]{:S(2)}) %collective-permute-start.6) | collective-permute-done | bytes 131104 | tf_op jit(solution)/shard_map/ppermute | solution.py:409
  22.6 1.1 %shard_map.81 = f32[2,4,32,256]{3,2,1,0:T(8,128)} custom-call(f32[16,8,128]{2,1,0:T(8,128)S(1)} %get-tuple-element.28.splats.refs_1_, f32[4,2,4,16,128]{4,3,2,1,0:T(8,128)S(1)} %get-tuple-element.43.kept, f32[4,2,4,16,128]{4,3,2,1,0:T(8,128)S(1)} %collective-permute-done.refs_0_, s16[4,2,4,16,128]{4,3,2,1,0:T(8,128)(2,1)S(1)} %collective-permute-done.2.refs_1_, ...), custom_call_target="tpu_custom_call" | custom-call | flops 6144000 | bytes 262144 | tf_op jit(solution)/shard_map/pallas_call | solution.py:286
Async XLA Ops:
  4.6 5.6 %collective-permute-start.4 = (f32[4,2,4,16,128]{4,3,2,1,0:T(8,128)S(1)}, f32[4,2,4,16,128]{4,3,2,1,0:T(8,128)S(1)}, u32[]{:S(2)}, u32[]{:S(2)}) collective-permute-start(f32[4,2,4,16,128]{4,3,2,1,0:T(8,128)S(1)} %get-tuple-element.50), channel_id=1, source_target_pairs={{0,4},{4,0},{8,12},{12,8},{16,20},{20,16},{24,28},{28,24},{1,5},{5... | collective-permute-start | bytes 786440 | tf_op jit(solution)/shard_map/ppermute | solution.py:409
  9.7 5.1 %collective-permute-start.1 = (f32[4,2,4,16,128]{4,3,2,1,0:T(8,128)S(1)}, f32[4,2,4,16,128]{4,3,2,1,0:T(8,128)S(1)}, u32[]{:S(2)}, u32[]{:S(2)}) collective-permute-start(f32[4,2,4,16,128]{4,3,2,1,0:T(8,128)S(1)} %get-tuple-element.46), channel_id=1, source_target_pairs={{0,4},{4,0},{8,12},{12,8},{16,20},{20,16},{24,28},{28,24},{1,5},{5... | collective-permute-start | bytes 786440 | tf_op jit(solution)/shard_map/ppermute | solution.py:409
  9.8 5.6 %collective-permute-start.3 = (f32[4,2,4,16,128]{4,3,2,1,0:T(8,128)S(1)}, f32[4,2,4,16,128]{4,3,2,1,0:T(8,128)S(1)}, u32[]{:S(2)}, u32[]{:S(2)}) collective-permute-start(f32[4,2,4,16,128]{4,3,2,1,0:T(8,128)S(1)} %get-tuple-element.48), channel_id=1, source_target_pairs={{0,4},{4,0},{8,12},{12,8},{16,20},{20,16},{24,28},{28,24},{1,5},{5... | collective-permute-start | bytes 786440 | tf_op jit(solution)/shard_map/ppermute | solution.py:409
  10.4 6.7 %collective-permute-start.5 = (s16[4,2,4,16,128]{4,3,2,1,0:T(8,128)(2,1)S(1)}, s16[4,2,4,16,128]{4,3,2,1,0:T(8,128)(2,1)S(1)}, u32[]{:S(2)}, u32[]{:S(2)}) collective-permute-start(s16[4,2,4,16,128]{4,3,2,1,0:T(8,128)(2,1)S(1)} %shard_map.79), channel_id=1, source_target_pairs={{0,8},{4,12},{8,0},{12,4},{16,24},{20,28},{24,16},{28,20},{1,9},{5... | collective-permute-start | bytes 393224 | tf_op jit(solution)/shard_map/ppermute | solution.py:409
  14.6 4.5 %collective-permute-start = (f32[4,2,4,16,128]{4,3,2,1,0:T(8,128)S(1)}, f32[4,2,4,16,128]{4,3,2,1,0:T(8,128)S(1)}, u32[]{:S(2)}, u32[]{:S(2)}) collective-permute-start(f32[4,2,4,16,128]{4,3,2,1,0:T(8,128)S(1)} %get-tuple-element.44), channel_id=1, source_target_pairs={{0,4},{4,0},{8,12},{12,8},{16,20},{20,16},{24,28},{28,24},{1,5},{5... | collective-permute-start | bytes 786440 | tf_op jit(solution)/shard_map/ppermute | solution.py:409
  15.0 5.8 %collective-permute-start.2 = (s16[4,2,4,16,128]{4,3,2,1,0:T(8,128)(2,1)S(1)}, s16[4,2,4,16,128]{4,3,2,1,0:T(8,128)(2,1)S(1)}, u32[]{:S(2)}, u32[]{:S(2)}) collective-permute-start(s16[4,2,4,16,128]{4,3,2,1,0:T(8,128)(2,1)S(1)} %shard_map.78), channel_id=1, source_target_pairs={{0,8},{4,12},{8,0},{12,4},{16,24},{20,28},{24,16},{28,20},{1,9},{5... | collective-permute-start | bytes 393224 | tf_op jit(solution)/shard_map/ppermute | solution.py:409
  17.3 5.3 %collective-permute-start.6 = (s16[4,2,4,16,128]{4,3,2,1,0:T(8,128)(2,1)S(1)}, s16[4,2,4,16,128]{4,3,2,1,0:T(8,128)(2,1)S(1)}, u32[]{:S(2)}, u32[]{:S(2)}) collective-permute-start(s16[4,2,4,16,128]{4,3,2,1,0:T(8,128)(2,1)S(1)} %shard_map.80), channel_id=1, source_target_pairs={{0,16},{4,20},{8,24},{12,28},{16,0},{20,4},{24,8},{28,12},{1,17},{... | collective-permute-start | bytes 393224 | tf_op jit(solution)/shard_map/ppermute | solution.py:409
